TPU v7x, 8 devices: a whole 2x2x1 slice. The times are simulated.
8 devices in a mesh: fsdp: 8 (over z, y, x, core).
Axes of the slice: x: 2, y: 2, z: 1, core: 2. Of those that a mesh axis runs over, the one named last changes fastest.
Arguments:
- tok_ids: int32 [16, 1024], P('fsdp')
- grad_out: bfloat16 [16, 1024, 2048], P('fsdp')
- emb_table: bfloat16 [151936, 2048], P('fsdp')
- norm_gain: bfloat16 [2048], P('fsdp')
- w_query: bfloat16 [2048, 2048], P('fsdp')
- b_query: bfloat16 [2048], P('fsdp')
- w_key: bfloat16 [2048, 2048], P('fsdp')
- b_key: bfloat16 [2048], P('fsdp')
- w_value: bfloat16 [2048, 2048], P('fsdp')
- b_value: bfloat16 [2048], P('fsdp')
- w_out: bfloat16 [2048, 2048], P('fsdp')
Outputs:
- output 1: bfloat16 [16, 1024, 2048], P('fsdp')
- output 2: bfloat16 [151936, 2048], P('fsdp')
- output 3: float32 [2048], P('fsdp')
- output 4: float32 [2048, 2048], P('fsdp')
- output 5: float32 [2048], P('fsdp')
- output 6: float32 [2048, 2048], P('fsdp')
- output 7: float32 [2048], P('fsdp')
- output 8: float32 [2048, 2048], P('fsdp')
- output 9: float32 [2048], P('fsdp')
- output 10: float32 [2048, 2048], P('fsdp')
All inputs are finite; a program needn't handle non-finite values.
Results may differ from a plain program's by a relative error of at most 0.0130164.
Values are sent between devices in bfloat16 or wider.
A program may use at most 1 GiB of HBM per device.

v0:
```python
import jax
import jax.numpy as jnp
from jax import lax
from jax.sharding import PartitionSpec as P

HEAD_DIM = 128
ROPE_THETA = 1.0e6
NORM_EPS = 1e-6
MASK_VALUE = -1e30


def rope_tables(seq_len):
    half_dim = HEAD_DIM // 2
    inv_freq = jnp.power(ROPE_THETA, -(jnp.arange(half_dim, dtype=jnp.float32) * 2.0 / HEAD_DIM))
    angles = jnp.arange(seq_len, dtype=jnp.float32)[:, None] * inv_freq[None, :]
    angles = jnp.concatenate([angles, angles], axis=-1)
    return jnp.cos(angles)[:, None, :], jnp.sin(angles)[:, None, :]


def rotate(vector, cos_t, sin_t):
    half_dim = HEAD_DIM // 2
    turned = jnp.concatenate([-vector[..., half_dim:], vector[..., :half_dim]], axis=-1)
    return vector * cos_t + turned * sin_t


def rotate_back(grad_in, cos_t, sin_t):
    half_dim = HEAD_DIM // 2
    scaled = grad_in * sin_t
    turned = jnp.concatenate([scaled[..., half_dim:], -scaled[..., :half_dim]], axis=-1)
    return grad_in * cos_t + turned


def block_fwd_bwd(x_rows, grad_out, gain_vec, w_query, b_query, w_key, b_key, w_value, b_value, w_out):
    batch_size, seq_len, model_width = x_rows.shape
    n_heads = w_query.shape[1] // HEAD_DIM
    kv_heads = w_key.shape[1] // HEAD_DIM
    q_group = n_heads // kv_heads
    score_scale = HEAD_DIM ** -0.5
    cos_t, sin_t = rope_tables(seq_len)
    x_full = x_rows.astype(jnp.float32)
    inv_rms = lax.rsqrt(jnp.mean(x_full * x_full, axis=-1, keepdims=True) + NORM_EPS)
    x_norm = x_full * inv_rms
    gain_f = gain_vec.astype(jnp.float32)
    hidden = (x_norm * gain_f).astype(jnp.bfloat16)
    q_lin = jnp.einsum("bli,io->blo", hidden, w_query, preferred_element_type=jnp.float32) + b_query.astype(jnp.float32)
    k_lin = jnp.einsum("bli,io->blo", hidden, w_key, preferred_element_type=jnp.float32) + b_key.astype(jnp.float32)
    v_lin = jnp.einsum("bli,io->blo", hidden, w_value, preferred_element_type=jnp.float32) + b_value.astype(jnp.float32)
    q_rot = rotate(q_lin.reshape(batch_size, seq_len, n_heads, HEAD_DIM), cos_t, sin_t).astype(jnp.bfloat16)
    q_rot = q_rot.reshape(batch_size, seq_len, kv_heads, q_group, HEAD_DIM)
    k_rot = rotate(k_lin.reshape(batch_size, seq_len, kv_heads, HEAD_DIM), cos_t, sin_t).astype(jnp.bfloat16)
    v_val = v_lin.astype(jnp.bfloat16).reshape(batch_size, seq_len, kv_heads, HEAD_DIM)
    scores = jnp.einsum("bqkgd,bskd->bkgqs", q_rot, k_rot, preferred_element_type=jnp.float32) * score_scale
    causal = jnp.arange(seq_len)[:, None] >= jnp.arange(seq_len)[None, :]
    scores = jnp.where(causal, scores, MASK_VALUE)
    prob_f = jax.nn.softmax(scores, axis=-1)
    prob_b = prob_f.astype(jnp.bfloat16)
    attn_out = jnp.einsum("bkgqs,bskd->bqkgd", prob_b, v_val, preferred_element_type=jnp.float32)
    attn_b = attn_out.astype(jnp.bfloat16).reshape(batch_size, seq_len, n_heads * HEAD_DIM)
    proj_out = jnp.einsum("bli,io->blo", attn_b, w_out, preferred_element_type=jnp.float32)
    block_out = (x_full + proj_out).astype(jnp.bfloat16)

    grad_wo = jnp.einsum("bli,blo->io", attn_b, grad_out, preferred_element_type=jnp.float32)
    d_attn = jnp.einsum("blo,io->bli", grad_out, w_out, preferred_element_type=jnp.float32)
    d_attn = d_attn.astype(jnp.bfloat16).reshape(batch_size, seq_len, kv_heads, q_group, HEAD_DIM)
    d_probs = jnp.einsum("bqkgd,bskd->bkgqs", d_attn, v_val, preferred_element_type=jnp.float32)
    d_val = jnp.einsum("bkgqs,bqkgd->bskd", prob_b, d_attn, preferred_element_type=jnp.float32)
    d_scores = prob_f * (d_probs - jnp.sum(d_probs * prob_f, axis=-1, keepdims=True))
    d_scores = (d_scores * score_scale).astype(jnp.bfloat16)
    d_qrot = jnp.einsum("bkgqs,bskd->bqkgd", d_scores, k_rot, preferred_element_type=jnp.float32)
    d_krot = jnp.einsum("bkgqs,bqkgd->bskd", d_scores, q_rot, preferred_element_type=jnp.float32)
    d_query = rotate_back(d_qrot.reshape(batch_size, seq_len, n_heads, HEAD_DIM), cos_t, sin_t)
    d_query = d_query.reshape(batch_size, seq_len, n_heads * HEAD_DIM)
    d_key = rotate_back(d_krot, cos_t, sin_t).reshape(batch_size, seq_len, kv_heads * HEAD_DIM)
    d_value = d_val.reshape(batch_size, seq_len, kv_heads * HEAD_DIM)
    grad_bq = jnp.sum(d_query, axis=(0, 1))
    grad_bk = jnp.sum(d_key, axis=(0, 1))
    grad_bv = jnp.sum(d_value, axis=(0, 1))
    dq_b = d_query.astype(jnp.bfloat16)
    dk_b = d_key.astype(jnp.bfloat16)
    dv_b = d_value.astype(jnp.bfloat16)
    grad_wq = jnp.einsum("bli,blo->io", hidden, dq_b, preferred_element_type=jnp.float32)
    grad_wk = jnp.einsum("bli,blo->io", hidden, dk_b, preferred_element_type=jnp.float32)
    grad_wv = jnp.einsum("bli,blo->io", hidden, dv_b, preferred_element_type=jnp.float32)
    d_hidden = jnp.einsum("blo,io->bli", dq_b, w_query, preferred_element_type=jnp.float32)
    d_hidden = d_hidden + jnp.einsum("blo,io->bli", dk_b, w_key, preferred_element_type=jnp.float32)
    d_hidden = d_hidden + jnp.einsum("blo,io->bli", dv_b, w_value, preferred_element_type=jnp.float32)
    grad_gain = jnp.sum(d_hidden * x_norm, axis=(0, 1))
    d_norm = d_hidden * gain_f
    d_x = grad_out.astype(jnp.float32) + inv_rms * (d_norm - x_norm * jnp.mean(d_norm * x_norm, axis=-1, keepdims=True))
    return block_out, d_x, (grad_gain, grad_wq, grad_bq, grad_wk, grad_bk, grad_wv, grad_bv, grad_wo)


def solution(mesh):
    row_spec = P("fsdp", None)
    vec_spec = P("fsdp")
    act_spec = P("fsdp", None, None)
    weight_specs = (vec_spec, row_spec, vec_spec, row_spec, vec_spec, row_spec, vec_spec, row_spec)
    in_specs = (row_spec, act_spec, row_spec) + weight_specs
    out_specs = (act_spec, row_spec) + weight_specs

    def device_step(tok_ids, grad_out, table_part, gain_part, wq_part, bq_part, wk_part, bk_part, wv_part, bv_part, wo_part):
        rows_dev = table_part.shape[0]
        model_width = table_part.shape[1]
        first_row = lax.axis_index("fsdp") * rows_dev
        all_ids = lax.all_gather(tok_ids, "fsdp")
        local_idx = all_ids - first_row
        is_owned = (local_idx >= 0) & (local_idx < rows_dev)
        looked = jnp.take(table_part, jnp.where(is_owned, local_idx, 0), axis=0)
        looked = jnp.where(is_owned[..., None], looked, jnp.zeros((), jnp.bfloat16))
        x_rows = lax.psum_scatter(looked, "fsdp", scatter_dimension=0)
        gain_full = lax.all_gather(gain_part, "fsdp", axis=0, tiled=True)
        wq_full = lax.all_gather(wq_part, "fsdp", axis=0, tiled=True)
        bq_full = lax.all_gather(bq_part, "fsdp", axis=0, tiled=True)
        wk_full = lax.all_gather(wk_part, "fsdp", axis=0, tiled=True)
        bk_full = lax.all_gather(bk_part, "fsdp", axis=0, tiled=True)
        wv_full = lax.all_gather(wv_part, "fsdp", axis=0, tiled=True)
        bv_full = lax.all_gather(bv_part, "fsdp", axis=0, tiled=True)
        wo_full = lax.all_gather(wo_part, "fsdp", axis=0, tiled=True)
        block_out, d_x, grad_list = block_fwd_bwd(x_rows, grad_out, gain_full, wq_full, bq_full, wk_full, bk_full, wv_full, bv_full, wo_full)
        all_dx = lax.all_gather(d_x, "fsdp")
        seg_idx = jnp.where(is_owned, local_idx, rows_dev)
        grad_part = jax.ops.segment_sum(all_dx.reshape(-1, model_width), seg_idx.reshape(-1), num_segments=rows_dev)
        reduced = tuple(lax.psum_scatter(grad_full, "fsdp", scatter_dimension=0, tiled=True) for grad_full in grad_list)
        return (block_out, grad_part.astype(jnp.bfloat16)) + reduced

    return jax.shard_map(device_step, mesh=mesh, in_specs=in_specs, out_specs=out_specs, check_vma=False)
```

profile of v0, /device:TPU:0, one launch (start us, length us, event | category | flops | bytes accessed | tf_op | source)
XLA Modules:
  0.0 3296.9 jit_solution(8875034995321657282)
XLA Ops:
  8.0 14.2 all-gather.2
  23.5 579.4 %gather_fusion = bf16[16384,2048]{1,0:T(8,128)(2,1)} fusion(bf16[18992,2048]{1,0:T(8,128)(2,1)} %param.13, s32[16384]{0:T(1024)S(1)} %broadcast_clamp_fusion.1), kind=kCustom, calls=%fused_computation | custom fusion | bytes 134283264 | tf_op jit(solution)/shard_map/jit(_take)/gather | solution.py:108
  603.0 44.6 %select_select_fusion = bf16[8,2,1024,2048]{3,2,1,0:T(8,128)(2,1)} fusion(bf16[8,2,1024,2048]{3,2,1,0:T(8,128)(2,1)} %bitcast.1, pred[8,2,1024]{2,1,0:T(4,128)(4,1)S(1)} %get-tuple-element.40, pred[8,2,1024]{2,1,0:T(4,128)(4,1)S(1)} %get-tuple-element.39), kind=kLoop, calls=%fused_computation.22 | loop fusion | flops 67108864 | bytes 134250496 | tf_op jit(solution)/shard_map/jit(_where)/select_n | solution.py:109
  651.0 285.1 %all-gather.4 = bf16[8,1,256]{2,1,0:T(2,128)(2,1)S(1)} all-gather(bf16[1,1,256]{2,1,0:T(2,128)(2,1)S(1)} %reshape.245), channel_id=1, replica_groups=mesh['fsdp'=8] {'fsdp'}, dimensions={0}, use_global_device_ids=true | all-gather | bytes 4608 | tf_op jit(solution)/shard_map/all_gather | solution.py:117
  936.7 10.7 all-gather.5
  947.4 10.7 all-gather.6
  958.2 11.2 all-gather.3
  972.8 7.4 copy.140
  980.3 23.6 fusion.75
  1003.9 12.0 copy.122
  1015.9 281.6 %reduce-scatter.6.cloned.1.call-done = bf16[1,2,1024,2048]{3,2,1,0:T(8,128)(2,1)} async-done(((bf16[8,2,1024,2048]{3,2,1,0:T(8,128)(2,1)}), bf16[1,2,1024,2048]{3,2,1,0:T(8,128)(2,1)}) %reduce-scatter.6.cloned.1.call-update) | async-done | bytes 8388624 | tf_op jit(solution)/shard_map/reduce_scatter | solution.py:110
  1302.7 45.1 %all-gather.17.cloned.1.call-done = bf16[2048,2048]{1,0:T(8,128)(2,1)} async-done(((bf16[256,2048]{1,0:T(8,128)(2,1)}), bf16[2048,2048]{1,0:T(8,128)(2,1)}) %all-gather.17.cloned.1.call-update) | async-done | bytes 8388624 | tf_op jit(solution)/shard_map/all_gather | solution.py:112
  1347.7 24.4 broadcast_add_fusion
  1372.1 18.0 copy.121
  1390.1 7.7 all-gather.15.cloned.1.call-done
  1397.8 24.4 broadcast_add_fusion.1
  1422.2 18.0 copy.120
  1440.2 11.4 slice_negate_fusion.3
  1451.6 11.3 slice_negate_fusion.2
  1462.9 29.8 fusion.39
  1492.7 51.0 %fusion.11 = (f32[2,16,1024]{2,1,0:T(8,128)S(1)}, f32[2,16,1024,1024]{3,2,1,0:T(8,128)}) fusion(pred[1024,1024]{0,1:T(8,128)(4,1)S(1)} %copy-done, bf16[2,1024,16,128]{1,3,2,0:T(8,128)(2,1)} %get-tuple-element.32, bf16[2,1024,16,128]{1,3,2,0:T(8,128)(2,1)} %get-tuple-element.31), kind=kOutput, calls=%fused_computation.15 | convolution fusion | flops 8690565120 | bytes 152174592 | tf_op jit(solution)/shard_map/bqkgd,bskd->bkgqs/dot_general | solution.py:52
  1543.7 41.1 %fusion.10 = f32[2,16,1024]{2,1,0:T(8,128)S(1)} fusion(f32[2,16,1024,1024]{3,2,1,0:T(8,128)} %get-tuple-element.42, f32[2,16,1024]{2,1,0:T(8,128)S(1)} %get-tuple-element.41, pred[1024,1024]{0,1:T(8,128)(4,1)S(1)} %copy-done), kind=kLoop, calls=%fused_computation.14 | loop fusion | flops 134184960 | bytes 135528448 | tf_op jit(solution)/shard_map/reduce_sum | solution.py:55
  1584.9 58.8 %bitcast_convert_fusion = (bf16[2,1024,16,128]{1,3,2,0:T(8,128)(2,1)}, f32[2,16,128,1024]{3,2,1,0:T(8,128)}) fusion(bf16[2,1024,16,128]{1,3,2,0:T(8,128)(2,1)} %bitcast.233, f32[2,16,1024]{2,1,0:T(8,128)S(1)} %fusion.10, f32[2,16,1024]{2,1,0:T(8,128)S(1)} %get-tuple-element.41, f32[2,16,1024,1024]{3,2,1,0:T(8,128)} %get-tuple-element.42, ...), kind=kOutput, calls=%fused_computation.55 | convolution fusion | flops 8761901056 | bytes 169082880 | tf_op jit(solution)/shard_map/bkgqs,bqkgd->bskd/dot_general | solution.py:66
  1643.8 24.3 fusion.41
  1668.1 106.9 %fusion.5 = (f32[2,16,1024]{2,1,0:T(8,128)S(1)}, f32[2,16,1024,1024]{3,2,1,0:T(8,128)}) fusion(f32[2,16,1024]{2,1,0:T(8,128)S(1)} %fusion.10, f32[2,16,1024]{2,1,0:T(8,128)S(1)} %get-tuple-element.41, f32[2,16,1024,1024]{3,2,1,0:T(8,128)} %get-tuple-element.42, pred[1024,1024]{0,1:T(8,128)(4,1)S(1)} %copy-done, bf16[2,1024,16,128]{1,3,2,0:T(8,128)(2,1)} %bitcast.234, ...), kind=kOutput, calls=%fused_computation.8 | convolution fusion | flops 8791228416 | bytes 286654464 | tf_op jit(solution)/shard_map/bqkgd,bskd->bkgqs/dot_general | solution.py:65
  1775.0 104.4 %fusion.13 = bf16[2,16,1024,1024]{2,3,1,0:T(8,128)(2,1)} fusion(f32[2,16,1024,1024]{3,2,1,0:T(8,128)} %get-tuple-element.44, f32[2,16,1024]{2,1,0:T(8,128)S(1)} %get-tuple-element.43, f32[2,16,1024]{2,1,0:T(8,128)S(1)} %fusion.10, f32[2,16,1024]{2,1,0:T(8,128)S(1)} %get-tuple-element.41, f32[2,16,1024,1024]{3,2,1,0:T(8,128)} %get-tuple-element.42, ...), kind=kLoop, calls=%fused_computation.17 | loop fusion | flops 268435456 | bytes 336986112 | tf_op jit(solution)/shard_map/reshape.10
  1879.4 31.7 fusion.100
  1911.1 49.4 %bitcast_multiply_fusion.3 = (f32[2,1024,16,128]{1,3,2,0:T(8,128)}, f32[2,1024,16,128]{1,3,2,0:T(8,128)}, f32[2,16,128,1024]{3,2,1,0:T(8,128)}) fusion(f32[1024,128]{0,1:T(8,128)S(1)} %copy-done.3, f32[2,16,128,1024]{3,2,1,0:T(8,128)} %fusion.100, bf16[2,1024,16,128]{1,3,2,0:T(8,128)(2,1)} %get-tuple-element.31, bf16[2,16,1024,1024]{2,3,1,0:T(8,128)(2,1)} %fusion.13), kind=kOutput, calls=%fused_computation.56 | convolution fusion | flops 8598323200 | bytes 143130624 | tf_op jit(solution)/shard_map/bkgqs,bqkgd->bskd/dot_general | solution.py:70
  1960.4 22.6 fusion.98
  1983.0 35.4 %fusion.91 = (f32[16,128]{1,0:T(8,128)}, f32[16,128]{1,0:T(8,128)}, bf16[2,1024,16,128]{1,3,2,0:T(8,128)(2,1)}, bf16[2,1024,16,128]{1,3,2,0:T(8,128)(2,1)}, f32[2,1024,16,128]{1,3,2,0:T(8,128)}) fusion(f32[2,1024,16,64]{1,3,2,0:T(8,128)} %get-tuple-element.24, f32[2,1024,16,64]{1,3,2,0:T(8,128)} %get-tuple-element.23, f32[1024,128]{0,1:T(8,128)S(1)} %copy-done.6, ...), kind=kLoop, calls=%fused_computation.101 | loop fusion | flops 41938944 | bytes 101203968 | tf_op jit(solution)/shard_map/reduce_sum | solution.py:76
  2018.4 17.3 copy.93
  2035.7 17.3 copy.92
  2053.1 24.4 fusion.54
  2077.5 28.0 fusion.42
  2105.5 35.0 %fusion.31 = (f32[2048]{0:T(1024)}, f32[2,1024]{1,0:T(2,128)S(1)}, f32[2,1024,2048]{2,1,0:T(8,128)}) fusion(bf16[1,2,1024,2048]{3,2,1,0:T(8,128)(2,1)} %reduce-scatter.6.cloned.1.call-done, f32[2,1024]{1,0:T(2,128)S(1)} %copy-done.20, f32[2048]{0:T(1024)S(1)} %bitcast.243, bf16[2,1024,2048]{1,2,0:T(8,128)(2,1)} %bitcast.257, ...), kind=kOutput, calls=%fused_computation.38 | convolution fusion | flops 17217613824 | bytes 75530240 | tf_op jit(solution)/shard_map/blo,io->bli/dot_general | solution.py:86
  2140.5 17.1 fusion.30
  2158.9 54.1 %fusion.78 = bf16[2,16,128,1024]{3,2,1,0:T(8,128)(2,1)} fusion(bf16[2,128,16,8,128]{4,3,2,1,0:T(8,128)(2,1)} %fusion.41, f32[2,16,1024]{2,1,0:T(8,128)S(1)} %copy-done.12, f32[2,16,1024]{2,1,0:T(8,128)S(1)} %copy-done.8, f32[2,16,1024,1024]{3,2,1,0:T(8,128)} %get-tuple-element.42, pred[1024,1024]{0,1:T(8,128)(4,1)S(1)} %copy-done.1), kind=kOutput, calls=%fused_computation.99 | convolution fusion | flops 8761901056 | bytes 152305664 | tf_op jit(solution)/shard_map/bkgqs,bskd->bqkgd/dot_general | solution.py:57
  2213.0 24.2 convolution_bitcast_fusion
  2237.9 26.7 convolution_bitcast_fusion.1
  2264.6 26.4 convolution_bitcast_fusion.2
  2291.1 26.9 convolution_bitcast_fusion.3
  2318.9 7.1 sort
  2326.1 6.6 bitcast_reduce_fusion
  2332.7 23.5 all-reduce.4
  2358.7 24.4 fusion.33
  2383.1 357.3 %all-gather.21.cloned.1.call-done = f32[16,1024,2048]{2,1,0:T(8,128)} async-done(((f32[2,1024,2048]{2,1,0:T(8,128)}), f32[16,1024,2048]{2,1,0:T(8,128)}) %all-gather.21.cloned.1.call-update) | async-done | bytes 134217744 | tf_op jit(solution)/shard_map/all_gather | solution.py:120
  2740.4 475.7 %scatter_custom_fusion = f32[18992,2048]{1,0:T(8,128)} fusion(s32[16384]{0:T(1024)S(1)} %get-tuple-element.10, f32[16384,2048]{1,0:T(8,128)} %bitcast.31, s32[16384]{0:T(1024)S(1)} %broadcast_clamp_fusion, f32[]{:T(128)} %constant.20.clone.1), kind=kCustom, calls=%fused_computation.3 | custom fusion | flops 33554432 | bytes 155582976 | tf_op jit(solution)/shard_map/scatter-add | solution.py:122
  3216.1 73.6 %convert_element_type.123 = bf16[18992,2048]{1,0:T(8,128)(2,1)} convert(f32[18992,2048]{1,0:T(8,128)} %scatter_custom_fusion) | non-fusion elementwise | flops 38895616 | bytes 233373696 | tf_op jit(solution)/shard_map/convert_element_type | solution.py:124
  (114 shorter events, 20.1 us)
Async XLA Ops:
  7.2 973.1 %all-gather.19.cloned.1.call-start = ((), (), s32[]{:S(2)}) async-start(), calls=%async_computation.9 | async-start | bytes 9437184 | tf_op jit(solution)/shard_map/all_gather | solution.py:118
  7.9 1289.6 %reduce-scatter.6.cloned.1.call-start = ((), (), s32[]{:S(2)}) async-start(), calls=%async_computation.5 | async-start | bytes 75497472 | tf_op jit(solution)/shard_map/reduce_scatter | solution.py:110
  22.2 0.6 copy-start.9
  23.5 579.4 %copy-start.10 = (s32[8,2,1024]{2,1,0:T(2,128)S(1)}, s32[8,2,1024]{2,1,0:T(2,128)}, u32[]{:S(2)}) copy-start(s32[8,2,1024]{2,1,0:T(2,128)} %copy-done.9) | copy-start | bytes 196612
  647.6 3.3 copy-start.26
  647.6 3.3 copy-start.27
  647.6 3.3 copy-start.28
  647.7 3.3 copy-start.29
  647.7 700.0 %all-gather.17.cloned.1.call-start = ((), (), s32[]{:S(2)}) async-start(), calls=%async_computation.8 | async-start | bytes 9437184 | tf_op jit(solution)/shard_map/all_gather | solution.py:112
  648.4 749.3 %all-gather.15.cloned.1.call-start = ((), (), s32[]{:S(2)}) async-start(), calls=%async_computation.7 | async-start | bytes 9437184 | tf_op jit(solution)/shard_map/all_gather | solution.py:114
  649.0 994.8 %all-gather.13.cloned.1.call-start = ((), (), s32[]{:S(2)}) async-start(), calls=%async_computation.6 | async-start | bytes 9437184 | tf_op jit(solution)/shard_map/all_gather | solution.py:116
  649.6 2090.8 %all-gather.21.cloned.1.call-start = ((), (), s32[]{:S(2)}) async-start(), calls=%async_computation.14 | async-start | bytes 150994944 | tf_op jit(solution)/shard_map/all_gather | solution.py:120
  969.4 428.3 %copy-start.14 = (f32[8,1,256]{2,1,0:T(1,128)}, f32[8,1,256]{2,1,0:T(1,128)S(1)}, u32[]{:S(2)}) copy-start(f32[8,1,256]{2,1,0:T(1,128)S(1)} %convert_element_type.130) | copy-start | bytes 24580
  972.1 31.8 copy-start.4
  1302.6 95.1 %copy-start.18 = (f32[2,1024]{1,0:T(2,128)}, f32[2,1024]{1,0:T(2,128)S(1)}, u32[]{:S(2)}) copy-start(f32[2,1024]{1,0:T(2,128)S(1)} %add_rsqrt_fusion) | copy-start | bytes 24580
  1451.5 11.3 copy-start.2
  1451.5 11.3 copy-start.5
  1462.9 29.8 copy-start
  1543.7 231.3 %copy-start.7 = (f32[2,16,1024]{2,1,0:T(8,128)}, f32[2,16,1024]{2,1,0:T(8,128)S(1)}, u32[]{:S(2)}) copy-start(f32[2,16,1024]{2,1,0:T(8,128)S(1)} %get-tuple-element.41) | copy-start | bytes 393220
  1584.9 190.2 %copy-start.11 = (f32[2,16,1024]{2,1,0:T(8,128)}, f32[2,16,1024]{2,1,0:T(8,128)S(1)}, u32[]{:S(2)}) copy-start(f32[2,16,1024]{2,1,0:T(8,128)S(1)} %fusion.10) | copy-start | bytes 393220
  1584.9 58.9 %copy-start.15 = (f32[8,1,256]{2,1,0:T(1,128)S(1)}, f32[8,1,256]{2,1,0:T(1,128)}, u32[]{:S(2)}) copy-start(f32[8,1,256]{2,1,0:T(1,128)} %copy-done.14) | copy-start | bytes 24580
  1584.9 58.9 %copy-start.19 = (f32[2,1024]{1,0:T(2,128)S(1)}, f32[2,1024]{1,0:T(2,128)}, u32[]{:S(2)}) copy-start(f32[2,1024]{1,0:T(2,128)} %copy-done.18) | copy-start | bytes 24580
  1584.9 58.9 %copy-start.24 = (f32[8,1,256]{2,1,0:T(1,128)S(1)}, f32[8,1,256]{2,1,0:T(1,128)}, u32[]{:S(2)}) copy-start(f32[8,1,256]{2,1,0:T(1,128)} %convert_element_type.131) | copy-start | bytes 24580
  1879.4 31.7 copy-start.3
  1960.4 22.6 copy-start.6
  2077.5 28.0 copy-start.16
  2077.5 28.0 copy-start.20
  2157.6 1.2 copy-start.1
  2157.6 1.2 copy-start.8
  2157.6 1.3 copy-start.12
  2157.6 1132.0 %reduce-scatter.14.cloned.1.call-start = ((), (), s32[]{:S(2)}) async-start(), calls=%async_computation.13 | async-start | bytes 18874368 | tf_op jit(solution)/shard_map/reduce_scatter | solution.py:123
  2237.1 0.7 copy-start.17
  2237.2 0.7 copy-start.21
  2237.2 1052.5 %reduce-scatter.12.cloned.1.call-start = ((), (), s32[]{:S(2)}) async-start(), calls=%async_computation.12 | async-start | bytes 18874368 | tf_op jit(solution)/shard_map/reduce_scatter | solution.py:123
  2264.6 1025.1 %reduce-scatter.10.cloned.1.call-start = ((), (), s32[]{:S(2)}) async-start(), calls=%async_computation.11 | async-start | bytes 18874368 | tf_op jit(solution)/shard_map/reduce_scatter | solution.py:123
  2291.1 998.6 %reduce-scatter.8.cloned.1.call-start = ((), (), s32[]{:S(2)}) async-start(), calls=%async_computation.10 | async-start | bytes 18874368 | tf_op jit(solution)/shard_map/reduce_scatter | solution.py:123
  2318.1 0.8 copy-start.13
  2318.1 14.6 copy-start.22
  2318.1 14.6 copy-start.23
  2318.1 14.6 copy-start.25
Sparse Core Ops, SparseCore 0:
  9.8 51.3 all-gather.18
  647.8 649.6 reduce-scatter.5
  1299.4 48.3 all-gather.16
  1349.4 48.3 all-gather.14
  1399.4 48.3 all-gather.12
  2157.8 582.5 all-gather.20
  2744.5 106.9 reduce-scatter.13
  2855.5 106.9 reduce-scatter.11
  2966.5 106.9 reduce-scatter.9
  3077.4 106.9 reduce-scatter.7
where the time goes:
time: 3320 us; the launch traced here: 3300 us
  other arithmetic  891 us (27%)
  waiting for transfers between devices  694 us (21%)
  local copies, waits for them, and re-layouts  676 us (20%)
  matrix products  665 us (20%)
  blocking collectives  355 us (11%)
    gather x1, local copies, waits for them, and re-layouts, device_step(): looked = jnp.take(table_part, jnp.where(is_owned, local_idx, 0), axis=0)  579 us
    scatter-add x3, other arithmetic, device_step(): jax.ops.segment_sum(all_dx.reshape(-1, model_width), seg_idx.reshape(-1),...  483 us
    all_gather x1, waiting for transfers between devices, device_step(): all_dx = lax.all_gather(d_x, 'fsdp')  357 us
    all_gather x1, blocking collectives, device_step(): bv_full = lax.all_gather(bv_part, 'fsdp', axis=0, tiled=True)  285 us
    reduce_scatter x1, waiting for transfers between devices, device_step(): x_rows = lax.psum_scatter(looked, 'fsdp', scatter_dimension=0)  282 us
    dot_general x1, matrix products, block_fwd_bwd(): jnp.einsum('bqkgd,bskd->bkgqs', d_attn, v_val, preferred_element_type=jnp...  107 us
    another operation x1, other arithmetic  104 us
    convert_element_type x1, other arithmetic, device_step(): return (block_out, grad_part.astype(jnp.bfloat16)) + reduced  73.6 us
  transfers between devices with their start and end apart: 10, of which 4 were waited for; matrix products, arithmetic and copies ran while one was open for 52% of the time, Pallas kernels for 0%

commit v1 on v0

v1 whole, which is shorter than its diff:
```python
import functools

import jax
import jax.numpy as jnp
from jax import lax
from jax.experimental import pallas as pl
from jax.experimental.pallas import tpu as pltpu
from jax.sharding import PartitionSpec as P

HEAD_DIM = 128
ROPE_THETA = 1.0e6
NORM_EPS = 1e-6
MASK_VALUE = -1e30
AXIS = "fsdp"
N_DEV = 8
HOT = 4096
CAP = 192
LANES = 128
BIG = 2**31 - 1
MESH = pl.DeviceIdType.MESH
BLOCK_Q = 256
ROW_BLOCK = 128
VMEM_MAX = 60 * 1024 * 1024


def dot_nn(a, b):
    return lax.dot_general(a, b, (((1,), (0,)), ((), ())), preferred_element_type=jnp.float32)


def dot_nt(a, b):
    return lax.dot_general(a, b, (((1,), (1,)), ((), ())), preferred_element_type=jnp.float32)


def attn_kernel(q_ref, k_ref, v_ref, do_ref, cos_ref, sin_ref, bq_ref, bk_ref,
                o_ref, dq_ref, dk_ref, dv_ref, gb_ref, qs, ks, dkt, dvt):
    seq_len = q_ref.shape[0]
    score_scale = HEAD_DIM ** -0.5
    cos_t = cos_ref[...]
    sin_t = sin_ref[...]
    half = HEAD_DIM // 2
    q_lin = q_ref[...] + bq_ref[...]
    qs[...] = (q_lin * cos_t + pltpu.roll(q_lin, half, 1) * sin_t).astype(jnp.bfloat16)
    k_lin = k_ref[...] + bk_ref[...]
    ks[...] = (k_lin * cos_t + pltpu.roll(k_lin, half, 1) * sin_t).astype(jnp.bfloat16)
    row_i = lax.broadcasted_iota(jnp.int32, (BLOCK_Q, BLOCK_Q), 0)
    col_i = lax.broadcasted_iota(jnp.int32, (BLOCK_Q, BLOCK_Q), 1)
    causal = row_i >= col_i
    n_blocks = seq_len // BLOCK_Q
    gbq = jnp.zeros((1, HEAD_DIM), jnp.float32)
    for blk in reversed(range(n_blocks)):
        lo = blk * BLOCK_Q
        width = lo + BLOCK_Q
        q_b = qs[pl.ds(lo, BLOCK_Q), :]
        do_b = do_ref[pl.ds(lo, BLOCK_Q), :]
        k_all = ks[pl.ds(0, width), :]
        v_all = v_ref[pl.ds(0, width), :]
        scores = dot_nt(q_b, k_all) * score_scale
        tail = jnp.where(causal, scores[:, lo:], MASK_VALUE)
        scores = jnp.concatenate([scores[:, :lo], tail], axis=1) if lo else tail
        top = jnp.max(scores, axis=1, keepdims=True)
        prob = jnp.exp(scores - top)
        prob = prob * (1.0 / jnp.sum(prob, axis=1, keepdims=True))
        prob_b = prob.astype(jnp.bfloat16)
        o_ref[pl.ds(lo, BLOCK_Q), :] = dot_nn(prob_b, v_all).astype(jnp.bfloat16)
        d_prob = dot_nt(do_b, v_all)
        inner = jnp.sum(d_prob * prob, axis=1, keepdims=True)
        d_score = ((prob * (d_prob - inner)) * score_scale).astype(jnp.bfloat16)
        d_q = dot_nn(d_score, k_all)
        scaled = d_q * sin_ref[pl.ds(lo, BLOCK_Q), :]
        d_q = d_q * cos_ref[pl.ds(lo, BLOCK_Q), :] + pltpu.roll(scaled, half, 1)
        gbq = gbq + jnp.sum(d_q, axis=0, keepdims=True)
        dq_ref[pl.ds(lo, BLOCK_Q), :] = d_q.astype(jnp.bfloat16)
        dv_part = dot_nn(do_b.T, prob_b)
        dk_part = dot_nn(q_b.T, d_score)
        if blk == n_blocks - 1:
            dvt[...] = dv_part
            dkt[...] = dk_part
        else:
            dvt[:, pl.ds(0, width)] += dv_part
            dkt[:, pl.ds(0, width)] += dk_part
    d_v = dvt[...].T
    d_k = dkt[...].T
    d_k = d_k * cos_t + pltpu.roll(d_k * sin_t, half, 1)
    dv_ref[...] = d_v.astype(jnp.bfloat16)
    dk_ref[...] = d_k.astype(jnp.bfloat16)
    gb_ref[0, 0:1, :] = gbq
    gb_ref[0, 1:2, :] = jnp.sum(d_k, axis=0, keepdims=True)
    gb_ref[0, 2:3, :] = jnp.sum(d_v, axis=0, keepdims=True)
    gb_ref[0, 3:8, :] = jnp.zeros((5, HEAD_DIM), jnp.float32)


def attention(q_lin, k_lin, v_val, d_attn, b_q, b_k, seq_len):
    tokens, width = q_lin.shape
    n_seq, n_heads = tokens // seq_len, width // HEAD_DIM
    half = HEAD_DIM // 2
    inv_freq = jnp.power(ROPE_THETA, -(jnp.arange(half, dtype=jnp.float32) * 2.0 / HEAD_DIM))
    angles = jnp.arange(seq_len, dtype=jnp.float32)[:, None] * inv_freq[None, :]
    cos_t = jnp.concatenate([jnp.cos(angles)] * 2, axis=-1)
    sin_t = jnp.concatenate([-jnp.sin(angles), jnp.sin(angles)], axis=-1)
    tile = pl.BlockSpec((seq_len, HEAD_DIM), lambda s, h: (s, h))
    table = pl.BlockSpec((seq_len, HEAD_DIM), lambda s, h: (0, 0))
    bias = pl.BlockSpec((1, HEAD_DIM), lambda s, h: (0, h))
    act = jax.ShapeDtypeStruct((tokens, width), jnp.bfloat16)
    pairs = n_seq * n_heads * seq_len * seq_len
    return pl.pallas_call(
        attn_kernel,
        grid=(n_seq, n_heads),
        in_specs=[tile, tile, tile, tile, table, table, bias, bias],
        out_specs=[tile, tile, tile, tile, pl.BlockSpec((1, 8, HEAD_DIM), lambda s, h: (s, 0, h))],
        out_shape=[act, act, act, act, jax.ShapeDtypeStruct((n_seq, 8, width), jnp.float32)],
        scratch_shapes=[
            pltpu.VMEM((seq_len, HEAD_DIM), jnp.bfloat16),
            pltpu.VMEM((seq_len, HEAD_DIM), jnp.bfloat16),
            pltpu.VMEM((HEAD_DIM, seq_len), jnp.float32),
            pltpu.VMEM((HEAD_DIM, seq_len), jnp.float32),
        ],
        compiler_params=pltpu.CompilerParams(
            dimension_semantics=("arbitrary", "arbitrary"), vmem_limit_bytes=VMEM_MAX),
        cost_estimate=pl.CostEstimate(
            flops=6 * 2 * HEAD_DIM * pairs, bytes_accessed=24 * tokens * width, transcendentals=pairs),
        name="attn_fwd_bwd",
    )(q_lin, k_lin, v_val, d_attn, cos_t, sin_t, b_q.astype(jnp.float32)[None], b_k.astype(jnp.float32)[None])


def block_fwd_bwd(x_rows, grad_out, seq_len, gain_vec, w_query, b_query, w_key, b_key, w_value, b_value, w_out):
    f32 = jnp.float32
    x_full = x_rows.astype(f32)
    inv_rms = lax.rsqrt(jnp.mean(x_full * x_full, axis=-1, keepdims=True) + NORM_EPS)
    x_norm = x_full * inv_rms
    gain_f = gain_vec.astype(f32)
    hidden = (x_norm * gain_f).astype(jnp.bfloat16)
    d_attn = dot_nt(grad_out, w_out).astype(jnp.bfloat16)
    q_lin = dot_nn(hidden, w_query)
    k_lin = dot_nn(hidden, w_key)
    v_val = (dot_nn(hidden, w_value) + b_value.astype(f32)).astype(jnp.bfloat16)
    attn_b, dq_b, dk_b, dv_b, grad_b = attention(q_lin, k_lin, v_val, d_attn, b_query, b_key, seq_len)
    block_out = (x_full + dot_nn(attn_b, w_out)).astype(jnp.bfloat16)
    tn = (((0,), (0,)), ((), ()))
    grad_wo = lax.dot_general(attn_b, grad_out, tn, preferred_element_type=f32)
    d_hidden = dot_nt(dq_b, w_query) + dot_nt(dk_b, w_key) + dot_nt(dv_b, w_value)
    grad_gain = jnp.sum(d_hidden * x_norm, axis=0)
    d_norm = d_hidden * gain_f
    d_x = grad_out.astype(f32) + inv_rms * (d_norm - x_norm * jnp.mean(d_norm * x_norm, axis=-1, keepdims=True))
    grad_wq = lax.dot_general(hidden, dq_b, tn, preferred_element_type=f32)
    grad_wk = lax.dot_general(hidden, dk_b, tn, preferred_element_type=f32)
    grad_wv = lax.dot_general(hidden, dv_b, tn, preferred_element_type=f32)
    grad_b = jnp.sum(grad_b, axis=0)
    vecs = (grad_gain, grad_b[0], grad_b[1], grad_b[2])
    return block_out, d_x, (grad_wq, grad_wk, grad_wv, grad_wo), vecs


def barrier_all(me):
    barrier = pltpu.get_barrier_semaphore()
    for step in range(1, N_DEV):
        pl.semaphore_signal(barrier, inc=1, device_id=(jnp.bitwise_xor(me, step),), device_id_type=MESH)
    pl.semaphore_wait(barrier, N_DEV - 1)


LOOK_CHUNK = 128
LOOK_N = HOT // 2 // LOOK_CHUNK


def lookup_kernel(cold_ref, _, rows_ref, recv_sem, link_sem, mate_sem, c_send, c_recv, l_sem):
    me = lax.axis_index(AXIS)
    chip, core = me // 2, me % 2
    barrier_all(me)
    own = pltpu.make_async_copy(cold_ref.at[me], rows_ref.at[pl.ds(HOT + me * CAP, CAP)], l_sem)
    own.start()

    def cold_copy(step):
        peer = jnp.bitwise_xor(me, step)
        return pltpu.make_async_remote_copy(
            src_ref=cold_ref.at[peer], dst_ref=rows_ref.at[pl.ds(HOT + me * CAP, CAP)],
            send_sem=c_send.at[step - 1], recv_sem=c_recv.at[step - 1],
            device_id=(peer,), device_id_type=MESH)

    def piece(part, k):
        return rows_ref.at[pl.ds(part * (HOT // 2) + k * LOOK_CHUNK, LOOK_CHUNK)]

    def link_copy(part, k, target):
        return pltpu.make_async_remote_copy(
            src_ref=piece(part, k), dst_ref=piece(part, k), send_sem=link_sem.at[part, k],
            recv_sem=recv_sem.at[part, k], device_id=(target,), device_id_type=MESH)

    def mate_copy(part, k):
        return pltpu.make_async_remote_copy(
            src_ref=piece(part, k), dst_ref=piece(part, k), send_sem=mate_sem.at[part, k],
            recv_sem=recv_sem.at[part, k], device_id=(jnp.bitwise_xor(me, 1),), device_id_type=MESH)

    place = [
        jnp.where(chip == 0, 0, jnp.where(chip == 1, 1, jnp.where(chip == 3, 2, 3))),
        jnp.where(chip == 0, 0, jnp.where(chip == 2, 1, jnp.where(chip == 3, 2, 3))),
    ]
    target = [
        2 * jnp.where(chip == 0, 1, jnp.where(chip == 1, 3, 2)),
        2 * jnp.where(chip == 0, 2, jnp.where(chip == 2, 3, 1)),
    ]

    def stage(step, carry):
        for part in range(2):
            k = step - place[part]
            live = (k >= 0) & (k < LOOK_N)

            @pl.when(live & (me != 0))
            def _():
                mate_copy(part, k).wait_recv()

            @pl.when(live & (core == 0) & (place[part] < 3))
            def _():
                link_copy(part, k, target[part]).start()

            @pl.when(live & (core == 0))
            def _():
                mate_copy(part, k).start()
        return carry

    for step in range(1, N_DEV):
        cold_copy(step).start()
    lax.fori_loop(0, LOOK_N + 3, stage, 0)

    def drain(k, carry):
        for part in range(2):
            @pl.when((core == 0) & (place[part] < 3))
            def _():
                link_copy(part, k, target[part]).wait_send()

            @pl.when(core == 0)
            def _():
                mate_copy(part, k).wait_send()
        return carry

    lax.fori_loop(0, LOOK_N, drain, 0)
    for step in range(1, N_DEV):
        cold_copy(step).wait()
    own.wait()


def lookup_exchange(cold_send, rows_in):
    any_spec = pl.BlockSpec(memory_space=pl.ANY)
    dma = pltpu.SemaphoreType.DMA
    return pl.pallas_call(
        lookup_kernel,
        out_shape=jax.ShapeDtypeStruct(rows_in.shape, rows_in.dtype),
        in_specs=[any_spec, any_spec],
        out_specs=any_spec,
        scratch_shapes=[dma((2, LOOK_N)), dma((2, LOOK_N)), dma((2, LOOK_N)), dma((N_DEV - 1,)), dma((N_DEV - 1,)), dma],
        input_output_aliases={1: 0},
        compiler_params=pltpu.CompilerParams(collective_id=0, has_side_effects=True),
        name="lookup_exchange",
    )(cold_send, rows_in)


def pick_kernel(idx_ref, rows_ref, out_ref):
    base = pl.program_id(0) * out_ref.shape[0]

    def body(step, carry):
        for j in range(8):
            i = step * 8 + j
            out_ref[i] = rows_ref[idx_ref[base + i]]
        return carry

    lax.fori_loop(0, out_ref.shape[0] // 8, body, 0)


def pick_rows(idx, rows, block):
    count = idx.shape[0]
    tail = rows.shape[1:]
    zeros = (0,) * len(tail)
    return pl.pallas_call(
        pick_kernel,
        grid_spec=pltpu.PrefetchScalarGridSpec(
            num_scalar_prefetch=1,
            grid=(count // block,),
            in_specs=[pl.BlockSpec(rows.shape, lambda i, s: (0,) + zeros, pipeline_mode=pl.Buffered(1))],
            out_specs=pl.BlockSpec((block,) + tail, lambda i, s: (i,) + zeros),
        ),
        out_shape=jax.ShapeDtypeStruct((count,) + tail, rows.dtype),
        compiler_params=pltpu.CompilerParams(dimension_semantics=("arbitrary",), vmem_limit_bytes=VMEM_MAX),
        name="pick_rows",
    )(idx, rows)


def take2d_kernel(idx_ref, rows_ref, out_ref):
    base = pl.program_id(0) * out_ref.shape[0]

    def body(step, carry):
        for j in range(8):
            i = step * 8 + j
            out_ref[pl.ds(i, 1), :] = rows_ref[pl.ds(idx_ref[base + i], 1), :]
        return carry

    lax.fori_loop(0, out_ref.shape[0] // 8, body, 0)


def take2d(idx, rows, block):
    count = idx.shape[0]
    width = rows.shape[1]
    return pl.pallas_call(
        take2d_kernel,
        grid_spec=pltpu.PrefetchScalarGridSpec(
            num_scalar_prefetch=1,
            grid=(count // block,),
            in_specs=[pl.BlockSpec(rows.shape, lambda i, s: (0, 0), pipeline_mode=pl.Buffered(1))],
            out_specs=pl.BlockSpec((block, width), lambda i, s: (i, 0)),
        ),
        out_shape=jax.ShapeDtypeStruct((count, width), rows.dtype),
        compiler_params=pltpu.CompilerParams(dimension_semantics=("arbitrary",), vmem_limit_bytes=VMEM_MAX),
        name="take_rows",
    )(idx, rows)


def seg_sum_kernel(key_ref, off_ref, mine_ref, mate_ref, out_ref, src, sem):
    blk = pl.program_id(0)
    count = mine_ref.shape[0]

    @pl.when(blk == 0)
    def _():
        first = pltpu.make_async_copy(mine_ref, src.at[pl.ds(0, count)], sem.at[0])
        second = pltpu.make_async_copy(mate_ref, src.at[pl.ds(count, count)], sem.at[1])
        first.start()
        second.start()
        first.wait()
        second.wait()

    out_ref[...] = jnp.zeros_like(out_ref)

    def body(e, carry):
        key = key_ref[e]
        row = lax.shift_right_logical(key, 12) - blk * ROW_BLOCK
        tok = jnp.bitwise_and(key, 4095)
        out_ref[pl.ds(row, 1), :] += src[pl.ds(tok, 1), :]
        return carry

    lax.fori_loop(off_ref[blk], off_ref[blk + 1], body, 0)


def seg_sum(keys, offs, dx_mine, dx_mate, n_rows):
    tokens, width = dx_mine.shape
    any_spec = pl.BlockSpec(memory_space=pl.ANY)
    return pl.pallas_call(
        seg_sum_kernel,
        grid_spec=pltpu.PrefetchScalarGridSpec(
            num_scalar_prefetch=2,
            grid=(n_rows // ROW_BLOCK,),
            in_specs=[any_spec, any_spec],
            out_specs=pl.BlockSpec((ROW_BLOCK, width), lambda i, a, b: (i, 0)),
            scratch_shapes=[pltpu.VMEM((2 * tokens, width), jnp.float32), pltpu.SemaphoreType.DMA((2,))],
        ),
        out_shape=jax.ShapeDtypeStruct((n_rows, width), jnp.float32),
        compiler_params=pltpu.CompilerParams(dimension_semantics=("arbitrary",), vmem_limit_bytes=VMEM_MAX),
        name="hot_seg_sum",
    )(keys, offs, dx_mine, dx_mate)


RED_CHUNK = 64
RED_N = HOT // 2 // RED_CHUNK


def reduce_kernel(part_ref, cold_ref, vec_ref, hot_ref, crecv_ref, vrecv_ref,
                  local, incoming, load_sem, send_sem, recv_sem, out_sem, c_send, c_recv, v_send, v_recv, l_sem):
    me = lax.axis_index(AXIS)
    chip, core = me // 2, me % 2
    mid = jnp.where(core == 0, 1, 2)
    first = 3 - mid
    place = jnp.where(chip == first, 0, jnp.where(chip == 3, 1, jnp.where(chip == mid, 2, 3)))
    nxt = jnp.where(chip == first, 3, jnp.where(chip == 3, mid, 0))
    target = nxt * 2 + core

    def rows(k):
        return pl.ds(k * RED_CHUNK, RED_CHUNK)

    def load(k):
        return pltpu.make_async_copy(part_ref.at[rows(k)], local.at[rows(k)], load_sem.at[k])

    def send(k):
        return pltpu.make_async_remote_copy(
            src_ref=local.at[rows(k)], dst_ref=incoming.at[rows(k)], send_sem=send_sem.at[k],
            recv_sem=recv_sem.at[k], device_id=(target,), device_id_type=MESH)

    def put_own(k):
        return pltpu.make_async_copy(local.at[rows(k)], hot_ref.at[rows(k)], send_sem.at[k])

    def put_far(k):
        return pltpu.make_async_remote_copy(
            src_ref=local.at[rows(k)], dst_ref=hot_ref.at[pl.ds(HOT // 2 + k * RED_CHUNK, RED_CHUNK)],
            send_sem=send_sem.at[k], recv_sem=out_sem.at[k], device_id=(jnp.bitwise_xor(me, 1),), device_id_type=MESH)

    def cold_copy(step):
        peer = jnp.bitwise_xor(me, step)
        return pltpu.make_async_remote_copy(
            src_ref=cold_ref.at[peer], dst_ref=crecv_ref.at[me],
            send_sem=c_send.at[step - 1], recv_sem=c_recv.at[step - 1],
            device_id=(peer,), device_id_type=MESH)

    def vec_copy(step):
        peer = jnp.bitwise_xor(me, step)
        return pltpu.make_async_remote_copy(
            src_ref=vec_ref.at[peer], dst_ref=vrecv_ref.at[me],
            send_sem=v_send.at[step - 1], recv_sem=v_recv.at[step - 1],
            device_id=(peer,), device_id_type=MESH)

    def start_load(k, carry):
        load(k).start()
        return carry

    lax.fori_loop(0, RED_N, start_load, 0)
    barrier_all(me)
    own_c = pltpu.make_async_copy(cold_ref.at[me], crecv_ref.at[me], l_sem.at[0])
    own_v = pltpu.make_async_copy(vec_ref.at[me], vrecv_ref.at[me], l_sem.at[1])
    own_c.start()
    own_v.start()
    for step in range(1, N_DEV):
        vec_copy(step).start()
    for step in range(1, N_DEV):
        cold_copy(step).start()

    def stage(k, carry):
        @pl.when(k < RED_N)
        def _():
            load(k).wait()

        @pl.when((k < RED_N) & (place > 0))
        def _():
            send(k).wait_recv()
            local[rows(k), :] += incoming[rows(k), :]

        @pl.when((k >= 1) & (place < 3))
        def _():
            send(k - 1).start()

        @pl.when((k >= 1) & (me == 0))
        def _():
            put_own(k - 1).start()

        @pl.when((k >= 1) & (me == 1))
        def _():
            put_far(k - 1).start()
        return carry

    lax.fori_loop(0, RED_N + 1, stage, 0)

    def drain(k, carry):
        @pl.when(place < 3)
        def _():
            send(k).wait_send()

        @pl.when(me == 0)
        def _():
            put_own(k).wait()
            put_far(k).wait_recv()

        @pl.when(me == 1)
        def _():
            put_far(k).wait_send()
        return carry

    lax.fori_loop(0, RED_N, drain, 0)
    for step in range(1, N_DEV):
        vec_copy(step).wait()
        cold_copy(step).wait()
    own_c.wait()
    own_v.wait()


def grad_exchange(part, cold_send, vecs):
    any_spec = pl.BlockSpec(memory_space=pl.ANY)
    dma = pltpu.SemaphoreType.DMA
    width = part.shape[1]
    peers = dma((N_DEV - 1,))
    return pl.pallas_call(
        reduce_kernel,
        out_shape=[
            jax.ShapeDtypeStruct((HOT, width), jnp.float32),
            jax.ShapeDtypeStruct(cold_send.shape, cold_send.dtype),
            jax.ShapeDtypeStruct(vecs.shape, vecs.dtype),
        ],
        in_specs=[any_spec] * 3,
        out_specs=[any_spec] * 3,
        scratch_shapes=[
            pltpu.VMEM(part.shape, jnp.float32), pltpu.VMEM(part.shape, jnp.float32),
            dma((RED_N,)), dma((RED_N,)), dma((RED_N,)), dma((RED_N,)), peers, peers, peers, peers, dma((2,)),
        ],
        compiler_params=pltpu.CompilerParams(
            collective_id=1, has_side_effects=True, vmem_limit_bytes=VMEM_MAX),
        name="grad_exchange",
    )(part, cold_send, vecs)


def table_kernel(key_ref, off_ref, n_hot_ref, src_ref, hot_ref, out_ref, acc):
    blk = pl.program_id(0)
    is_hot = blk < n_hot_ref[0]

    @pl.when(is_hot)
    def _():
        acc[...] = hot_ref[...]

    @pl.when(jnp.logical_not(is_hot))
    def _():
        acc[...] = jnp.zeros_like(acc)

    def body(e, carry):
        key = key_ref[e]
        row = lax.shift_right_logical(key, 11) - blk * ROW_BLOCK
        idx = jnp.bitwise_and(key, 2047)
        acc[pl.ds(row, 1), :] += src_ref[pl.ds(idx, 1), :]
        return carry

    lax.fori_loop(off_ref[blk], off_ref[blk + 1], body, 0)
    out_ref[...] = acc[...].astype(out_ref.dtype)


def build_table(keys, offs, n_hot, src, hot, n_rows):
    width = src.shape[1]

    def hot_index(i, k, o, n):
        return (jnp.minimum(i, jnp.maximum(n[0] - 1, 0)), 0)

    return pl.pallas_call(
        table_kernel,
        grid_spec=pltpu.PrefetchScalarGridSpec(
            num_scalar_prefetch=3,
            grid=(pl.cdiv(n_rows, ROW_BLOCK),),
            in_specs=[
                pl.BlockSpec(src.shape, lambda i, k, o, n: (0, 0), pipeline_mode=pl.Buffered(1)),
                pl.BlockSpec((ROW_BLOCK, width), hot_index),
            ],
            out_specs=pl.BlockSpec((ROW_BLOCK, width), lambda i, k, o, n: (i, 0)),
            scratch_shapes=[pltpu.VMEM((ROW_BLOCK, width), jnp.float32)],
        ),
        out_shape=jax.ShapeDtypeStruct((n_rows, width), jnp.bfloat16),
        compiler_params=pltpu.CompilerParams(dimension_semantics=("arbitrary",), vmem_limit_bytes=VMEM_MAX),
        name="build_table",
    )(keys, offs, n_hot, src, hot)


def fast_lookup(all_ids, own_ids, table_part, me):
    rows_dev, width = table_part.shape
    tokens = own_ids.shape[0]
    first_row = me * rows_dev
    t_idx = jnp.arange(tokens, dtype=jnp.int32)
    mine = (all_ids >= HOT) & (all_ids >= first_row) & (all_ids < first_row + rows_dev)
    key = jnp.where(mine, t_idx[None, :] * 32768 + (all_ids - first_row), BIG)
    key = lax.sort(key, dimension=1)[:, :CAP]
    asked = key != BIG
    ask_row = jnp.where(asked, jnp.bitwise_and(key, 32767), 0)
    send = jnp.take(table_part, ask_row.reshape(-1), axis=0, mode="clip")
    tiles = (width // LANES, LANES)
    send = send.reshape((N_DEV, CAP) + tiles)
    rows_in = jnp.pad(table_part[:HOT].reshape((HOT,) + tiles), ((0, N_DEV * CAP), (0, 0), (0, 0)))
    rows_all = lookup_exchange(send, rows_in)
    owners = own_ids // rows_dev
    hit = (owners[None, :] == jnp.arange(N_DEV, dtype=jnp.int32)[:, None]) & (own_ids >= HOT)[None, :]
    place = jnp.cumsum(hit.astype(jnp.int32), axis=1) - 1 + jnp.arange(N_DEV, dtype=jnp.int32)[:, None] * CAP
    slot = jnp.sum(jnp.where(hit, place, 0), axis=0)
    idx = jnp.where(own_ids >= HOT, HOT + slot, own_ids)
    x_rows = pick_rows(idx, rows_all, 256).reshape(tokens, width)
    slot_tok = lax.sort(jnp.where(hit, t_idx[None, :], BIG), dimension=1)[:, :CAP]
    slot_tok = jnp.where(slot_tok == BIG, 0, slot_tok).reshape(-1)
    src = jnp.arange(N_DEV * CAP, dtype=jnp.int32).reshape(N_DEV, CAP)
    owner_keys = lax.sort(jnp.where(asked, ask_row * 2048 + src, BIG).reshape(-1))
    return x_rows, slot_tok, owner_keys


def block_offsets(keys, n_blocks, shift):
    edges = jnp.arange(n_blocks + 1, dtype=jnp.int32) * (ROW_BLOCK << shift)
    return jnp.sum(keys[None, :] < edges[:, None], axis=1).astype(jnp.int32)


def fast_table_grad(all_ids, own_ids, d_x, vecs, slot_tok, owner_keys, me, rows_dev):
    tokens, width = d_x.shape
    mate_of = [(i, i ^ 1) for i in range(N_DEV)]
    dx_mate = lax.ppermute(d_x, AXIS, mate_of)
    mate_ids = lax.dynamic_index_in_dim(all_ids, jnp.bitwise_xor(me, 1), 0, keepdims=False)
    pair_ids = jnp.concatenate([own_ids, mate_ids])
    base = (me % 2) * (HOT // 2)
    inside = (pair_ids >= base) & (pair_ids < base + HOT // 2)
    keys = jnp.where(inside, (pair_ids - base) * 4096 + jnp.arange(2 * tokens, dtype=jnp.int32), BIG)
    keys = lax.sort(keys)
    part = seg_sum(keys, block_offsets(keys, HOT // 2 // ROW_BLOCK, 12), d_x, dx_mate, HOT // 2)
    cold = take2d(slot_tok, d_x, 192).reshape(N_DEV, CAP, width)
    hot, recv, vec_recv = grad_exchange(part, cold, vecs)
    n_hot = jnp.where(me == 0, HOT // ROW_BLOCK, 0).astype(jnp.int32)[None]
    offs = block_offsets(owner_keys, pl.cdiv(rows_dev, ROW_BLOCK), 11)
    grad_part = build_table(owner_keys, offs, n_hot, recv.reshape(N_DEV * CAP, width), hot, rows_dev)
    return grad_part, jnp.sum(vec_recv, axis=0)


def slow_lookup(all_ids, table_part, me):
    rows_dev = table_part.shape[0]
    local_idx = all_ids - me * rows_dev
    is_owned = (local_idx >= 0) & (local_idx < rows_dev)
    looked = jnp.take(table_part, jnp.where(is_owned, local_idx, 0), axis=0)
    looked = jnp.where(is_owned[..., None], looked, jnp.zeros((), jnp.bfloat16))
    return lax.psum_scatter(looked, AXIS, scatter_dimension=0)


def slow_table_grad(all_ids, d_x, me, rows_dev):
    local_idx = all_ids - me * rows_dev
    is_owned = (local_idx >= 0) & (local_idx < rows_dev)
    all_dx = lax.all_gather(d_x, AXIS)
    seg_idx = jnp.where(is_owned, local_idx, rows_dev)
    grad_part = jax.ops.segment_sum(all_dx.reshape(-1, d_x.shape[-1]), seg_idx.reshape(-1), num_segments=rows_dev)
    return grad_part.astype(jnp.bfloat16)


def solution(mesh):
    row_spec = P(AXIS, None)
    vec_spec = P(AXIS)
    act_spec = P(AXIS, None, None)
    weight_specs = (vec_spec, row_spec, vec_spec, row_spec, vec_spec, row_spec, vec_spec, row_spec)
    in_specs = (row_spec, act_spec, row_spec) + weight_specs
    out_specs = (act_spec, row_spec) + weight_specs

    def run(fast, tok_ids, all_ids, grad_out, table_part, gain_part, wq_part, bq_part, wk_part, bk_part, wv_part, bv_part, wo_part):
        me = lax.axis_index(AXIS)
        rows_dev, width = table_part.shape
        n_seq, seq_len = tok_ids.shape
        own_ids = tok_ids.reshape(-1)

        def whole(part):
            return lax.all_gather(part, AXIS, axis=0, tiled=True)

        vec_parts = jnp.stack([gain_part, bq_part, bk_part, bv_part])
        vec_full = lax.all_gather(vec_parts, AXIS, axis=1, tiled=True)
        wo_full, wq_full, wk_full, wv_full = whole(wo_part), whole(wq_part), whole(wk_part), whole(wv_part)
        if fast:
            x_rows, slot_tok, owner_keys = fast_lookup(all_ids, own_ids, table_part, me)
        else:
            x_rows = slow_lookup(all_ids, table_part, me)
        grad_flat = grad_out.reshape(-1, width)
        block_out, d_x, w_grads, vecs = block_fwd_bwd(
            x_rows, grad_flat, seq_len, vec_full[0], wq_full, vec_full[1], wk_full, vec_full[2], wv_full, vec_full[3], wo_full)
        reduced = tuple(lax.psum_scatter(g, AXIS, scatter_dimension=0, tiled=True) for g in w_grads)
        part_w = gain_part.shape[0]
        vecs = jnp.stack(vecs).reshape(4, N_DEV, part_w).transpose(1, 0, 2)
        if fast:
            vecs = jnp.pad(vecs, ((0, 0), (0, 4), (0, 0)))
            grad_part, vec_sum = fast_table_grad(all_ids, own_ids, d_x, vecs, slot_tok, owner_keys, me, rows_dev)
        else:
            grad_part = slow_table_grad(all_ids, d_x, me, rows_dev)
            vec_sum = lax.psum_scatter(vecs, AXIS, scatter_dimension=0)
        gq, gk, gv, go = reduced
        return (block_out.reshape(grad_out.shape), grad_part, vec_sum[0], gq, vec_sum[1], gk, vec_sum[2], gv, vec_sum[3], go)

    def device_step(tok_ids, grad_out, table_part, *weights):
        rows_dev = table_part.shape[0]
        all_ids = lax.all_gather(tok_ids.reshape(-1), AXIS)
        owners = jnp.where(all_ids >= HOT, all_ids // rows_dev, -1)
        counts = jnp.sum((owners[None] == jnp.arange(N_DEV, dtype=jnp.int32)[:, None, None]).astype(jnp.int32), axis=-1)
        fits = jnp.max(counts) <= CAP
        args = (tok_ids, all_ids, grad_out, table_part) + weights
        return lax.cond(fits, functools.partial(run, True), functools.partial(run, False), *args)

    return jax.shard_map(device_step, mesh=mesh, in_specs=in_specs, out_specs=out_specs, check_vma=False)
```

time: 3320 us -> 1560 us (0.47)
  Pallas kernels: 0 us -> 1020 us
  other arithmetic: 891 us -> 94 us
  waiting for transfers between devices: 694 us -> 2.54 us
  local copies, waits for them, and re-layouts: 676 us -> 87.4 us
  matrix products: 665 us -> 309 us
  blocking collectives: 355 us -> 24.7 us
    pallas_call x0 -> x7, Pallas kernels: none -> 1020 us  [the longest x1 488 us: grad_exchange(): pl.pallas_call(reduce_kernel, out_shape=[jax.ShapeDtypeStruct((HOT, width...]
    gather x1, local copies, waits for them, and re-layouts: 579 us -> 32.7 us  [fast_lookup(): send = jnp.take(table_part, ask_row.reshape(-1), axis=0, mode='clip')]
    scatter-add x3 -> x0, other arithmetic: 483 us -> none  [device_step(): jax.ops.segment_sum(all_dx.reshape(-1, model_width), seg_idx.reshape(-1),...]
    all_gather x5 -> x4, waiting for transfers between devices: 410 us -> 0.01 us  [whole(): return lax.all_gather(part, AXIS, axis=0, tiled=True)]
    dot_general x18 -> x12, matrix products: 665 us -> 309 us  [the longest x4 108 us: dot_nt(): lax.dot_general(a, b, (((1,), (1,)), ((), ())), preferred_element_type=jn...]
    all_gather x5 -> x2, blocking collectives: 332 us -> 24.7 us  [the longest x1 13.9 us: device_step(): all_ids = lax.all_gather(tok_ids.reshape(-1), AXIS)]
    reduce_scatter x5 -> x4, waiting for transfers between devices: 282 us -> 0.03 us  [run(): lax.psum_scatter(g, AXIS, scatter_dimension=0, tiled=True)]
    another operation x1 -> x3, other arithmetic: 104 us -> 2.46 us
  transfers between devices with their start and end apart: 10 -> 9, of which waited for: 4 -> 0; matrix products, arithmetic and copies ran while one was open for 52% -> 28% of each run, Pallas kernels for 0% -> 56%
where the time goes in v1:
time: 1560 us
  Pallas kernels  1020 us (65%)
  matrix products  309 us (20%)
  other arithmetic  94 us (6%)
  local copies, waits for them, and re-layouts  87.4 us (6%)
  blocking collectives  24.7 us (2%)
    pallas_call x1, Pallas kernels, grad_exchange(): pl.pallas_call(reduce_kernel, out_shape=[jax.ShapeDtypeStruct((HOT, width...  488 us
    pallas_call x1, Pallas kernels, lookup_exchange(): pl.pallas_call(lookup_kernel, out_shape=jax.ShapeDtypeStruct(rows_in.shap...  227 us
    pallas_call x1, Pallas kernels, attention(): pl.pallas_call(attn_kernel, grid=(n_seq, n_heads), in_specs=[tile, tile,...  147 us
    dot_general x4, matrix products, dot_nt(): lax.dot_general(a, b, (((1,), (1,)), ((), ())), preferred_element_type=jn...  108 us
    dot_general x4, matrix products, dot_nn(): lax.dot_general(a, b, (((1,), (0,)), ((), ())), preferred_element_type=jn...  103 us
    pallas_call x1, Pallas kernels, build_table(): pl.pallas_call(table_kernel, grid_spec=pltpu.PrefetchScalarGridSpec(num_s...  91.1 us
    pallas_call x1, Pallas kernels, seg_sum(): pl.pallas_call(seg_sum_kernel, grid_spec=pltpu.PrefetchScalarGridSpec(num...  34.3 us
    gather x1, local copies, waits for them, and re-layouts, fast_lookup(): send = jnp.take(table_part, ask_row.reshape(-1), axis=0, mode='clip')  32.7 us
  transfers between devices with their start and end apart: 9, of which 0 were waited for; matrix products, arithmetic and copies ran while one was open for 28% of the time, Pallas kernels for 56%

profile of v1, /device:TPU:0, one launch (start us, length us, event | category | flops | bytes accessed | tf_op | source)
XLA Modules:
  0.0 1556.1 jit_solution(7287029076169476547)
XLA Ops:
  7.2 0.7 reshape.270
  7.9 13.9 all-gather.1
  23.4 1525.6 %conditional.1 = (bf16[2,1024,2048]{2,1,0:T(8,128)(2,1)}, bf16[18992,2048]{1,0:T(8,128)(2,1)}, f32[256]{0:T(256)}, f32[256,2048]{1,0:T(8,128)}, f32[256]{0:T(256...) conditional(s32[]{:T(128)} %convert_element_type.93, ...), branch_computations={%region_2.14_spmd, %region_14.33_spmd} | conditional | flops 258048327680 | bytes 2336673024 | solution.py:652
  30.4 0.7 broadcast_divide_fusion
  31.1 0.7 broadcast_compare_fusion
  31.9 2.3 reduce-window.4
  34.7 0.7 broadcast_compare_fusion.1
  35.4 1.3 add_select_fusion.2
  40.1 10.9 all_gather.33
  51.6 2.0 fusion.4
  53.6 8.2 slice_bitcast_fusion
  61.8 3.5 copy.45
  65.3 27.8 %pad.6._ = bf16[5632,16,128]{2,1,0:T(8,128)(2,1)} pad(bf16[4096,16,128]{2,1,0:T(8,128)(2,1)S(1)} %bitcast.133, bf16[]{:T(256)} %constant.87.clone), padding=0_1536x0_0x0_0 | pad | bytes 39845888 | tf_op jit(solution)/shard_map/cond/branch_1_fun/jit(_pad)/pad | solution.py:549
  93.1 1.3 pad_maximum_fusion
  94.4 1.3 add_select_fusion.4
  95.7 0.7 and_select_fusion
  96.5 32.7 %gather_fusion.1 = bf16[1536,2048]{1,0:T(8,128)(2,1)} fusion(bf16[18992,2048]{1,0:T(8,128)(2,1)} %get-tuple-element.65, s32[2048]{0:T(1024)S(1)} %pad_clamp_fusion), kind=kCustom, calls=%fused_computation.1 | custom fusion | bytes 12589056 | tf_op jit(solution)/shard_map/cond/branch_1_fun/jit(_take)/gather | solution.py:546
  129.2 7.8 copy.44
  137.0 226.9 %lookup_exchange.1.rows_ref = bf16[5632,16,128]{2,1,0:T(8,128)(2,1)} custom-call(bf16[8,192,16,128]{3,2,1,0:T(8,128)(2,1)} %bitcast.139, bf16[5632,16,128]{2,1,0:T(8,128)(2,1)} %pad.6._), custom_call_target="tpu_custom_call", output_to_operand_aliasing={{}: (1, {})} | custom-call | tf_op jit(solution)/shard_map/cond/branch_1_fun/lookup_exchange/pallas_call | solution.py:241
  363.9 14.7 pick_rows.1
  378.6 17.2 %multiply_reduce_fusion.2 = f32[2048]{0:T(1024)S(1)} fusion(bf16[2048,16,128]{2,1,0:T(8,128)(2,1)} %pick_rows.1), kind=kLoop, calls=%fused_computation.13 | loop fusion | flops 12580864 | bytes 8396800 | tf_op jit(solution)/shard_map/cond/branch_1_fun/reduce_sum | solution.py:128
  395.8 11.7 bitcast_convert_fusion
  408.1 14.1 multiply_convert_fusion
  422.3 24.1 %fusion.48.k_ref = f32[2048,2048]{1,0:T(8,128)} fusion(bf16[2048,2048]{1,0:T(8,128)(2,1)} %multiply_convert_fusion, bf16[2048,2048]{1,0:T(8,128)(2,1)} %all-gather.24.cloned.1.call-done), kind=kOutput, calls=%fused_computation.132 | convolution fusion | flops 17179869184 | bytes 33554432 | tf_op jit(solution)/shard_map/cond/branch_1_fun/dot_general | solution.py:27
  446.4 24.1 %fusion.47.q_ref = f32[2048,2048]{1,0:T(8,128)} fusion(bf16[2048,2048]{1,0:T(8,128)(2,1)} %multiply_convert_fusion, bf16[2048,2048]{1,0:T(8,128)(2,1)} %all-gather.22.cloned.1.call-done), kind=kOutput, calls=%fused_computation.131 | convolution fusion | flops 17179869184 | bytes 33554432 | tf_op jit(solution)/shard_map/cond/branch_1_fun/dot_general | solution.py:27
  470.5 24.2 %convolution_convert_fusion.do_ref = bf16[2048,2048]{1,0:T(8,128)(2,1)} fusion(bf16[2048,2048]{1,0:T(8,128)(2,1)} %bitcast.137, bf16[2048,2048]{1,0:T(8,128)(2,1)} %all-gather.28.cloned.1.call-done), kind=kOutput, calls=%fused_computation.15 | convolution fusion | flops 17184063488 | bytes 25165824 | tf_op jit(solution)/shard_map/cond/branch_1_fun/dot_general | solution.py:31
  494.7 23.6 %add_convert_fusion.v_ref = bf16[2048,2048]{1,0:T(8,128)(2,1)} fusion(bf16[2048,2048]{1,0:T(8,128)(2,1)} %multiply_convert_fusion, bf16[2048,2048]{1,0:T(8,128)(2,1)} %all-gather.26.cloned.1.call-done, f32[2048]{0:T(1024)S(1)} %bitcast.167), kind=kOutput, calls=%fused_computation.11 | convolution fusion | flops 17188257792 | bytes 25174016 | tf_op jit(solution)/shard_map/cond/branch_1_fun/dot_general | solution.py:27
  518.3 146.8 %attn_fwd_bwd.3 = (bf16[2048,2048]{1,0:T(8,128)(2,1)}, bf16[2048,2048]{1,0:T(8,128)(2,1)}, bf16[2048,2048]{1,0:T(8,128)(2,1)}, bf16[2048,2048]{1,0:T(8,128)(2,1)}, f32[2,8,2048]{2,1,0:T(8,128)}) custom-call(f32[2048,2048]{1,0:T(8,128)} %fusion.47.q_ref, f32[2048,2048]{1,0:T(8,128)} %fusion.48.k_ref, bf16[2048,2048]{1,0:T(8,128)(2,1)} %add_convert_fusion.v_ref, ...), custom_call_target="tpu_custom_call" | custom-call | flops 51539607552 | bytes 100663296 | tf_op jit(solution)/shard_map/cond/branch_1_fun/attn_fwd_bwd/pallas_call | solution.py:105
  665.1 24.3 %fusion.54 = f32[2048,2048]{1,0:T(8,128)} fusion(bf16[2048,2048]{1,0:T(8,128)(2,1)} %get-tuple-element.76, bf16[2048,2048]{1,0:T(8,128)(2,1)} %bitcast.138), kind=kOutput, calls=%fused_computation.138 | convolution fusion | flops 17179869184 | bytes 33554432 | tf_op jit(solution)/shard_map/cond/branch_1_fun/dot_general | solution.py:139
  689.6 24.6 %fusion.51 = f32[2048,2048]{1,0:T(8,128)} fusion(bf16[2048,2048]{1,0:T(8,128)(2,1)} %multiply_convert_fusion, bf16[2048,2048]{1,0:T(8,128)(2,1)} %get-tuple-element.79), kind=kOutput, calls=%fused_computation.135 | convolution fusion | flops 17179869184 | bytes 33554432 | tf_op jit(solution)/shard_map/cond/branch_1_fun/dot_general | solution.py:144
  714.2 24.3 %fusion.52 = f32[2048,2048]{1,0:T(8,128)} fusion(bf16[2048,2048]{1,0:T(8,128)(2,1)} %multiply_convert_fusion, bf16[2048,2048]{1,0:T(8,128)(2,1)} %get-tuple-element.80), kind=kOutput, calls=%fused_computation.136 | convolution fusion | flops 17179869184 | bytes 33554432 | tf_op jit(solution)/shard_map/cond/branch_1_fun/dot_general | solution.py:145
  738.6 24.6 %fusion.53 = f32[2048,2048]{1,0:T(8,128)} fusion(bf16[2048,2048]{1,0:T(8,128)(2,1)} %multiply_convert_fusion, bf16[2048,2048]{1,0:T(8,128)(2,1)} %get-tuple-element.81), kind=kOutput, calls=%fused_computation.137 | convolution fusion | flops 17179869184 | bytes 33554432 | tf_op jit(solution)/shard_map/cond/branch_1_fun/dot_general | solution.py:146
  763.2 24.3 %fusion.49 = f32[2048,2048]{1,0:T(8,128)} fusion(bf16[2048,2048]{1,0:T(8,128)(2,1)} %get-tuple-element.79, bf16[2048,2048]{1,0:T(8,128)(2,1)} %all-gather.22.cloned.1.call-done), kind=kOutput, calls=%fused_computation.133 | convolution fusion | flops 17179869184 | bytes 33554432 | tf_op jit(solution)/shard_map/cond/branch_1_fun/dot_general | solution.py:31
  787.5 24.7 %fusion.50 = f32[2048,2048]{1,0:T(8,128)} fusion(bf16[2048,2048]{1,0:T(8,128)(2,1)} %get-tuple-element.80, bf16[2048,2048]{1,0:T(8,128)(2,1)} %all-gather.24.cloned.1.call-done), kind=kOutput, calls=%fused_computation.134 | convolution fusion | flops 17179869184 | bytes 33554432 | tf_op jit(solution)/shard_map/cond/branch_1_fun/dot_general | solution.py:31
  812.3 35.2 %multiply_reduce_fusion = (f32[2048]{0:T(1024)S(1)}, f32[2048]{0:T(1024)S(1)}, f32[2048,2048]{1,0:T(8,128)}) fusion(f32[256,8,16,128]{3,2,1,0:T(8,128)} %bitcast_convert_fusion, f32[2048]{0:T(1024)S(1)} %copy-done.7, f32[2048]{0:T(1024)S(1)} %bitcast.152, bf16[2048,2048]{1,0:T(8,128)(2,1)} %get-tuple-element.81, ...), kind=kOutput, calls=%fused_computation.7 | convolution fusion | flops 17213419520 | bytes 83918848 | tf_op jit(solution)/shard_map/cond/branch_1_fun/dot_general | solution.py:31
  847.5 22.9 %multiply_add_fusion.mine_ref.rows_ref = f32[2048,2048]{1,0:T(8,128)} fusion(f32[2048,2048]{1,0:T(8,128)} %get-tuple-element.147, f32[256,8,16,128]{3,2,1,0:T(8,128)} %bitcast_convert_fusion, f32[2048]{0:T(1024)S(1)} %broadcast_multiply_fusion, f32[2048]{0:T(1024)S(1)} %bitcast.153, f32[2048]{0:T(1024)S(1)} %copy-done.7, ...), kind=kLoop, calls=%fused_computation.8 | loop fusion | flops 29360128 | bytes 58744832 | tf_op jit(solution)/shard_map/cond/branch_1_fun/add | solution.py:143
  870.4 0.9 constant_dynamic-slice_fusion
  871.3 5.8 sort.28
  877.1 0.7 convert_reduce_fusion.1.off_ref
  877.9 0.7 compare_select_fusion
  879.3 5.0 sort.27
  884.3 0.8 convert_reduce_fusion.off_ref
  885.8 16.2 %take_rows.1 = f32[1536,2048]{1,0:T(8,128)} custom-call(s32[1536]{0:T(1024)} %reshape.231.idx_ref, f32[2048,2048]{1,0:T(8,128)} %multiply_add_fusion.mine_ref.rows_ref), custom_call_target="tpu_custom_call" | custom-call | tf_op jit(solution)/shard_map/cond/branch_1_fun/take_rows/pallas_call | solution.py:298
  902.1 31.4 %fusion.1 = bf16[2048,2048]{1,0:T(8,128)(2,1)} fusion(f32[256,8,16,128]{3,2,1,0:T(8,128)} %bitcast_convert_fusion, bf16[2048,2048]{1,0:T(8,128)(2,1)} %get-tuple-element.76, bf16[2048,2048]{1,0:T(8,128)(2,1)} %all-gather.28.cloned.1.call-done), kind=kOutput, calls=%fused_computation.6 | convolution fusion | flops 17188257792 | bytes 41943040 | tf_op jit(solution)/shard_map/cond/branch_1_fun/dot_general | solution.py:27
  933.5 34.3 %hot_seg_sum.1.part_ref = f32[2048,2048]{1,0:T(8,128)} custom-call(s32[4096]{0:T(1024)} %copy-done.10, s32[17]{0:T(128)} %convert_reduce_fusion.1.off_ref, f32[2048,2048]{1,0:T(8,128)} %multiply_add_fusion.mine_ref.rows_ref, f32[2048,2048]{1,0:T(8,128)} %collective-permute-done.mate_ref), custom_call_target="tpu_custom_call" | custom-call | tf_op jit(solution)/shard_map/cond/branch_1_fun/hot_seg_sum/pallas_call | solution.py:340
  967.8 488.3 %grad_exchange.1 = (f32[4096,2048]{1,0:T(8,128)}, f32[8,192,2048]{2,1,0:T(8,128)}, f32[8,8,256]{2,1,0:T(8,128)}) custom-call(f32[2048,2048]{1,0:T(8,128)} %hot_seg_sum.1.part_ref, f32[8,192,2048]{2,1,0:T(8,128)} %bitcast.134, f32[8,8,256]{2,1,0:T(8,128)} %pad.7.vec_ref), custom_call_target="tpu_custom_call" | custom-call | tf_op jit(solution)/shard_map/cond/branch_1_fun/grad_exchange/pallas_call | solution.py:470
  1456.1 0.9 reduce_sum.115
  1457.0 91.1 %build_table.1 = bf16[18992,2048]{1,0:T(8,128)(2,1)} custom-call(s32[1536]{0:T(1024)} %copy-done.11, s32[150]{0:T(256)} %convert_reduce_fusion.off_ref, s32[1]{0:T(128)} %bitcast.19.n_hot_ref, f32[1536,2048]{1,0:T(8,128)} %bitcast.141, f32[4096,2048]{1,0:T(8,128)} %get-tuple-element.84.hot_ref), custom_call_target="tpu_custom_call" | custom-call | tf_op jit(solution)/shard_map/cond/branch_1_fun/build_table/pallas_call | solution.py:518
  (94 shorter events, 11.9 us)
Async XLA Ops:
  26.9 34.9 %copy-start.1 = (s32[8,2048]{1,0:T(8,128)}, s32[8,2048]{1,0:T(8,128)S(1)}, u32[]{:S(2)}) copy-start(s32[8,2048]{1,0:T(8,128)S(1)} %get-tuple-element.66) | copy-start | bytes 196612 | tf_op jit(solution)/shard_map/cond
  26.9 67.5 %sort.42.cloned.1.call-start = ((), (), s32[]{:S(2)}) async-start(), calls=%async_computation.27 | async-start | bytes 196640 | tf_op jit(solution)/shard_map/cond/branch_1_fun/sort | solution.py:543
  27.7 394.6 %all-gather.24.cloned.1.call-start = ((), (), s32[]{:S(2)}) async-start(), calls=%async_computation.20 | async-start | bytes 9437184 | tf_op jit(solution)/shard_map/cond/branch_1_fun/all_gather | solution.py:621
  28.4 418.0 %all-gather.22.cloned.1.call-start = ((), (), s32[]{:S(2)}) async-start(), calls=%async_computation.19 | async-start | bytes 9437184 | tf_op jit(solution)/shard_map/cond/branch_1_fun/all_gather | solution.py:621
  29.1 441.4 %all-gather.28.cloned.1.call-start = ((), (), s32[]{:S(2)}) async-start(), calls=%async_computation.22 | async-start | bytes 9437184 | tf_op jit(solution)/shard_map/cond/branch_1_fun/all_gather | solution.py:621
  29.7 465.0 %all-gather.26.cloned.1.call-start = ((), (), s32[]{:S(2)}) async-start(), calls=%async_computation.21 | async-start | bytes 9437184 | tf_op jit(solution)/shard_map/cond/branch_1_fun/all_gather | solution.py:621
  30.3 847.6 %sort.44.cloned.1.call-start = ((), (), s32[]{:S(2)}) async-start(), calls=%async_computation.28 | async-start | bytes 196640 | tf_op jit(solution)/shard_map/cond/branch_1_fun/sort | solution.py:557
  37.4 1511.3 %reduce-scatter.26.cloned.1.call-start = ((), (), s32[]{:S(2)}) async-start(), calls=%async_computation.26 | async-start | bytes 18874368 | tf_op jit(solution)/shard_map/cond/branch_1_fun/reduce_scatter | solution.py:633
  51.6 355.9 %copy-start.8 = (f32[1,2048]{1,0:T(1,128)}, f32[1,2048]{1,0:T(1,128)S(1)}, u32[]{:S(2)}) copy-start(f32[1,2048]{1,0:T(1,128)S(1)} %get-tuple-element.135) | copy-start | bytes 24580 | tf_op jit(solution)/shard_map/cond
  407.6 0.6 copy-start.6
  470.5 24.2 %copy-start.17 = (f32[1,2048]{1,0:T(1,128)S(1)}, f32[1,2048]{1,0:T(1,128)}, u32[]{:S(2)}) copy-start(f32[1,2048]{1,0:T(1,128)} %get-tuple-element.134) | copy-start | bytes 24580 | tf_op jit(solution)/shard_map/cond
  689.5 859.2 %reduce-scatter.20.cloned.1.call-start = ((), (), s32[]{:S(2)}) async-start(), calls=%async_computation.23 | async-start | bytes 18874368 | tf_op jit(solution)/shard_map/cond/branch_1_fun/reduce_scatter | solution.py:633
  714.1 834.6 %reduce-scatter.22.cloned.1.call-start = ((), (), s32[]{:S(2)}) async-start(), calls=%async_computation.24 | async-start | bytes 18874368 | tf_op jit(solution)/shard_map/cond/branch_1_fun/reduce_scatter | solution.py:633
  738.5 810.2 %reduce-scatter.24.cloned.1.call-start = ((), (), s32[]{:S(2)}) async-start(), calls=%async_computation.25 | async-start | bytes 18874368 | tf_op jit(solution)/shard_map/cond/branch_1_fun/reduce_scatter | solution.py:633
  787.5 24.7 %copy-start.7 = (f32[2048]{0:T(1024)S(1)}, f32[2048]{0:T(1024)}, u32[]{:S(2)}) copy-start(f32[2048]{0:T(1024)} %copy-done.6) | copy-start | bytes 24580 | tf_op jit(solution)/shard_map/cond
  787.5 24.7 %copy-start.9 = (f32[1,2048]{1,0:T(1,128)S(1)}, f32[1,2048]{1,0:T(1,128)}, u32[]{:S(2)}) copy-start(f32[1,2048]{1,0:T(1,128)} %copy-done.8) | copy-start | bytes 24580 | tf_op jit(solution)/shard_map/cond
  847.5 22.9 %copy-start.2 = (s32[2,1024]{1,0:T(2,128)S(1)}, s32[2,1024]{1,0:T(2,128)}, u32[]{:S(2)}) copy-start(s32[2,1024]{1,0:T(2,128)} %get-tuple-element.64) | copy-start | bytes 24580 | tf_op jit(solution)/shard_map/cond
  847.5 30.3 %copy-start.16 = (s32[8,192]{1,0:T(8,128)S(1)}, s32[8,192]{1,0:T(8,128)}, u32[]{:S(2)}) copy-start(s32[8,192]{1,0:T(8,128)} %get-tuple-element.112) | copy-start | bytes 18436 | tf_op jit(solution)/shard_map/cond
  847.5 37.6 %copy-start.4 = (f32[2,8,2048]{2,1,0:T(8,128)S(1)}, f32[2,8,2048]{2,1,0:T(8,128)}, u32[]{:S(2)}) copy-start(f32[2,8,2048]{2,1,0:T(8,128)} %get-tuple-element.82) | copy-start | bytes 393220 | tf_op jit(solution)/shard_map/cond
  870.4 63.1 %collective-permute-start = (f32[2048,2048]{1,0:T(8,128)}, f32[2048,2048]{1,0:T(8,128)}, u32[]{:S(2)}, u32[]{:S(2)}) collective-permute-start(f32[2048,2048]{1,0:T(8,128)} %multiply_add_fusion.mine_ref.rows_ref), channel_id=1, source_target_pairs={{0,1},{1,0},{2,3},{3,2},{4,5},{5,4},{6,7},{7,6}} | collective-permute-start | bytes 50331656 | tf_op jit(solution)/shard_map/cond/branch_1_fun/ppermute | solution.py:572
  877.1 25.0 %copy-start.10 = (s32[4096]{0:T(1024)}, s32[4096]{0:T(1024)S(1)}, u32[]{:S(2)}) copy-start(s32[4096]{0:T(1024)S(1)} %get-tuple-element.78.key_ref) | copy-start | bytes 49156 | tf_op jit(solution)/shard_map/cond
  884.3 17.8 %copy-start.11 = (s32[1536]{0:T(1024)}, s32[1536]{0:T(1024)S(1)}, u32[]{:S(2)}) copy-start(s32[1536]{0:T(1024)S(1)} %get-tuple-element.77.key_ref) | copy-start | bytes 18436 | tf_op jit(solution)/shard_map/cond
Sparse Core Ops, SparseCore 0:
  30.7 7.5 sort.46.cloned.1.call-done
  40.3 48.3 all-gather.23
  90.5 48.8 all-gather.21
  141.2 105.0 all-gather.27
  248.0 64.3 all-gather.25
  314.7 7.5 sort.48.cloned.1.call-done
  689.6 138.6 reduce-scatter.25
  832.4 106.9 reduce-scatter.19
  943.5 148.9 reduce-scatter.21
  1096.4 190.9 reduce-scatter.23
  (2 shorter events, 0.0 us)

commit v2 on v1

v2 whole, which is shorter than its diff:
```python
import functools

import jax
import jax.numpy as jnp
from jax import lax
from jax.experimental import pallas as pl
from jax.experimental.pallas import tpu as pltpu
from jax.sharding import PartitionSpec as P

HEAD_DIM = 128
ROPE_THETA = 1.0e6
NORM_EPS = 1e-6
MASK_VALUE = -1e30
AXIS = "fsdp"
N_DEV = 8
HOT = 4096
CAP = 176
MORE = 32
LANES = 128
BIG = 2**31 - 1
MESH = pl.DeviceIdType.MESH
BLOCK_Q = 256
GROUPS = 4
ROW_BLOCK = 128
VMEM_MAX = 60 * 1024 * 1024


def dot_nn(a, b):
    return lax.dot_general(a, b, (((1,), (0,)), ((), ())), preferred_element_type=jnp.float32)


def dot_nt(a, b):
    return lax.dot_general(a, b, (((1,), (1,)), ((), ())), preferred_element_type=jnp.float32)


def attn_kernel(q_ref, k_ref, v_ref, do_ref, cos_ref, sin_ref, bq_ref, bk_ref, bv_ref,
                o_ref, dlin_ref, gb_ref, qs, ks, vs, dkt, dvt):
    seq_len = q_ref.shape[0]
    start = pl.program_id(1) * HEAD_DIM
    third = dlin_ref.shape[1] // 3
    q_cols, k_cols, v_cols = (pl.ds(pl.multiple_of(start + j * third, HEAD_DIM), HEAD_DIM) for j in range(3))
    score_scale = HEAD_DIM ** -0.5
    cos_t = cos_ref[...]
    sin_t = sin_ref[...]
    half = HEAD_DIM // 2
    q_lin = q_ref[...] + bq_ref[...]
    qs[...] = (q_lin * cos_t + pltpu.roll(q_lin, half, 1) * sin_t).astype(jnp.bfloat16)
    k_lin = k_ref[...] + bk_ref[...]
    ks[...] = (k_lin * cos_t + pltpu.roll(k_lin, half, 1) * sin_t).astype(jnp.bfloat16)
    vs[...] = (v_ref[...] + bv_ref[...]).astype(jnp.bfloat16)
    row_i = lax.broadcasted_iota(jnp.int32, (BLOCK_Q, BLOCK_Q), 0)
    col_i = lax.broadcasted_iota(jnp.int32, (BLOCK_Q, BLOCK_Q), 1)
    causal = row_i >= col_i
    n_blocks = seq_len // BLOCK_Q
    gbq = jnp.zeros((1, HEAD_DIM), jnp.float32)
    for blk in reversed(range(n_blocks)):
        lo = blk * BLOCK_Q
        width = lo + BLOCK_Q
        q_b = qs[pl.ds(lo, BLOCK_Q), :]
        do_b = do_ref[pl.ds(lo, BLOCK_Q), :]
        k_all = ks[pl.ds(0, width), :]
        v_all = vs[pl.ds(0, width), :]
        scores = dot_nt(q_b, k_all) * score_scale
        tail = jnp.where(causal, scores[:, lo:], MASK_VALUE)
        scores = jnp.concatenate([scores[:, :lo], tail], axis=1) if lo else tail
        top = jnp.max(scores, axis=1, keepdims=True)
        prob = jnp.exp(scores - top)
        prob = prob * (1.0 / jnp.sum(prob, axis=1, keepdims=True))
        prob_b = prob.astype(jnp.bfloat16)
        o_ref[pl.ds(lo, BLOCK_Q), :] = dot_nn(prob_b, v_all).astype(jnp.bfloat16)
        d_prob = dot_nt(do_b, v_all)
        inner = jnp.sum(d_prob * prob, axis=1, keepdims=True)
        d_score = ((prob * (d_prob - inner)) * score_scale).astype(jnp.bfloat16)
        d_q = dot_nn(d_score, k_all)
        scaled = d_q * sin_ref[pl.ds(lo, BLOCK_Q), :]
        d_q = d_q * cos_ref[pl.ds(lo, BLOCK_Q), :] + pltpu.roll(scaled, half, 1)
        gbq = gbq + jnp.sum(d_q, axis=0, keepdims=True)
        dlin_ref[pl.ds(lo, BLOCK_Q), q_cols] = d_q.astype(jnp.bfloat16)
        dv_part = dot_nn(do_b.T, prob_b)
        dk_part = dot_nn(q_b.T, d_score)
        if blk == n_blocks - 1:
            dvt[...] = dv_part
            dkt[...] = dk_part
        else:
            dvt[:, pl.ds(0, width)] += dv_part
            dkt[:, pl.ds(0, width)] += dk_part
    d_v = dvt[...].T
    d_k = dkt[...].T
    d_k = d_k * cos_t + pltpu.roll(d_k * sin_t, half, 1)
    dlin_ref[:, v_cols] = d_v.astype(jnp.bfloat16)
    dlin_ref[:, k_cols] = d_k.astype(jnp.bfloat16)
    gb_ref[0, 0:1, q_cols] = gbq
    gb_ref[0, 0:1, k_cols] = jnp.sum(d_k, axis=0, keepdims=True)
    gb_ref[0, 0:1, v_cols] = jnp.sum(d_v, axis=0, keepdims=True)


def rope_tables(seq_len):
    half = HEAD_DIM // 2
    inv_freq = jnp.power(ROPE_THETA, -(jnp.arange(half, dtype=jnp.float32) * 2.0 / HEAD_DIM))
    angles = jnp.arange(seq_len, dtype=jnp.float32)[:, None] * inv_freq[None, :]
    cos_t = jnp.concatenate([jnp.cos(angles)] * 2, axis=-1)
    sin_t = jnp.concatenate([-jnp.sin(angles), jnp.sin(angles)], axis=-1)
    return cos_t, sin_t


def attention(lin, d_attn, bias, cos_t, sin_t):
    tokens, width = d_attn.shape
    seq_len = cos_t.shape[0]
    n_seq, n_heads = tokens // seq_len, width // HEAD_DIM
    tile = pl.BlockSpec((seq_len, HEAD_DIM), lambda s, h: (s, h))
    third = [pl.BlockSpec((seq_len, HEAD_DIM), lambda s, h, j=j: (s, j * n_heads + h)) for j in range(3)]
    third_b = [pl.BlockSpec((1, HEAD_DIM), lambda s, h, j=j: (0, j * n_heads + h)) for j in range(3)]
    table = pl.BlockSpec((seq_len, HEAD_DIM), lambda s, h: (0, 0))
    pairs = n_seq * n_heads * seq_len * seq_len
    head_buf = pltpu.VMEM((seq_len, HEAD_DIM), jnp.bfloat16)
    turned = pltpu.VMEM((HEAD_DIM, seq_len), jnp.float32)
    return pl.pallas_call(
        attn_kernel,
        grid=(n_seq, n_heads),
        in_specs=[*third, tile, table, table, *third_b],
        out_specs=[
            tile,
            pl.BlockSpec((seq_len, 3 * width), lambda s, h: (s, 0)),
            pl.BlockSpec((1, 8, 3 * width), lambda s, h: (s, 0, 0)),
        ],
        out_shape=[
            jax.ShapeDtypeStruct((tokens, width), jnp.bfloat16),
            jax.ShapeDtypeStruct((tokens, 3 * width), jnp.bfloat16),
            jax.ShapeDtypeStruct((n_seq, 8, 3 * width), jnp.float32),
        ],
        scratch_shapes=[head_buf, head_buf, head_buf, turned, turned],
        compiler_params=pltpu.CompilerParams(
            dimension_semantics=("arbitrary", "arbitrary"), vmem_limit_bytes=VMEM_MAX),
        cost_estimate=pl.CostEstimate(
            flops=6 * 2 * HEAD_DIM * pairs, bytes_accessed=22 * tokens * width, transcendentals=pairs),
        name="attn_fwd_bwd",
    )(lin, lin, lin, d_attn, cos_t, sin_t, bias, bias, bias)


def block_fwd_bwd(x_rows, hidden, inv_rms, grad_out, seq_len, gain_f, biases, w_groups, w_out, on_grad):
    f32 = jnp.float32
    tn = (((0,), (0,)), ((), ()))
    n_groups = len(w_groups)
    group = w_out.shape[0] // n_groups
    cos_t, sin_t = rope_tables(seq_len)
    x_full = x_rows.astype(f32)
    x_norm = x_full * inv_rms
    outs, d_lins, bias_grads, grad_ws = [], [], [], []
    hid = hidden
    for g in range(n_groups):
        lin = dot_nn(hid, w_groups[g])
        d_attn = dot_nt(grad_out, w_out[g * group:(g + 1) * group]).astype(jnp.bfloat16)
        o_g, d_lin, gb = attention(lin, d_attn, biases[g], cos_t, sin_t)
        grad_w = lax.dot_general(hidden, d_lin, tn, preferred_element_type=f32)
        hid, grad_w = lax.optimization_barrier((hidden, grad_w))
        grad_ws.append(on_grad(grad_w))
        outs.append(o_g)
        d_lins.append(d_lin)
        bias_grads.append(jnp.sum(gb[:, 0], axis=0))
    attn_b = jnp.concatenate(outs, axis=1)
    grad_wo = on_grad(lax.dot_general(attn_b, grad_out, tn, preferred_element_type=f32))
    block_out = (x_full + dot_nn(attn_b, w_out)).astype(jnp.bfloat16)
    d_hidden = dot_nt(d_lins[0], w_groups[0])
    for g in range(1, n_groups):
        d_hidden = d_hidden + dot_nt(d_lins[g], w_groups[g])
    grad_gain = jnp.sum(d_hidden * x_norm, axis=0)
    d_norm = d_hidden * gain_f
    d_x = grad_out.astype(f32) + inv_rms * (d_norm - x_norm * jnp.mean(d_norm * x_norm, axis=-1, keepdims=True))
    return block_out, d_x, grad_ws, grad_wo, grad_gain, jnp.stack(bias_grads)


def barrier_all(me):
    barrier = pltpu.get_barrier_semaphore()
    for step in range(1, N_DEV):
        pl.semaphore_signal(barrier, inc=1, device_id=(jnp.bitwise_xor(me, step),), device_id_type=MESH)
    pl.semaphore_wait(barrier, N_DEV - 1)


LOOK_CHUNK = 128
LOOK_N = HOT // 2 // LOOK_CHUNK


def lookup_kernel(cold_ref, _, vec_ref, rows_ref, got_ref, vgot_ref,
                  recv_sem, link_sem, mate_sem, c_send, c_recv, v_send, v_recv, l_sem):
    me = lax.axis_index(AXIS)
    chip, core = me // 2, me % 2
    barrier_all(me)
    own = pltpu.make_async_copy(cold_ref.at[me], got_ref.at[me], l_sem.at[0])
    own_v = pltpu.make_async_copy(vec_ref, vgot_ref.at[me], l_sem.at[1])
    own.start()
    own_v.start()

    def cold_copy(step):
        peer = jnp.bitwise_xor(me, step)
        return pltpu.make_async_remote_copy(
            src_ref=cold_ref.at[peer], dst_ref=got_ref.at[me],
            send_sem=c_send.at[step - 1], recv_sem=c_recv.at[step - 1],
            device_id=(peer,), device_id_type=MESH)

    def vec_copy(step):
        peer = jnp.bitwise_xor(me, step)
        return pltpu.make_async_remote_copy(
            src_ref=vec_ref, dst_ref=vgot_ref.at[me], send_sem=v_send.at[step - 1], recv_sem=v_recv.at[step - 1],
            device_id=(peer,), device_id_type=MESH)

    def piece(part, k):
        return rows_ref.at[pl.ds(part * (HOT // 2) + k * LOOK_CHUNK, LOOK_CHUNK)]

    def link_copy(part, k, target):
        return pltpu.make_async_remote_copy(
            src_ref=piece(part, k), dst_ref=piece(part, k), send_sem=link_sem.at[part, k],
            recv_sem=recv_sem.at[part, k], device_id=(target,), device_id_type=MESH)

    def mate_copy(part, k):
        return pltpu.make_async_remote_copy(
            src_ref=piece(part, k), dst_ref=piece(part, k), send_sem=mate_sem.at[part, k],
            recv_sem=recv_sem.at[part, k], device_id=(jnp.bitwise_xor(me, 1),), device_id_type=MESH)

    place = [
        jnp.where(chip == 0, 0, jnp.where(chip == 1, 1, jnp.where(chip == 3, 2, 3))),
        jnp.where(chip == 0, 0, jnp.where(chip == 2, 1, jnp.where(chip == 3, 2, 3))),
    ]
    target = [
        2 * jnp.where(chip == 0, 1, jnp.where(chip == 1, 3, 2)),
        2 * jnp.where(chip == 0, 2, jnp.where(chip == 2, 3, 1)),
    ]

    def stage(step, carry):
        for part in range(2):
            k = step - place[part]
            live = (k >= 0) & (k < LOOK_N)

            @pl.when(live & (me != 0))
            def _():
                mate_copy(part, k).wait_recv()

            @pl.when(live & (core == 0) & (place[part] < 3))
            def _():
                link_copy(part, k, target[part]).start()

            @pl.when(live & (core == 0))
            def _():
                mate_copy(part, k).start()
        return carry

    for step in range(1, N_DEV):
        vec_copy(step).start()
        cold_copy(step).start()
    lax.fori_loop(0, LOOK_N + 3, stage, 0)

    def drain(k, carry):
        for part in range(2):
            @pl.when((core == 0) & (place[part] < 3))
            def _():
                link_copy(part, k, target[part]).wait_send()

            @pl.when(core == 0)
            def _():
                mate_copy(part, k).wait_send()
        return carry

    lax.fori_loop(0, LOOK_N, drain, 0)
    for step in range(1, N_DEV):
        vec_copy(step).wait()
        cold_copy(step).wait()
    own.wait()
    own_v.wait()


def lookup_exchange(cold_send, hot_rows, vecs):
    any_spec = pl.BlockSpec(memory_space=pl.ANY)
    dma = pltpu.SemaphoreType.DMA
    return pl.pallas_call(
        lookup_kernel,
        out_shape=[
            jax.ShapeDtypeStruct(hot_rows.shape, hot_rows.dtype),
            jax.ShapeDtypeStruct(cold_send.shape, cold_send.dtype),
            jax.ShapeDtypeStruct((N_DEV,) + vecs.shape, vecs.dtype),
        ],
        in_specs=[any_spec] * 3,
        out_specs=[any_spec] * 3,
        scratch_shapes=[dma((2, LOOK_N))] * 3 + [dma((N_DEV - 1,))] * 4 + [dma((2,))],
        input_output_aliases={1: 0},
        compiler_params=pltpu.CompilerParams(collective_id=0, has_side_effects=True),
        name="lookup_exchange",
    )(cold_send, hot_rows, vecs)


def pick_kernel(idx_ref, hot_ref, cold_ref, gain_ref, x_ref, hid_ref, inv_ref, rows, picked, sem):
    step = pl.program_id(0)
    count, width = x_ref.shape
    base = step * count

    @pl.when(step == 0)
    def _():
        hot = pltpu.make_async_copy(hot_ref, rows.at[pl.ds(0, HOT)], sem.at[0])
        cold = pltpu.make_async_copy(cold_ref, rows.at[pl.ds(HOT, cold_ref.shape[0])], sem.at[1])
        hot.start()
        cold.start()
        hot.wait()
        cold.wait()

    def body(i8, carry):
        for j in range(8):
            i = i8 * 8 + j
            picked[i] = rows[idx_ref[base + i]]
        return carry

    lax.fori_loop(0, count // 8, body, 0)
    x = picked[...].reshape(count, width)
    x_ref[...] = x
    x_full = x.astype(jnp.float32)
    inv = lax.rsqrt(jnp.mean(x_full * x_full, axis=-1, keepdims=True) + NORM_EPS)
    inv_ref[...] = inv
    hid_ref[...] = (x_full * inv * gain_ref[...]).astype(jnp.bfloat16)


def pick_rows(idx, hot, cold, gain, block):
    count = idx.shape[0]
    tail = hot.shape[1:]
    width = tail[0] * tail[1]
    any_spec = pl.BlockSpec(memory_space=pl.ANY)
    wide = pl.BlockSpec((block, width), lambda i, s: (i, 0))
    act = jax.ShapeDtypeStruct((count, width), hot.dtype)
    return pl.pallas_call(
        pick_kernel,
        grid_spec=pltpu.PrefetchScalarGridSpec(
            num_scalar_prefetch=1,
            grid=(count // block,),
            in_specs=[any_spec, any_spec, pl.BlockSpec((1, width), lambda i, s: (0, 0))],
            out_specs=[wide, wide, pl.BlockSpec((block, 1), lambda i, s: (i, 0))],
            scratch_shapes=[
                pltpu.VMEM((hot.shape[0] + cold.shape[0],) + tail, hot.dtype),
                pltpu.VMEM((block,) + tail, hot.dtype),
                pltpu.SemaphoreType.DMA((2,)),
            ],
        ),
        out_shape=[act, act, jax.ShapeDtypeStruct((count, 1), jnp.float32)],
        compiler_params=pltpu.CompilerParams(dimension_semantics=("arbitrary",), vmem_limit_bytes=VMEM_MAX),
        name="pick_rows",
    )(idx, hot, cold, gain)


def take2d_kernel(idx_ref, idx2_ref, rows_ref, out_ref, out2_ref, buf):
    step = pl.program_id(0)

    def copy_rows(idx, dst, count):
        def body(i8, carry):
            for j in range(8):
                i = i8 * 8 + j
                dst[pl.ds(i, 1), :] = rows_ref[pl.ds(idx[step * count + i], 1), :]
            return carry

        lax.fori_loop(0, count // 8, body, 0)

    copy_rows(idx_ref, buf, buf.shape[0])
    out_ref[...] = buf[...].astype(out_ref.dtype)
    copy_rows(idx2_ref, out2_ref, out2_ref.shape[0])


def take2d(idx, idx2, rows, steps):
    count, count2 = idx.shape[0] // steps, idx2.shape[0] // steps
    width = rows.shape[1]
    return pl.pallas_call(
        take2d_kernel,
        grid_spec=pltpu.PrefetchScalarGridSpec(
            num_scalar_prefetch=2,
            grid=(steps,),
            in_specs=[pl.BlockSpec(rows.shape, lambda i, a, b: (0, 0), pipeline_mode=pl.Buffered(1))],
            out_specs=[
                pl.BlockSpec((count, width), lambda i, a, b: (i, 0)),
                pl.BlockSpec((count2, width), lambda i, a, b: (i, 0)),
            ],
            scratch_shapes=[pltpu.VMEM((count, width), jnp.float32)],
        ),
        out_shape=[
            jax.ShapeDtypeStruct((count * steps, width), jnp.bfloat16),
            jax.ShapeDtypeStruct((count2 * steps, width), jnp.float32),
        ],
        compiler_params=pltpu.CompilerParams(dimension_semantics=("arbitrary",), vmem_limit_bytes=VMEM_MAX),
        name="take_rows",
    )(idx, idx2, rows)


def seg_sum_kernel(key_ref, off_ref, mine_ref, mate_ref, out_ref, src, sem):
    blk = pl.program_id(0)
    count = mine_ref.shape[0]

    @pl.when(blk == 0)
    def _():
        first = pltpu.make_async_copy(mine_ref, src.at[pl.ds(0, count)], sem.at[0])
        second = pltpu.make_async_copy(mate_ref, src.at[pl.ds(count, count)], sem.at[1])
        first.start()
        second.start()
        first.wait()
        second.wait()

    out_ref[...] = jnp.zeros_like(out_ref)

    def body(e, carry):
        key = key_ref[e]
        row = lax.shift_right_logical(key, 12) - blk * ROW_BLOCK
        tok = jnp.bitwise_and(key, 4095)
        out_ref[pl.ds(row, 1), :] += src[pl.ds(tok, 1), :]
        return carry

    lax.fori_loop(off_ref[blk], off_ref[blk + 1], body, 0)


def seg_sum(keys, offs, dx_mine, dx_mate, n_rows):
    tokens, width = dx_mine.shape
    any_spec = pl.BlockSpec(memory_space=pl.ANY)
    return pl.pallas_call(
        seg_sum_kernel,
        grid_spec=pltpu.PrefetchScalarGridSpec(
            num_scalar_prefetch=2,
            grid=(n_rows // ROW_BLOCK,),
            in_specs=[any_spec, any_spec],
            out_specs=pl.BlockSpec((ROW_BLOCK, width), lambda i, a, b: (i, 0)),
            scratch_shapes=[pltpu.VMEM((2 * tokens, width), jnp.float32), pltpu.SemaphoreType.DMA((2,))],
        ),
        out_shape=jax.ShapeDtypeStruct((n_rows, width), jnp.float32),
        compiler_params=pltpu.CompilerParams(dimension_semantics=("arbitrary",), vmem_limit_bytes=VMEM_MAX),
        name="hot_seg_sum",
    )(keys, offs, dx_mine, dx_mate)


RED_CHUNK = 64
RED_N = HOT // 2 // RED_CHUNK


def reduce_kernel(part_ref, cold_ref, more_ref, vec_ref, hot_ref, crecv_ref, mrecv_ref, vrecv_ref,
                  local, incoming, load_sem, send_sem, recv_sem, out_sem,
                  c_send, c_recv, m_send, m_recv, v_send, v_recv, l_sem):
    me = lax.axis_index(AXIS)
    chip, core = me // 2, me % 2
    mid = jnp.where(core == 0, 1, 2)
    first = 3 - mid
    place = jnp.where(chip == first, 0, jnp.where(chip == 3, 1, jnp.where(chip == mid, 2, 3)))
    nxt = jnp.where(chip == first, 3, jnp.where(chip == 3, mid, 0))
    target = nxt * 2 + core

    def rows(k):
        return pl.ds(k * RED_CHUNK, RED_CHUNK)

    def load(k):
        return pltpu.make_async_copy(part_ref.at[rows(k)], local.at[rows(k)], load_sem.at[k])

    def send(k):
        return pltpu.make_async_remote_copy(
            src_ref=local.at[rows(k)], dst_ref=incoming.at[rows(k)], send_sem=send_sem.at[k],
            recv_sem=recv_sem.at[k], device_id=(target,), device_id_type=MESH)

    def put_own(k):
        return pltpu.make_async_copy(local.at[rows(k)], hot_ref.at[rows(k)], send_sem.at[k])

    def put_far(k):
        return pltpu.make_async_remote_copy(
            src_ref=local.at[rows(k)], dst_ref=hot_ref.at[pl.ds(HOT // 2 + k * RED_CHUNK, RED_CHUNK)],
            send_sem=send_sem.at[k], recv_sem=out_sem.at[k], device_id=(jnp.bitwise_xor(me, 1),), device_id_type=MESH)

    swaps = (
        (vec_ref, vrecv_ref, v_send, v_recv),
        (more_ref, mrecv_ref, m_send, m_recv),
        (cold_ref, crecv_ref, c_send, c_recv),
    )

    def swap(which, step):
        src, dst, s_sem, r_sem = swaps[which]
        peer = jnp.bitwise_xor(me, step)
        return pltpu.make_async_remote_copy(
            src_ref=src.at[peer], dst_ref=dst.at[me], send_sem=s_sem.at[step - 1], recv_sem=r_sem.at[step - 1],
            device_id=(peer,), device_id_type=MESH)

    def keep(which):
        src, dst, _, _ = swaps[which]
        return pltpu.make_async_copy(src.at[me], dst.at[me], l_sem.at[which])

    def start_load(k, carry):
        load(k).start()
        return carry

    lax.fori_loop(0, RED_N, start_load, 0)
    barrier_all(me)
    for which in range(3):
        keep(which).start()
    for which in range(3):
        for step in range(1, N_DEV):
            swap(which, step).start()

    def stage(k, carry):
        @pl.when(k < RED_N)
        def _():
            load(k).wait()

        @pl.when((k < RED_N) & (place > 0))
        def _():
            send(k).wait_recv()
            local[rows(k), :] += incoming[rows(k), :]

        @pl.when((k >= 1) & (place < 3))
        def _():
            send(k - 1).start()

        @pl.when((k >= 1) & (me == 0))
        def _():
            put_own(k - 1).start()

        @pl.when((k >= 1) & (me == 1))
        def _():
            put_far(k - 1).start()
        return carry

    lax.fori_loop(0, RED_N + 1, stage, 0)

    def drain(k, carry):
        @pl.when(place < 3)
        def _():
            send(k).wait_send()

        @pl.when(me == 0)
        def _():
            put_own(k).wait()
            put_far(k).wait_recv()

        @pl.when(me == 1)
        def _():
            put_far(k).wait_send()
        return carry

    lax.fori_loop(0, RED_N, drain, 0)
    for which in range(3):
        for step in range(1, N_DEV):
            swap(which, step).wait()
        keep(which).wait()


def grad_exchange(part, cold_send, more_send, vecs):
    any_spec = pl.BlockSpec(memory_space=pl.ANY)
    dma = pltpu.SemaphoreType.DMA
    width = part.shape[1]
    return pl.pallas_call(
        reduce_kernel,
        out_shape=[jax.ShapeDtypeStruct((HOT, width), jnp.float32)]
        + [jax.ShapeDtypeStruct(a.shape, a.dtype) for a in (cold_send, more_send, vecs)],
        in_specs=[any_spec] * 4,
        out_specs=[any_spec] * 4,
        scratch_shapes=[pltpu.VMEM(part.shape, jnp.float32)] * 2
        + [dma((RED_N,))] * 4 + [dma((N_DEV - 1,))] * 6 + [dma((3,))],
        compiler_params=pltpu.CompilerParams(
            collective_id=1, has_side_effects=True, vmem_limit_bytes=VMEM_MAX),
        name="grad_exchange",
    )(part, cold_send, more_send, vecs)


def table_kernel(key_ref, off_ref, n_hot_ref, src_ref, more_ref, hot_ref, out_ref, acc, rows, half_rows, sem):
    blk = pl.program_id(0)
    n_src = src_ref.shape[0]

    @pl.when(blk == 0)
    def _():
        low = pltpu.make_async_copy(src_ref, half_rows, sem.at[0])
        high = pltpu.make_async_copy(more_ref, rows.at[pl.ds(n_src, more_ref.shape[0])], sem.at[1])
        low.start()
        high.start()
        low.wait()
        for c in range(N_DEV):
            part = pl.ds(c * (n_src // N_DEV), n_src // N_DEV)
            rows[part, :] = half_rows[part, :].astype(jnp.float32)
        high.wait()

    is_hot = blk < n_hot_ref[0]

    @pl.when(is_hot)
    def _():
        acc[...] = hot_ref[...]

    @pl.when(jnp.logical_not(is_hot))
    def _():
        acc[...] = jnp.zeros_like(acc)

    def body(e, carry):
        key = key_ref[e]
        row = lax.shift_right_logical(key, 11) - blk * ROW_BLOCK
        idx = jnp.bitwise_and(key, 2047)
        acc[pl.ds(row, 1), :] += rows[pl.ds(idx, 1), :]
        return carry

    lax.fori_loop(off_ref[blk], off_ref[blk + 1], body, 0)
    out_ref[...] = acc[...].astype(out_ref.dtype)


def build_table(keys, offs, n_hot, src, more, hot, n_rows):
    width = src.shape[1]

    def hot_index(i, k, o, n):
        return (jnp.minimum(i, jnp.maximum(n[0] - 1, 0)), 0)

    return pl.pallas_call(
        table_kernel,
        grid_spec=pltpu.PrefetchScalarGridSpec(
            num_scalar_prefetch=3,
            grid=(pl.cdiv(n_rows, ROW_BLOCK),),
            in_specs=[
                pl.BlockSpec(memory_space=pl.ANY),
                pl.BlockSpec(memory_space=pl.ANY),
                pl.BlockSpec((ROW_BLOCK, width), hot_index),
            ],
            out_specs=pl.BlockSpec((ROW_BLOCK, width), lambda i, k, o, n: (i, 0)),
            scratch_shapes=[
                pltpu.VMEM((ROW_BLOCK, width), jnp.float32),
                pltpu.VMEM((src.shape[0] + more.shape[0], width), jnp.float32),
                pltpu.VMEM(src.shape, src.dtype),
                pltpu.SemaphoreType.DMA((2,)),
            ],
        ),
        out_shape=jax.ShapeDtypeStruct((n_rows, width), jnp.bfloat16),
        compiler_params=pltpu.CompilerParams(dimension_semantics=("arbitrary",), vmem_limit_bytes=VMEM_MAX),
        name="build_table",
    )(keys, offs, n_hot, src, more, hot)


def fast_lookup(all_ids, own_ids, table_part, gain_vecs, me):
    rows_dev, width = table_part.shape
    tokens = own_ids.shape[0]
    first_row = me * rows_dev
    t_idx = jnp.arange(tokens, dtype=jnp.int32)
    mine = (all_ids >= HOT) & (all_ids >= first_row) & (all_ids < first_row + rows_dev)
    key = jnp.where(mine, t_idx[None, :] * 32768 + (all_ids - first_row), BIG)
    key = lax.sort(key, dimension=1)[:, :CAP]
    asked = key != BIG
    ask_row = jnp.where(asked, jnp.bitwise_and(key, 32767), 0)
    send = jnp.take(table_part, ask_row.reshape(-1), axis=0, mode="clip")
    tiles = (width // LANES, LANES)
    send = send.reshape((N_DEV, CAP) + tiles)
    hot, cold, vecs = lookup_exchange(send, table_part[:HOT].reshape((HOT,) + tiles), gain_vecs)
    vecs = vecs.transpose(1, 0, 2).reshape(gain_vecs.shape[0], -1).astype(jnp.float32)
    owners = own_ids // rows_dev
    hit = (owners[None, :] == jnp.arange(N_DEV, dtype=jnp.int32)[:, None]) & (own_ids >= HOT)[None, :]
    place = jnp.cumsum(hit.astype(jnp.int32), axis=1) - 1 + jnp.arange(N_DEV, dtype=jnp.int32)[:, None] * CAP
    slot = jnp.sum(jnp.where(hit, place, 0), axis=0)
    idx = jnp.where(own_ids >= HOT, HOT + slot, own_ids)
    normed = pick_rows(idx, hot, cold.reshape((N_DEV * CAP,) + tiles), vecs[:1], 256)
    return normed, cold, vecs


def first_of(mask, values, count):
    return lax.sort(jnp.where(mask, values, BIG), dimension=1)[:, :count]


def grad_plan(all_ids, own_ids, me, rows_dev):
    tokens = own_ids.shape[0]
    flat = all_ids.reshape(-1).astype(jnp.uint32)
    pos = jnp.arange(flat.shape[0], dtype=jnp.uint32)
    ordered = lax.sort(flat * jnp.uint32(16384) + pos)
    ident = ordered // jnp.uint32(16384)
    same = ident[1:] == ident[:-1]
    no = jnp.zeros((1,), jnp.bool_)
    again = jnp.concatenate([no, same]) | jnp.concatenate([same, no])
    again = lax.sort((ordered % jnp.uint32(16384)) * jnp.uint32(2) + again.astype(jnp.uint32)) % jnp.uint32(2)
    again = (again == 1).reshape(all_ids.shape)
    t_idx = jnp.arange(tokens, dtype=jnp.int32)[None, :]
    devices = jnp.arange(N_DEV, dtype=jnp.int32)
    owners = jnp.where(all_ids >= HOT, all_ids // rows_dev, -1)
    counts = jnp.sum(((owners[None] == devices[:, None, None]) & again[None]).astype(jnp.int32), axis=-1)
    fits = jnp.max(counts) <= MORE
    hit = lax.dynamic_index_in_dim(owners, me, 0, keepdims=False)[None, :] == devices[:, None]
    own_again = lax.dynamic_index_in_dim(again, me, 0, keepdims=True)
    slot_tok = first_of(hit, t_idx, CAP)
    more_tok = first_of(hit & own_again, t_idx, MORE)
    mine = owners == me
    local = all_ids - me * rows_dev
    row = first_of(mine, t_idx * 65536 + local * 2 + again, CAP)
    more_row = first_of(mine & again, t_idx * 65536 + local * 2 + again, MORE)
    slots = jnp.arange(N_DEV * CAP, dtype=jnp.int32).reshape(N_DEV, CAP)
    more_slots = N_DEV * CAP + jnp.arange(N_DEV * MORE, dtype=jnp.int32).reshape(N_DEV, MORE)

    def owner_key(packed, slot, wanted):
        where = jnp.bitwise_and(lax.shift_right_logical(packed, 1), 32767)
        return jnp.where((packed != BIG) & (jnp.bitwise_and(packed, 1) == wanted), where * 2048 + slot, BIG).reshape(-1)

    owner_keys = lax.sort(jnp.concatenate([owner_key(row, slots, 0), owner_key(more_row, more_slots, 1)]))

    def clean(tok):
        return jnp.where(tok == BIG, 0, tok).reshape(-1)

    return fits, clean(slot_tok), clean(more_tok), owner_keys


def block_offsets(keys, n_blocks, shift):
    edges = jnp.arange(n_blocks + 1, dtype=jnp.int32) * (ROW_BLOCK << shift)
    return jnp.sum(keys[None, :] < edges[:, None], axis=1).astype(jnp.int32)


def fast_table_grad(rows_dev, all_ids, own_ids, d_x, vecs, slot_tok, more_tok, owner_keys):
    tokens, width = d_x.shape
    me = lax.axis_index(AXIS)
    mate_of = [(i, i ^ 1) for i in range(N_DEV)]
    dx_mate = lax.ppermute(d_x, AXIS, mate_of)
    mate_ids = lax.dynamic_index_in_dim(all_ids, jnp.bitwise_xor(me, 1), 0, keepdims=False)
    pair_ids = jnp.concatenate([own_ids, mate_ids])
    base = (me % 2) * (HOT // 2)
    inside = (pair_ids >= base) & (pair_ids < base + HOT // 2)
    keys = jnp.where(inside, (pair_ids - base) * 4096 + jnp.arange(2 * tokens, dtype=jnp.int32), BIG)
    keys = lax.sort(keys)
    part = seg_sum(keys, block_offsets(keys, HOT // 2 // ROW_BLOCK, 12), d_x, dx_mate, HOT // 2)
    cold, more = take2d(slot_tok, more_tok, d_x, N_DEV)
    cold = cold.reshape(N_DEV, CAP, width)
    more = more.reshape(N_DEV, MORE, width)
    hot, recv, more_recv, vec_recv = grad_exchange(part, cold, more, vecs)
    n_hot = jnp.where(me == 0, HOT // ROW_BLOCK, 0).astype(jnp.int32)[None]
    offs = block_offsets(owner_keys, pl.cdiv(rows_dev, ROW_BLOCK), 11)
    recv = recv.reshape(N_DEV * CAP, width)
    more_recv = more_recv.reshape(N_DEV * MORE, width)
    grad_part = build_table(owner_keys, offs, n_hot, recv, more_recv, hot, rows_dev)
    return grad_part, jnp.sum(vec_recv, axis=0)


def slow_lookup(all_ids, table_part, me):
    rows_dev = table_part.shape[0]
    local_idx = all_ids - me * rows_dev
    is_owned = (local_idx >= 0) & (local_idx < rows_dev)
    looked = jnp.take(table_part, jnp.where(is_owned, local_idx, 0), axis=0)
    looked = jnp.where(is_owned[..., None], looked, jnp.zeros((), jnp.bfloat16))
    return lax.psum_scatter(looked, AXIS, scatter_dimension=0)


def slow_table_grad(rows_dev, all_ids, own_ids, d_x, vecs, *_):
    me = lax.axis_index(AXIS)
    local_idx = all_ids - me * rows_dev
    is_owned = (local_idx >= 0) & (local_idx < rows_dev)
    all_dx = lax.all_gather(d_x, AXIS)
    seg_idx = jnp.where(is_owned, local_idx, rows_dev)
    grad_part = jax.ops.segment_sum(all_dx.reshape(-1, d_x.shape[-1]), seg_idx.reshape(-1), num_segments=rows_dev)
    return grad_part.astype(jnp.bfloat16), lax.psum_scatter(vecs, AXIS, scatter_dimension=0)


def solution(mesh):
    row_spec = P(AXIS, None)
    vec_spec = P(AXIS)
    act_spec = P(AXIS, None, None)
    weight_specs = (vec_spec, row_spec, vec_spec, row_spec, vec_spec, row_spec, vec_spec, row_spec)
    in_specs = (row_spec, act_spec, row_spec) + weight_specs
    out_specs = (act_spec, row_spec) + weight_specs

    def run(fast, tok_ids, all_ids, grad_out, table_part, gain_part, wq_part, bq_part, wk_part, bk_part, wv_part, bv_part, wo_part):
        me = lax.axis_index(AXIS)
        rows_dev, width = table_part.shape
        n_seq, seq_len = tok_ids.shape
        own_ids = tok_ids.reshape(-1)

        def whole(part):
            return lax.all_gather(part, AXIS, axis=0, tiled=True)

        def scatter(grad):
            return lax.psum_scatter(grad, AXIS, scatter_dimension=0, tiled=True)

        part_w = gain_part.shape[0]
        group = wq_part.shape[1] // GROUPS
        cols = [slice(g * group, (g + 1) * group) for g in range(GROUPS)]
        vec_parts = jnp.pad(jnp.stack([gain_part, bq_part, bk_part, bv_part]), ((0, 12), (0, 0)))
        w_parts = [jnp.concatenate([wq_part[:, c], wk_part[:, c], wv_part[:, c]], axis=1) for c in cols]
        if fast:
            (x_rows, hidden, inv_rms), marker, vec_full = fast_lookup(all_ids, own_ids, table_part, vec_parts, me)
            late = lax.optimization_barrier((marker, *w_parts[1:]))
            w_parts = [w_parts[0], *late[1:]]
        else:
            x_rows = slow_lookup(all_ids, table_part, me)
            vec_full = lax.all_gather(vec_parts, AXIS, axis=1, tiled=True).astype(jnp.float32)
            x_full = x_rows.astype(jnp.float32)
            inv_rms = lax.rsqrt(jnp.mean(x_full * x_full, axis=-1, keepdims=True) + NORM_EPS)
            hidden = (x_full * inv_rms * vec_full[0]).astype(jnp.bfloat16)
        biases = [jnp.concatenate([vec_full[1, c], vec_full[2, c], vec_full[3, c]])[None] for c in cols]
        wo_full = whole(wo_part)
        w_groups = [whole(part) for part in w_parts]
        grad_flat = grad_out.reshape(-1, width)
        block_out, d_x, grad_ws, grad_wo, grad_gain, grad_bias = block_fwd_bwd(
            x_rows, hidden, inv_rms, grad_flat, seq_len, vec_full[0], biases, w_groups, wo_full, scatter)
        gq, gk, gv = (
            jnp.concatenate([grad_w[:, j * group:(j + 1) * group] for grad_w in grad_ws], axis=1) for j in range(3))
        grad_bias = grad_bias.reshape(GROUPS, 3, group)
        vecs = jnp.stack([grad_gain] + [grad_bias[:, j].reshape(-1) for j in range(3)])
        vecs = jnp.pad(vecs.reshape(4, N_DEV, part_w).transpose(1, 0, 2), ((0, 0), (0, 4), (0, 0)))
        rest = (all_ids, own_ids, d_x, vecs)
        if fast:
            few, slot_tok, more_tok, owner_keys = grad_plan(all_ids, own_ids, me, rows_dev)
            rest = rest + (slot_tok, more_tok, owner_keys)
            grad_part, vec_sum = lax.cond(
                few, functools.partial(fast_table_grad, rows_dev), functools.partial(slow_table_grad, rows_dev), *rest)
        else:
            grad_part, vec_sum = slow_table_grad(rows_dev, *rest)
        return (block_out.reshape(grad_out.shape), grad_part, vec_sum[0], gq, vec_sum[1], gk, vec_sum[2], gv, vec_sum[3], grad_wo)

    def device_step(tok_ids, grad_out, table_part, *weights):
        rows_dev = table_part.shape[0]
        all_ids = lax.all_gather(tok_ids.reshape(-1), AXIS)
        owners = jnp.where(all_ids >= HOT, all_ids // rows_dev, -1)
        counts = jnp.sum((owners[None] == jnp.arange(N_DEV, dtype=jnp.int32)[:, None, None]).astype(jnp.int32), axis=-1)
        fits = jnp.max(counts) <= CAP
        args = (tok_ids, all_ids, grad_out, table_part) + weights
        return lax.cond(fits, functools.partial(run, True), functools.partial(run, False), *args)

    return jax.shard_map(device_step, mesh=mesh, in_specs=in_specs, out_specs=out_specs, check_vma=False)
```

time: 1560 us -> 1770 us (1.13)
  waiting for transfers between devices: 2.54 us -> 368 us
  Pallas kernels: 1020 us -> 847 us
  matrix products: 309 us -> 327 us
    reduce_scatter x4 -> x5, waiting for transfers between devices: 0.03 us -> 364 us  [scatter(): return lax.psum_scatter(grad, AXIS, scatter_dimension=0, tiled=True)]
    pallas_call x1, Pallas kernels: 488 us -> 333 us  [grad_exchange(): pl.pallas_call(reduce_kernel, out_shape=[jax.ShapeDtypeStruct((HOT, width...]
    pad x2 -> x1, local copies, waits for them, and re-layouts: 28.5 us -> 0.01 us  [run(): jnp.pad(vecs.reshape(4, N_DEV, part_w).transpose(1, 0, 2), ((0, 0), (0, 4...]
    pallas_call x2 -> x5, Pallas kernels: 374 us -> 352 us  [the longest x1 188 us: lookup_exchange(): pl.pallas_call(lookup_kernel, out_shape=[jax.ShapeDtypeStruct(hot_rows.sh...]
    dot_general x4 -> x8, matrix products: 108 us -> 128 us  [dot_nt(): lax.dot_general(a, b, (((1,), (1,)), ((), ())), preferred_element_type=jn...]
    cond x28 -> x73, local copies, waits for them, and re-layouts: 20.2 us -> 36.4 us
    dot_general x4 -> x5, matrix products: 103 us -> 102 us  [dot_nn(): lax.dot_general(a, b, (((1,), (0,)), ((), ())), preferred_element_type=jn...]
    dot_general x4 -> x5, matrix products: 97.8 us -> 97.5 us  [the longest x4 76.5 us: block_fwd_bwd(): grad_w = lax.dot_general(hidden, d_lin, tn, preferred_element_type=f32)]
  transfers between devices with their start and end apart: 9 -> 11, of which waited for: 0 -> 5; matrix products, arithmetic and copies ran while one was open for 28% -> 19% of each run, Pallas kernels for 56% -> 20%
where the time goes in v2:
time: 1770 us; the launch traced here: 1760 us
  Pallas kernels  847 us (48%)
  waiting for transfers between devices  368 us (21%)
  matrix products  327 us (18%)
  local copies, waits for them, and re-layouts  89.9 us (5%)
  other arithmetic  78.7 us (4%)
    reduce_scatter x5, waiting for transfers between devices, scatter(): return lax.psum_scatter(grad, AXIS, scatter_dimension=0, tiled=True)  364 us
    pallas_call x1, Pallas kernels, grad_exchange(): pl.pallas_call(reduce_kernel, out_shape=[jax.ShapeDtypeStruct((HOT, width...  333 us
    pallas_call x1, Pallas kernels, lookup_exchange(): pl.pallas_call(lookup_kernel, out_shape=[jax.ShapeDtypeStruct(hot_rows.sh...  188 us
    pallas_call x4, Pallas kernels, attention(): pl.pallas_call(attn_kernel, grid=(n_seq, n_heads), in_specs=[*third, tile...  164 us
    dot_general x8, matrix products, dot_nt(): lax.dot_general(a, b, (((1,), (1,)), ((), ())), preferred_element_type=jn...  128 us
    dot_general x5, matrix products, dot_nn(): lax.dot_general(a, b, (((1,), (0,)), ((), ())), preferred_element_type=jn...  102 us
    pallas_call x1, Pallas kernels, build_table(): pl.pallas_call(table_kernel, grid_spec=pltpu.PrefetchScalarGridSpec(num_s...  90.5 us
    dot_general x4, matrix products, block_fwd_bwd(): grad_w = lax.dot_general(hidden, d_lin, tn, preferred_element_type=f32)  76.5 us
  transfers between devices with their start and end apart: 11, of which 5 were waited for; matrix products, arithmetic and copies ran while one was open for 19% of the time, Pallas kernels for 20%

profile of v2, /device:TPU:0, one launch (start us, length us, event | category | flops | bytes accessed | tf_op | source)
XLA Modules:
  0.0 1756.7 jit_solution(5730069800911737053)
XLA Ops:
  7.9 13.9 all-gather.2
  23.4 1726.5 %conditional.2 = (bf16[2,1024,2048]{2,1,0:T(8,128)(2,1)}, bf16[18992,2048]{1,0:T(8,128)(2,1)}, f32[256]{0:T(256)}, f32[256,2048]{1,0:T(8,128)}, f32[256]{0:T(256...) conditional(s32[]{:T(128)} %convert_element_type.107, ...), branch_computations={%region_2.18_spmd, %region_18.51_spmd} | conditional | flops 257974468608 | bytes 2609134848 | solution.py:801
  32.5 7.7 sort.62
  40.4 7.7 sort.68
  55.8 8.0 slice_bitcast_fusion.4
  63.9 8.4 copy.52
  76.6 33.3 %gather_fusion.1 = bf16[1408,2048]{1,0:T(8,128)(2,1)} fusion(bf16[18992,2048]{1,0:T(8,128)(2,1)} %get-tuple-element.147, s32[2048]{0:T(1024)S(1)} %pad_clamp_fusion), kind=kCustom, calls=%fused_computation.1 | custom fusion | bytes 11539968 | tf_op jit(solution)/shard_map/cond/branch_1_fun/jit(_take)/gather | solution.py:633
  109.9 7.3 copy.51
  117.2 188.4 %lookup_exchange.1 = (bf16[4096,16,128]{2,1,0:T(8,128)(2,1)}, bf16[8,176,16,128]{3,2,1,0:T(8,128)(2,1)}, bf16[8,16,256]{2,1,0:T(8,128)(2,1)}) custom-call(bf16[8,176,16,128]{3,2,1,0:T(8,128)(2,1)} %bitcast.207, bf16[4096,16,128]{2,1,0:T(8,128)(2,1)} %bitcast.190, bf16[16,256]{1,0:T(8,128)(2,1)} %fusion.68.vec_ref), custom_call_target="tpu_custom_call", output_to_operand_aliasing={{0}: (1, {})} | custom-call | tf_op jit(solution)/shard_map/cond/branch_1_fun/lookup_exchange/pallas_call | solution.py:273
  323.1 5.0 sort.89
  328.1 19.7 %pick_rows.1 = (bf16[2048,2048]{1,0:T(8,128)(2,1)}, bf16[2048,2048]{1,0:T(8,128)(2,1)}, f32[2048,1]{1,0:T(8,128)}) custom-call(s32[2048]{0:T(1024)} %compare_select_fusion.3.idx_ref, bf16[4096,16,128]{2,1,0:T(8,128)(2,1)} %get-tuple-element.153.hot_ref, bf16[1408,16,128]{2,1,0:T(8,128)(2,1)} %bitcast.210, f32[1,2048]{1,0:T(1,128)} %bitcast.226), custom_call_target="tpu_custom_call" | custom-call | tf_op jit(solution)/shard_map/cond/branch_1_fun/pick_rows/pallas_call | solution.py:325
  350.0 19.2 %fusion.107.q_ref.k_ref.v_ref = f32[2048,1536]{1,0:T(8,128)} fusion(bf16[2048,2048]{1,0:T(8,128)(2,1)} %get-tuple-element.173, bf16[2048,1536]{1,0:T(8,128)(2,1)} %all-gather.30.cloned.1.call-done), kind=kOutput, calls=%fused_computation.248 | convolution fusion | flops 12884901888 | bytes 27262976 | tf_op jit(solution)/shard_map/cond/branch_1_fun/dot_general | solution.py:29
  369.2 9.9 convolution_convert_fusion.7.do_ref
  379.1 41.0 %attn_fwd_bwd.12 = (bf16[2048,512]{1,0:T(8,128)(2,1)}, bf16[2048,1536]{1,0:T(8,128)(2,1)}, f32[2,8,1536]{2,1,0:T(8,128)}) custom-call(f32[2048,1536]{1,0:T(8,128)} %fusion.107.q_ref.k_ref.v_ref, f32[2048,1536]{1,0:T(8,128)} %fusion.107.q_ref.k_ref.v_ref, f32[2048,1536]{1,0:T(8,128)} %fusion.107.q_ref.k_ref.v_ref, ...), custom_call_target="tpu_custom_call" | custom-call | flops 12884901888 | bytes 23068672 | tf_op jit(solution)/shard_map/cond/branch_1_fun/attn_fwd_bwd/pallas_call | solution.py:117
  421.6 19.0 %fusion.108 = f32[2048,1536]{1,0:T(8,128)} fusion(bf16[2048,2048]{1,0:T(8,128)(2,1)} %get-tuple-element.173, bf16[2048,1536]{1,0:T(8,128)(2,1)} %get-tuple-element.164), kind=kOutput, calls=%fused_computation.249 | convolution fusion | flops 12884901888 | bytes 27262976 | tf_op jit(solution)/shard_map/cond/branch_1_fun/dot_general | solution.py:154
  440.6 9.9 convolution_convert_fusion.6.do_ref
  450.5 19.4 %fusion.109.q_ref.k_ref.v_ref = f32[2048,1536]{1,0:T(8,128)} fusion(bf16[2048,2048]{1,0:T(8,128)(2,1)} %get-tuple-element.173, bf16[2048,1536]{1,0:T(8,128)(2,1)} %all-gather.34.cloned.1.call-done), kind=kOutput, calls=%fused_computation.250 | convolution fusion | flops 12884901888 | bytes 27262976 | tf_op jit(solution)/shard_map/cond/branch_1_fun/dot_general | solution.py:29
  469.9 40.9 %attn_fwd_bwd.13 = (bf16[2048,512]{1,0:T(8,128)(2,1)}, bf16[2048,1536]{1,0:T(8,128)(2,1)}, f32[2,8,1536]{2,1,0:T(8,128)}) custom-call(f32[2048,1536]{1,0:T(8,128)} %fusion.109.q_ref.k_ref.v_ref, f32[2048,1536]{1,0:T(8,128)} %fusion.109.q_ref.k_ref.v_ref, f32[2048,1536]{1,0:T(8,128)} %fusion.109.q_ref.k_ref.v_ref, ...), custom_call_target="tpu_custom_call" | custom-call | flops 12884901888 | bytes 23068672 | tf_op jit(solution)/shard_map/cond/branch_1_fun/attn_fwd_bwd/pallas_call | solution.py:117
  512.3 19.4 %fusion.110 = f32[2048,1536]{1,0:T(8,128)} fusion(bf16[2048,2048]{1,0:T(8,128)(2,1)} %get-tuple-element.173, bf16[2048,1536]{1,0:T(8,128)(2,1)} %get-tuple-element.168), kind=kOutput, calls=%fused_computation.251 | convolution fusion | flops 12884901888 | bytes 27262976 | tf_op jit(solution)/shard_map/cond/branch_1_fun/dot_general | solution.py:154
  531.7 9.9 convolution_convert_fusion.5.do_ref
  541.6 19.2 %fusion.111.q_ref.k_ref.v_ref = f32[2048,1536]{1,0:T(8,128)} fusion(bf16[2048,2048]{1,0:T(8,128)(2,1)} %get-tuple-element.173, bf16[2048,1536]{1,0:T(8,128)(2,1)} %all-gather.36.cloned.1.call-done), kind=kOutput, calls=%fused_computation.252 | convolution fusion | flops 12884901888 | bytes 27262976 | tf_op jit(solution)/shard_map/cond/branch_1_fun/dot_general | solution.py:29
  560.8 40.9 %attn_fwd_bwd.14 = (bf16[2048,512]{1,0:T(8,128)(2,1)}, bf16[2048,1536]{1,0:T(8,128)(2,1)}, f32[2,8,1536]{2,1,0:T(8,128)}) custom-call(f32[2048,1536]{1,0:T(8,128)} %fusion.111.q_ref.k_ref.v_ref, f32[2048,1536]{1,0:T(8,128)} %fusion.111.q_ref.k_ref.v_ref, f32[2048,1536]{1,0:T(8,128)} %fusion.111.q_ref.k_ref.v_ref, ...), custom_call_target="tpu_custom_call" | custom-call | flops 12884901888 | bytes 23068672 | tf_op jit(solution)/shard_map/cond/branch_1_fun/attn_fwd_bwd/pallas_call | solution.py:117
  602.6 19.2 %fusion.112 = f32[2048,1536]{1,0:T(8,128)} fusion(bf16[2048,2048]{1,0:T(8,128)(2,1)} %get-tuple-element.173, bf16[2048,1536]{1,0:T(8,128)(2,1)} %get-tuple-element.172), kind=kOutput, calls=%fused_computation.253 | convolution fusion | flops 12884901888 | bytes 27262976 | tf_op jit(solution)/shard_map/cond/branch_1_fun/dot_general | solution.py:154
  621.8 9.9 convolution_convert_fusion.4.do_ref
  631.6 19.2 %fusion.113.q_ref.k_ref.v_ref = f32[2048,1536]{1,0:T(8,128)} fusion(bf16[2048,2048]{1,0:T(8,128)(2,1)} %get-tuple-element.173, bf16[2048,1536]{1,0:T(8,128)(2,1)} %all-gather.38.cloned.1.call-done), kind=kOutput, calls=%fused_computation.254 | convolution fusion | flops 12884901888 | bytes 27262976 | tf_op jit(solution)/shard_map/cond/branch_1_fun/dot_general | solution.py:29
  650.9 41.1 %attn_fwd_bwd.15 = (bf16[2048,512]{1,0:T(8,128)(2,1)}, bf16[2048,1536]{1,0:T(8,128)(2,1)}, f32[2,8,1536]{2,1,0:T(8,128)}) custom-call(f32[2048,1536]{1,0:T(8,128)} %fusion.113.q_ref.k_ref.v_ref, f32[2048,1536]{1,0:T(8,128)} %fusion.113.q_ref.k_ref.v_ref, f32[2048,1536]{1,0:T(8,128)} %fusion.113.q_ref.k_ref.v_ref, ...), custom_call_target="tpu_custom_call" | custom-call | flops 12884901888 | bytes 23068672 | tf_op jit(solution)/shard_map/cond/branch_1_fun/attn_fwd_bwd/pallas_call | solution.py:117
  693.1 19.6 %fusion.114 = f32[2048,2048]{1,0:T(8,128)} fusion(bf16[2048,1536]{1,0:T(8,128)(2,1)} %get-tuple-element.164, bf16[2048,1536]{1,0:T(8,128)(2,1)} %all-gather.30.cloned.1.call-done), kind=kOutput, calls=%fused_computation.255 | convolution fusion | flops 12884901888 | bytes 29360128 | tf_op jit(solution)/shard_map/cond/branch_1_fun/dot_general | solution.py:33
  712.7 19.7 %fusion.115 = f32[2048,2048]{1,0:T(8,128)} fusion(bf16[2048,1536]{1,0:T(8,128)(2,1)} %get-tuple-element.168, bf16[2048,1536]{1,0:T(8,128)(2,1)} %all-gather.34.cloned.1.call-done), kind=kOutput, calls=%fused_computation.256 | convolution fusion | flops 12884901888 | bytes 29360128 | tf_op jit(solution)/shard_map/cond/branch_1_fun/dot_general | solution.py:33
  732.4 16.4 fusion.116
  748.8 32.7 %fusion.46 = (f32[2048]{0:T(1024)S(1)}, f32[2048]{0:T(1024)S(1)}, f32[2048,2048]{1,0:T(8,128)}) fusion(bf16[2048,2048]{1,0:T(8,128)(2,1)} %get-tuple-element.156, f32[2048]{0:T(1024)S(1)} %copy-done.23, f32[2048]{0:T(1024)S(1)} %bitcast.227, bf16[2048,1536]{1,0:T(8,128)(2,1)} %get-tuple-element.179, bf16[2048,1536]{1,0:T(8,128)(2,1)} %all-gather.38.cloned.1.call-done, ...), kind=kOutput, calls=%fused_computation.106 | convolution fusion | flops 12926840832 | bytes 88113152 | tf_op jit(solution)/shard_map/cond/branch_1_fun/dot_general | solution.py:33
  781.6 17.3 fusion.45
  799.1 496.8 %conditional = (bf16[18992,2048]{1,0:T(8,128)(2,1)}, f32[8,256]{1,0:T(8,128)}, f32[1,256]{1,0:T(1,128)}, f32[1,256]{1,0:T(1,128)}, f32[1,256]{1,0:T(1,128)}, /*i...) conditional(s32[]{:T(128)} %convert_element_type.101, ...), branch_computations={%region_38.40_spmd, %region_41.45_spmd} | conditional | flops 72777728 | bytes 843158144 | solution.py:788
  807.6 5.8 sort.60
  813.4 18.0 %take_rows.1 = (bf16[1408,2048]{1,0:T(8,128)(2,1)}, f32[256,2048]{1,0:T(8,128)}) custom-call(s32[1408]{0:T(1024)} %reshape.281.idx_ref, s32[256]{0:T(256)} %reshape.282.idx2_ref, f32[2048,2048]{1,0:T(8,128)} %get-tuple-element.133.mine_ref.rows_ref), custom_call_target="tpu_custom_call" | custom-call | tf_op jit(solution)/shard_map/cond/branch_1_fun/cond/branch_1_fun/take_rows/pallas_call | solution.py:364
  833.0 33.3 %hot_seg_sum.1.part_ref = f32[2048,2048]{1,0:T(8,128)} custom-call(s32[4096]{0:T(1024)} %copy-done.22, s32[17]{0:T(128)} %convert_reduce_fusion.1.off_ref, f32[2048,2048]{1,0:T(8,128)} %get-tuple-element.133.mine_ref.rows_ref, f32[2048,2048]{1,0:T(8,128)} %collective-permute-done.mate_ref), custom_call_target="tpu_custom_call" | custom-call | tf_op jit(solution)/shard_map/cond/branch_1_fun/cond/branch_1_fun/hot_seg_sum/pallas_call | solution.py:413
  866.3 333.5 %grad_exchange.1 = (f32[4096,2048]{1,0:T(8,128)}, bf16[8,176,2048]{2,1,0:T(8,128)(2,1)}, f32[8,32,2048]{2,1,0:T(8,128)}, f32[8,8,256]{2,1,0:T(8,128)}) custom-call(f32[2048,2048]{1,0:T(8,128)} %hot_seg_sum.1.part_ref, bf16[8,176,2048]{2,1,0:T(8,128)(2,1)} %bitcast.211, f32[8,32,2048]{2,1,0:T(8,128)} %bitcast.215, f32[8,8,256]{2,1,0:T(8,128)S(1)} %get-tuple-element.141.vec_ref), custom_call_target="tpu_custom_call" | custom-call | tf_op jit(solution)/shard_map/cond/branch_1_fun/cond/branch_1_fun/grad_exchange/pallas_call | solution.py:542
  1205.4 90.5 %build_table.1 = bf16[18992,2048]{1,0:T(8,128)(2,1)} custom-call(s32[1664]{0:T(1024)S(1)} %get-tuple-element.129.key_ref, s32[150]{0:T(256)} %convert_reduce_fusion.off_ref, s32[1]{0:T(128)} %bitcast.33.n_hot_ref, bf16[1408,2048]{1,0:T(8,128)(2,1)} %bitcast.209, f32[256,2048]{1,0:T(8,128)} %bitcast.214, f32[4096,2048]{1,0:T(8,128)} %get-tuple-element.144.hot_ref), custom_call_target="tpu_custom_call" | custom-call | tf_op jit(solution)/shard_map/cond/branch_1_fun/cond/branch_1_fun/build_table/pallas_call | solution.py:599
  1298.0 19.0 %fusion.117 = f32[2048,1536]{1,0:T(8,128)} fusion(bf16[2048,2048]{1,0:T(8,128)(2,1)} %get-tuple-element.173, bf16[2048,1536]{1,0:T(8,128)(2,1)} %get-tuple-element.179), kind=kOutput, calls=%fused_computation.258 | convolution fusion | flops 12884901888 | bytes 27262976 | tf_op jit(solution)/shard_map/cond/branch_1_fun/dot_general | solution.py:154
  1322.0 3.4 copy-done.14
  1325.4 21.0 %fusion.118 = f32[2048,2048]{1,0:T(8,128)} fusion(bf16[2048,2048]{1,0:T(8,128)(2,1)S(1)} %constant_dynamic-update-slice_fusion.4, bf16[2048,2048]{1,0:T(8,128)(2,1)S(1)} %bitcast.206), kind=kOutput, calls=%fused_computation.259 | convolution fusion | flops 17179869184 | bytes 33554432 | tf_op jit(solution)/shard_map/cond/branch_1_fun/dot_general | solution.py:161
  1346.4 24.6 %fusion.47 = bf16[2048,2048]{1,0:T(8,128)(2,1)} fusion(bf16[2048,2048]{1,0:T(8,128)(2,1)} %get-tuple-element.156, bf16[2048,2048]{1,0:T(8,128)(2,1)} %copy-done.14, bf16[2048,2048]{1,0:T(8,128)(2,1)} %all-gather.32.cloned.1.call-done), kind=kOutput, calls=%fused_computation.107 | convolution fusion | flops 17192452096 | bytes 33554432 | tf_op jit(solution)/shard_map/cond/branch_1_fun/dot_general | solution.py:29
  1371.0 10.3 reduce-scatter.30.cloned.1.call-done
  1382.7 84.3 %reduce-scatter.32.cloned.1.call-done = f32[256,1536]{1,0:T(8,128)} async-done(((f32[2048,1536]{1,0:T(8,128)}), f32[256,1536]{1,0:T(8,128)}) %reduce-scatter.32.cloned.1.call-update) | async-done | bytes 1572880 | tf_op jit(solution)/shard_map/cond/branch_1_fun/reduce_scatter | solution.py:756
  1469.4 83.6 %reduce-scatter.34.cloned.1.call-done = f32[256,1536]{1,0:T(8,128)} async-done(((f32[2048,1536]{1,0:T(8,128)}), f32[256,1536]{1,0:T(8,128)}) %reduce-scatter.34.cloned.1.call-update) | async-done | bytes 1572880 | tf_op jit(solution)/shard_map/cond/branch_1_fun/reduce_scatter | solution.py:756
  1555.4 83.3 %reduce-scatter.36.cloned.1.call-done = f32[256,1536]{1,0:T(8,128)} async-done(((f32[2048,1536]{1,0:T(8,128)}), f32[256,1536]{1,0:T(8,128)}) %reduce-scatter.36.cloned.1.call-update) | async-done | bytes 1572880 | tf_op jit(solution)/shard_map/cond/branch_1_fun/reduce_scatter | solution.py:756
  1640.3 2.7 pad_maximum_fusion.16
  1643.0 2.5 pad_maximum_fusion.15
  1647.0 102.7 %reduce-scatter.38.cloned.1.call-done = f32[256,2048]{1,0:T(8,128)} async-done(((f32[2048,2048]{1,0:T(8,128)}), f32[256,2048]{1,0:T(8,128)}) %reduce-scatter.38.cloned.1.call-update) | async-done | bytes 2097168 | tf_op jit(solution)/shard_map/cond/branch_1_fun/reduce_scatter | solution.py:756
  (218 shorter events, 63.8 us)
Async XLA Ops:
  32.3 31.6 %copy-start.4 = (s32[8,2048]{1,0:T(8,128)}, s32[8,2048]{1,0:T(8,128)S(1)}, u32[]{:S(2)}) copy-start(s32[8,2048]{1,0:T(8,128)S(1)} %get-tuple-element.148) | copy-start | bytes 196612 | tf_op jit(solution)/shard_map/cond
  32.3 23.4 %copy-start.35 = (bf16[256]{0:T(256)(128)(2,1)S(1)}, bf16[256]{0:T(256)(128)(2,1)}, u32[]{:S(2)}) copy-start(bf16[256]{0:T(256)(128)(2,1)} %get-tuple-element.149) | copy-start | bytes 1540 | tf_op jit(solution)/shard_map/cond
  32.3 23.4 %copy-start.37 = (bf16[256]{0:T(256)(128)(2,1)S(1)}, bf16[256]{0:T(256)(128)(2,1)}, u32[]{:S(2)}) copy-start(bf16[256]{0:T(256)(128)(2,1)} %get-tuple-element.150) | copy-start | bytes 1540 | tf_op jit(solution)/shard_map/cond
  32.3 23.4 %copy-start.39 = (bf16[256]{0:T(256)(128)(2,1)S(1)}, bf16[256]{0:T(256)(128)(2,1)}, u32[]{:S(2)}) copy-start(bf16[256]{0:T(256)(128)(2,1)} %get-tuple-element.151) | copy-start | bytes 1540 | tf_op jit(solution)/shard_map/cond
  32.3 23.5 %copy-start.41 = (bf16[256]{0:T(256)(128)(2,1)S(1)}, bf16[256]{0:T(256)(128)(2,1)}, u32[]{:S(2)}) copy-start(bf16[256]{0:T(256)(128)(2,1)} %get-tuple-element.152) | copy-start | bytes 1540 | tf_op jit(solution)/shard_map/cond
  32.3 43.4 %sort.96.cloned.1.call-start = ((), (), s32[]{:S(2)}) async-start(), calls=%async_computation.38 | async-start | bytes 196640 | tf_op jit(solution)/shard_map/cond/branch_1_fun/sort | solution.py:630
  49.7 267.9 %sort.98.cloned.1.call-start = ((), (), s32[]{:S(2)}) async-start(), calls=%async_computation.39 | async-start | bytes 196640 | tf_op jit(solution)/shard_map/cond/branch_1_fun/sort | solution.py:648
  50.4 267.9 %sort.100.cloned.1.call-start = ((), (), s32[]{:S(2)}) async-start(), calls=%async_computation.40 | async-start | bytes 196640 | tf_op jit(solution)/shard_map/cond/branch_1_fun/sort | solution.py:648
  51.1 298.8 %all-gather.30.cloned.1.call-start = ((), (), s32[]{:S(2)}) async-start(), calls=%async_computation.28 | async-start | bytes 7077888 | tf_op jit(solution)/shard_map/cond/branch_1_fun/all_gather | solution.py:753
  55.1 314.1 %all-gather.32.cloned.1.call-start = ((), (), s32[]{:S(2)}) async-start(), calls=%async_computation.29 | async-start | bytes 9437184 | tf_op jit(solution)/shard_map/cond/branch_1_fun/all_gather | solution.py:753
  55.7 394.8 %all-gather.34.cloned.1.call-start = ((), (), s32[]{:S(2)}) async-start(), calls=%async_computation.30 | async-start | bytes 7077888 | tf_op jit(solution)/shard_map/cond/branch_1_fun/all_gather | solution.py:753
  117.2 191.3 %copy-start.16 = (s32[2,1024]{1,0:T(2,128)S(1)}, s32[2,1024]{1,0:T(2,128)}, u32[]{:S(2)}) copy-start(s32[2,1024]{1,0:T(2,128)} %get-tuple-element.146) | copy-start | bytes 24580 | tf_op jit(solution)/shard_map/cond
  305.6 236.0 %all-gather.36.cloned.1.call-start = ((), (), s32[]{:S(2)}) async-start(), calls=%async_computation.31 | async-start | bytes 7077888 | tf_op jit(solution)/shard_map/cond/branch_1_fun/all_gather | solution.py:753
  306.4 325.3 %all-gather.38.cloned.1.call-start = ((), (), s32[]{:S(2)}) async-start(), calls=%async_computation.32 | async-start | bytes 7077888 | tf_op jit(solution)/shard_map/cond/branch_1_fun/all_gather | solution.py:753
  307.1 491.9 %sort.104.cloned.1.call-start = ((), (), s32[]{:S(2)}) async-start(), calls=%async_computation.42 | async-start | bytes 196640 | tf_op jit(solution)/shard_map/cond/branch_1_fun/sort | solution.py:648
  307.9 491.1 %sort.102.cloned.1.call-start = ((), (), s32[]{:S(2)}) async-start(), calls=%async_computation.41 | async-start | bytes 196640 | tf_op jit(solution)/shard_map/cond/branch_1_fun/sort | solution.py:648
  650.9 42.1 %copy-start.26 = (f32[1,3,512]{2,0,1:T(1,128)S(1)}, f32[1,3,512]{2,0,1:T(1,128)}, u32[]{:S(2)}) copy-start(f32[1,3,512]{2,0,1:T(1,128)} %stack.75) | copy-start | bytes 18436 | tf_op jit(solution)/shard_map/cond
  650.9 42.1 %copy-start.28 = (f32[1,3,512]{2,0,1:T(1,128)S(1)}, f32[1,3,512]{2,0,1:T(1,128)}, u32[]{:S(2)}) copy-start(f32[1,3,512]{2,0,1:T(1,128)} %stack.76) | copy-start | bytes 18436 | tf_op jit(solution)/shard_map/cond
  693.1 39.3 %slice-start.6 = ((s8[6291456]{0:T(1024)(128)(4,1)}), s8[4194304]{0:T(1024)(128)(4,1)S(1)}, s32[]{:S(2)}) async-start(s8[6291456]{0:T(1024)(128)(4,1)} %bitcast.267), calls=%async_computation.54 | async-start | bytes 8388608 | tf_op jit(solution)/shard_map/cond
  693.1 39.3 %slice-start.10 = ((s8[6291456]{0:T(1024)(128)(4,1)}), s8[4194304]{0:T(1024)(128)(4,1)S(1)}, s32[]{:S(2)}) async-start(s8[6291456]{0:T(1024)(128)(4,1)} %bitcast.273), calls=%async_computation.58 | async-start | bytes 8388608 | tf_op jit(solution)/shard_map/cond
  712.7 19.7 %slice-start.7 = ((s8[6291456]{0:T(1024)(128)(4,1)}), s8[2097152]{0:T(1024)(128)(4,1)S(1)}, s32[]{:S(2)}) async-start(s8[6291456]{0:T(1024)(128)(4,1)} %bitcast.267), calls=%async_computation.55 | async-start | bytes 4194304 | tf_op jit(solution)/shard_map/cond
  712.7 19.7 %slice-start.11 = ((s8[6291456]{0:T(1024)(128)(4,1)}), s8[2097152]{0:T(1024)(128)(4,1)S(1)}, s32[]{:S(2)}) async-start(s8[6291456]{0:T(1024)(128)(4,1)} %bitcast.273), calls=%async_computation.59 | async-start | bytes 4194304 | tf_op jit(solution)/shard_map/cond
  732.4 16.4 copy-start.21
  732.4 16.4 copy-start.23
  781.6 17.5 copy-start.5
  781.6 17.5 copy-start.24
  781.6 17.5 copy-start.25
  804.8 28.1 %collective-permute-start = (f32[2048,2048]{1,0:T(8,128)}, f32[2048,2048]{1,0:T(8,128)}, u32[]{:S(2)}, u32[]{:S(2)}) collective-permute-start(f32[2048,2048]{1,0:T(8,128)} %get-tuple-element.133.mine_ref.rows_ref), channel_id=1, source_target_pairs={{0,1},{1,0},{2,3},{3,2},{4,5},{5,4},{6,7},{7,6}} | collective-permute-start | bytes 50331656 | tf_op jit(solution)/shard_map/cond/branch_1_fun/cond/branch_1_fun/ppermute | solution.py:699
  813.4 18.0 %copy-start.22 = (s32[4096]{0:T(1024)}, s32[4096]{0:T(1024)S(1)}, u32[]{:S(2)}) copy-start(s32[4096]{0:T(1024)S(1)} %get-tuple-element.132.key_ref) | copy-start | bytes 49156 | tf_op jit(solution)/shard_map/cond/branch_1_fun/cond
  1295.8 1.4 copy-start.29
  1295.9 1.4 copy-start.30
  1295.9 1.4 copy-start.31
  1295.9 1.4 copy-start.32
  1295.9 85.4 %reduce-scatter.30.cloned.1.call-start = ((), (), s32[]{:S(2)}) async-start(), calls=%async_computation.33 | async-start | bytes 14155776 | tf_op jit(solution)/shard_map/cond/branch_1_fun/reduce_scatter | solution.py:756
  1296.6 170.4 %reduce-scatter.32.cloned.1.call-start = ((), (), s32[]{:S(2)}) async-start(), calls=%async_computation.34 | async-start | bytes 14155776 | tf_op jit(solution)/shard_map/cond/branch_1_fun/reduce_scatter | solution.py:756
  1297.2 255.7 %reduce-scatter.34.cloned.1.call-start = ((), (), s32[]{:S(2)}) async-start(), calls=%async_computation.35 | async-start | bytes 14155776 | tf_op jit(solution)/shard_map/cond/branch_1_fun/reduce_scatter | solution.py:756
  1298.0 340.8 %reduce-scatter.36.cloned.1.call-start = ((), (), s32[]{:S(2)}) async-start(), calls=%async_computation.36 | async-start | bytes 14155776 | tf_op jit(solution)/shard_map/cond/branch_1_fun/reduce_scatter | solution.py:756
  1317.0 1.6 copy-start.6
  1317.1 432.6 %reduce-scatter.38.cloned.1.call-start = ((), (), s32[]{:S(2)}) async-start(), calls=%async_computation.37 | async-start | bytes 18874368 | tf_op jit(solution)/shard_map/cond/branch_1_fun/reduce_scatter | solution.py:756
  1317.3 4.0 copy-start.7
  1317.3 4.3 copy-start.8
  1318.6 6.7 slice-start.4
  1321.3 4.1 slice-start.5
  1322.0 3.4 copy-start.14
Sparse Core Ops, SparseCore 0:
  49.8 7.5 sort.106.cloned.1.call-done
  60.6 7.5 sort.108.cloned.1.call-done
  70.9 7.5 sort.110.cloned.1.call-done
  81.0 39.9 all-gather.29
  122.7 100.8 all-gather.31
  305.7 73.7 all-gather.33
  381.9 39.7 all-gather.35
  423.5 39.5 all-gather.37
  465.5 7.5 sort.114.cloned.1.call-done
  475.7 7.5 sort.112.cloned.1.call-done
  1300.1 81.0 reduce-scatter.29
  1384.5 82.4 reduce-scatter.31
  1470.5 82.4 reduce-scatter.33
  1556.3 82.4 reduce-scatter.35
  1642.7 106.9 reduce-scatter.37
  (5 shorter events, 0.1 us)

commit v3 on v2

--- a/solution.py
+++ b/solution.py
@@ -15,13 +15,14 @@
 N_DEV = 8
 HOT = 4096
 CAP = 176
-MORE = 32
+MORE = 24
 LANES = 128
 BIG = 2**31 - 1
 MESH = pl.DeviceIdType.MESH
-BLOCK_Q = 256
+BLOCK_Q = 512
 GROUPS = 4
 ROW_BLOCK = 128
+TABLE_BLOCK = 512
 VMEM_MAX = 60 * 1024 * 1024
 
 
@@ -103,13 +104,15 @@
     return cos_t, sin_t
 
 
-def attention(lin, d_attn, bias, cos_t, sin_t):
-    tokens, width = d_attn.shape
+def attention(lin, d_attn, bias, cos_t, sin_t, part, parts):
+    tokens = lin.shape[0]
+    width = d_attn.shape[1] // parts
     seq_len = cos_t.shape[0]
     n_seq, n_heads = tokens // seq_len, width // HEAD_DIM
     tile = pl.BlockSpec((seq_len, HEAD_DIM), lambda s, h: (s, h))
     third = [pl.BlockSpec((seq_len, HEAD_DIM), lambda s, h, j=j: (s, j * n_heads + h)) for j in range(3)]
     third_b = [pl.BlockSpec((1, HEAD_DIM), lambda s, h, j=j: (0, j * n_heads + h)) for j in range(3)]
+    tile_in = pl.BlockSpec((seq_len, HEAD_DIM), lambda s, h: (s, part * n_heads + h))
     table = pl.BlockSpec((seq_len, HEAD_DIM), lambda s, h: (0, 0))
     pairs = n_seq * n_heads * seq_len * seq_len
     head_buf = pltpu.VMEM((seq_len, HEAD_DIM), jnp.bfloat16)
@@ -117,7 +120,7 @@
     return pl.pallas_call(
         attn_kernel,
         grid=(n_seq, n_heads),
-        in_specs=[*third, tile, table, table, *third_b],
+        in_specs=[*third, tile_in, table, table, *third_b],
         out_specs=[
             tile,
             pl.BlockSpec((seq_len, 3 * width), lambda s, h: (s, 0)),
@@ -141,16 +144,15 @@
     f32 = jnp.float32
     tn = (((0,), (0,)), ((), ()))
     n_groups = len(w_groups)
-    group = w_out.shape[0] // n_groups
     cos_t, sin_t = rope_tables(seq_len)
     x_full = x_rows.astype(f32)
     x_norm = x_full * inv_rms
     outs, d_lins, bias_grads, grad_ws = [], [], [], []
     hid = hidden
+    d_attn = dot_nt(grad_out, w_out).astype(jnp.bfloat16)
     for g in range(n_groups):
         lin = dot_nn(hid, w_groups[g])
-        d_attn = dot_nt(grad_out, w_out[g * group:(g + 1) * group]).astype(jnp.bfloat16)
-        o_g, d_lin, gb = attention(lin, d_attn, biases[g], cos_t, sin_t)
+        o_g, d_lin, gb = attention(lin, d_attn, biases[g], cos_t, sin_t, g, n_groups)
         grad_w = lax.dot_general(hidden, d_lin, tn, preferred_element_type=f32)
         hid, grad_w = lax.optimization_barrier((hidden, grad_w))
         grad_ws.append(on_grad(grad_w))
@@ -176,7 +178,7 @@
     pl.semaphore_wait(barrier, N_DEV - 1)
 
 
-LOOK_CHUNK = 128
+LOOK_CHUNK = 64
 LOOK_N = HOT // 2 // LOOK_CHUNK
 
 
@@ -243,10 +245,15 @@
                 mate_copy(part, k).start()
         return carry
 
+    def start_cold():
+        for step in range(1, N_DEV):
+            cold_copy(step).start()
+
     for step in range(1, N_DEV):
         vec_copy(step).start()
-        cold_copy(step).start()
+    pl.when(me != 0)(start_cold)
     lax.fori_loop(0, LOOK_N + 3, stage, 0)
+    pl.when(me == 0)(start_cold)
 
     def drain(k, carry):
         for part in range(2):
@@ -425,7 +432,7 @@
     )(keys, offs, dx_mine, dx_mate)
 
 
-RED_CHUNK = 64
+RED_CHUNK = 32
 RED_N = HOT // 2 // RED_CHUNK
 
 
@@ -484,9 +491,12 @@
     barrier_all(me)
     for which in range(3):
         keep(which).start()
-    for which in range(3):
+    for which in range(2):
         for step in range(1, N_DEV):
             swap(which, step).start()
+
+    def cold_at(k, step):
+        return jnp.where(place >= 2, k == 0, k == 4 * step)
 
     def stage(k, carry):
         @pl.when(k < RED_N)
@@ -501,6 +511,11 @@
         @pl.when((k >= 1) & (place < 3))
         def _():
             send(k - 1).start()
+
+        for step in range(1, N_DEV):
+            @pl.when(cold_at(k, step))
+            def _():
+                swap(2, step).start()
 
         @pl.when((k >= 1) & (me == 0))
         def _():
@@ -581,7 +596,7 @@
 
     def body(e, carry):
         key = key_ref[e]
-        row = lax.shift_right_logical(key, 11) - blk * ROW_BLOCK
+        row = lax.shift_right_logical(key, 11) - blk * TABLE_BLOCK
         idx = jnp.bitwise_and(key, 2047)
         acc[pl.ds(row, 1), :] += rows[pl.ds(idx, 1), :]
         return carry
@@ -600,15 +615,15 @@
         table_kernel,
         grid_spec=pltpu.PrefetchScalarGridSpec(
             num_scalar_prefetch=3,
-            grid=(pl.cdiv(n_rows, ROW_BLOCK),),
+            grid=(pl.cdiv(n_rows, TABLE_BLOCK),),
             in_specs=[
                 pl.BlockSpec(memory_space=pl.ANY),
                 pl.BlockSpec(memory_space=pl.ANY),
-                pl.BlockSpec((ROW_BLOCK, width), hot_index),
+                pl.BlockSpec((TABLE_BLOCK, width), hot_index),
             ],
-            out_specs=pl.BlockSpec((ROW_BLOCK, width), lambda i, k, o, n: (i, 0)),
+            out_specs=pl.BlockSpec((TABLE_BLOCK, width), lambda i, k, o, n: (i, 0)),
             scratch_shapes=[
-                pltpu.VMEM((ROW_BLOCK, width), jnp.float32),
+                pltpu.VMEM((TABLE_BLOCK, width), jnp.float32),
                 pltpu.VMEM((src.shape[0] + more.shape[0], width), jnp.float32),
                 pltpu.VMEM(src.shape, src.dtype),
                 pltpu.SemaphoreType.DMA((2,)),
@@ -620,26 +635,27 @@
     )(keys, offs, n_hot, src, more, hot)
 
 
-def fast_lookup(all_ids, own_ids, table_part, gain_vecs, me):
-    rows_dev, width = table_part.shape
+def lookup_plan(all_ids, own_ids, me, rows_dev):
     tokens = own_ids.shape[0]
+    t_idx = jnp.arange(tokens, dtype=jnp.int32)
+    devices = jnp.arange(N_DEV, dtype=jnp.int32)
     first_row = me * rows_dev
-    t_idx = jnp.arange(tokens, dtype=jnp.int32)
     mine = (all_ids >= HOT) & (all_ids >= first_row) & (all_ids < first_row + rows_dev)
-    key = jnp.where(mine, t_idx[None, :] * 32768 + (all_ids - first_row), BIG)
-    key = lax.sort(key, dimension=1)[:, :CAP]
-    asked = key != BIG
-    ask_row = jnp.where(asked, jnp.bitwise_and(key, 32767), 0)
-    send = jnp.take(table_part, ask_row.reshape(-1), axis=0, mode="clip")
+    key = first_of(mine, t_idx[None, :] * 32768 + (all_ids - first_row), CAP)
+    ask_row = jnp.where(key != BIG, jnp.bitwise_and(key, 32767), 0).reshape(-1)
+    hit = (own_ids // rows_dev == devices[:, None]) & (own_ids >= HOT)[None, :]
+    place = jnp.cumsum(hit.astype(jnp.int32), axis=1) - 1 + devices[:, None] * CAP
+    idx = jnp.where(own_ids >= HOT, HOT + jnp.sum(jnp.where(hit, place, 0), axis=0), own_ids)
+    return ask_row, idx
+
+
+def fast_lookup(ask_row, idx, table_part, gain_vecs):
+    width = table_part.shape[1]
+    send = jnp.take(table_part, ask_row, axis=0, mode="clip")
     tiles = (width // LANES, LANES)
     send = send.reshape((N_DEV, CAP) + tiles)
     hot, cold, vecs = lookup_exchange(send, table_part[:HOT].reshape((HOT,) + tiles), gain_vecs)
     vecs = vecs.transpose(1, 0, 2).reshape(gain_vecs.shape[0], -1).astype(jnp.float32)
-    owners = own_ids // rows_dev
-    hit = (owners[None, :] == jnp.arange(N_DEV, dtype=jnp.int32)[:, None]) & (own_ids >= HOT)[None, :]
-    place = jnp.cumsum(hit.astype(jnp.int32), axis=1) - 1 + jnp.arange(N_DEV, dtype=jnp.int32)[:, None] * CAP
-    slot = jnp.sum(jnp.where(hit, place, 0), axis=0)
-    idx = jnp.where(own_ids >= HOT, HOT + slot, own_ids)
     normed = pick_rows(idx, hot, cold.reshape((N_DEV * CAP,) + tiles), vecs[:1], 256)
     return normed, cold, vecs
 
@@ -648,8 +664,7 @@
     return lax.sort(jnp.where(mask, values, BIG), dimension=1)[:, :count]
 
 
-def grad_plan(all_ids, own_ids, me, rows_dev):
-    tokens = own_ids.shape[0]
+def repeats(all_ids):
     flat = all_ids.reshape(-1).astype(jnp.uint32)
     pos = jnp.arange(flat.shape[0], dtype=jnp.uint32)
     ordered = lax.sort(flat * jnp.uint32(16384) + pos)
@@ -658,12 +673,14 @@
     no = jnp.zeros((1,), jnp.bool_)
     again = jnp.concatenate([no, same]) | jnp.concatenate([same, no])
     again = lax.sort((ordered % jnp.uint32(16384)) * jnp.uint32(2) + again.astype(jnp.uint32)) % jnp.uint32(2)
-    again = (again == 1).reshape(all_ids.shape)
+    return (again == 1).reshape(all_ids.shape)
+
+
+def grad_plan(all_ids, own_ids, again, me, rows_dev):
+    tokens = own_ids.shape[0]
     t_idx = jnp.arange(tokens, dtype=jnp.int32)[None, :]
     devices = jnp.arange(N_DEV, dtype=jnp.int32)
     owners = jnp.where(all_ids >= HOT, all_ids // rows_dev, -1)
-    counts = jnp.sum(((owners[None] == devices[:, None, None]) & again[None]).astype(jnp.int32), axis=-1)
-    fits = jnp.max(counts) <= MORE
     hit = lax.dynamic_index_in_dim(owners, me, 0, keepdims=False)[None, :] == devices[:, None]
     own_again = lax.dynamic_index_in_dim(again, me, 0, keepdims=True)
     slot_tok = first_of(hit, t_idx, CAP)
@@ -684,11 +701,11 @@
     def clean(tok):
         return jnp.where(tok == BIG, 0, tok).reshape(-1)
 
-    return fits, clean(slot_tok), clean(more_tok), owner_keys
-
-
-def block_offsets(keys, n_blocks, shift):
-    edges = jnp.arange(n_blocks + 1, dtype=jnp.int32) * (ROW_BLOCK << shift)
+    return clean(slot_tok), clean(more_tok), owner_keys
+
+
+def block_offsets(keys, n_blocks, block, shift):
+    edges = jnp.arange(n_blocks + 1, dtype=jnp.int32) * (block << shift)
     return jnp.sum(keys[None, :] < edges[:, None], axis=1).astype(jnp.int32)
 
 
@@ -703,13 +720,13 @@
     inside = (pair_ids >= base) & (pair_ids < base + HOT // 2)
     keys = jnp.where(inside, (pair_ids - base) * 4096 + jnp.arange(2 * tokens, dtype=jnp.int32), BIG)
     keys = lax.sort(keys)
-    part = seg_sum(keys, block_offsets(keys, HOT // 2 // ROW_BLOCK, 12), d_x, dx_mate, HOT // 2)
+    part = seg_sum(keys, block_offsets(keys, HOT // 2 // ROW_BLOCK, ROW_BLOCK, 12), d_x, dx_mate, HOT // 2)
     cold, more = take2d(slot_tok, more_tok, d_x, N_DEV)
     cold = cold.reshape(N_DEV, CAP, width)
     more = more.reshape(N_DEV, MORE, width)
     hot, recv, more_recv, vec_recv = grad_exchange(part, cold, more, vecs)
-    n_hot = jnp.where(me == 0, HOT // ROW_BLOCK, 0).astype(jnp.int32)[None]
-    offs = block_offsets(owner_keys, pl.cdiv(rows_dev, ROW_BLOCK), 11)
+    n_hot = jnp.where(me == 0, HOT // TABLE_BLOCK, 0).astype(jnp.int32)[None]
+    offs = block_offsets(owner_keys, pl.cdiv(rows_dev, TABLE_BLOCK), TABLE_BLOCK, 11)
     recv = recv.reshape(N_DEV * CAP, width)
     more_recv = more_recv.reshape(N_DEV * MORE, width)
     grad_part = build_table(owner_keys, offs, n_hot, recv, more_recv, hot, rows_dev)
@@ -725,7 +742,7 @@
     return lax.psum_scatter(looked, AXIS, scatter_dimension=0)
 
 
-def slow_table_grad(rows_dev, all_ids, own_ids, d_x, vecs, *_):
+def slow_table_grad(rows_dev, all_ids, d_x, vecs):
     me = lax.axis_index(AXIS)
     local_idx = all_ids - me * rows_dev
     is_owned = (local_idx >= 0) & (local_idx < rows_dev)
@@ -743,7 +760,7 @@
     in_specs = (row_spec, act_spec, row_spec) + weight_specs
     out_specs = (act_spec, row_spec) + weight_specs
 
-    def run(fast, tok_ids, all_ids, grad_out, table_part, gain_part, wq_part, bq_part, wk_part, bk_part, wv_part, bv_part, wo_part):
+    def run(fast, tok_ids, all_ids, again, ask_row, idx, grad_out, table_part, gain_part, wq_part, bq_part, wk_part, bk_part, wv_part, bv_part, wo_part):
         me = lax.axis_index(AXIS)
         rows_dev, width = table_part.shape
         n_seq, seq_len = tok_ids.shape
@@ -761,9 +778,9 @@
         vec_parts = jnp.pad(jnp.stack([gain_part, bq_part, bk_part, bv_part]), ((0, 12), (0, 0)))
         w_parts = [jnp.concatenate([wq_part[:, c], wk_part[:, c], wv_part[:, c]], axis=1) for c in cols]
         if fast:
-            (x_rows, hidden, inv_rms), marker, vec_full = fast_lookup(all_ids, own_ids, table_part, vec_parts, me)
-            late = lax.optimization_barrier((marker, *w_parts[1:]))
-            w_parts = [w_parts[0], *late[1:]]
+            (x_rows, hidden, inv_rms), marker, vec_full = fast_lookup(ask_row, idx, table_part, vec_parts)
+            late = lax.optimization_barrier((marker, all_ids, own_ids, again, wo_part, *w_parts[1:]))
+            plan_ids, wo_part, w_parts = late[1:4], late[4], [w_parts[0], *late[5:]]
         else:
             x_rows = slow_lookup(all_ids, table_part, me)
             vec_full = lax.all_gather(vec_parts, AXIS, axis=1, tiled=True).astype(jnp.float32)
@@ -783,21 +800,23 @@
         vecs = jnp.pad(vecs.reshape(4, N_DEV, part_w).transpose(1, 0, 2), ((0, 0), (0, 4), (0, 0)))
         rest = (all_ids, own_ids, d_x, vecs)
         if fast:
-            few, slot_tok, more_tok, owner_keys = grad_plan(all_ids, own_ids, me, rows_dev)
-            rest = rest + (slot_tok, more_tok, owner_keys)
-            grad_part, vec_sum = lax.cond(
-                few, functools.partial(fast_table_grad, rows_dev), functools.partial(slow_table_grad, rows_dev), *rest)
+            grad_part, vec_sum = fast_table_grad(rows_dev, *rest, *grad_plan(*plan_ids, me, rows_dev))
         else:
-            grad_part, vec_sum = slow_table_grad(rows_dev, *rest)
+            grad_part, vec_sum = slow_table_grad(rows_dev, all_ids, d_x, vecs)
         return (block_out.reshape(grad_out.shape), grad_part, vec_sum[0], gq, vec_sum[1], gk, vec_sum[2], gv, vec_sum[3], grad_wo)
 
     def device_step(tok_ids, grad_out, table_part, *weights):
         rows_dev = table_part.shape[0]
         all_ids = lax.all_gather(tok_ids.reshape(-1), AXIS)
+        me = lax.axis_index(AXIS)
+        again = repeats(all_ids)
         owners = jnp.where(all_ids >= HOT, all_ids // rows_dev, -1)
-        counts = jnp.sum((owners[None] == jnp.arange(N_DEV, dtype=jnp.int32)[:, None, None]).astype(jnp.int32), axis=-1)
-        fits = jnp.max(counts) <= CAP
-        args = (tok_ids, all_ids, grad_out, table_part) + weights
+        asked = owners[None] == jnp.arange(N_DEV, dtype=jnp.int32)[:, None, None]
+        counts = jnp.sum(asked.astype(jnp.int32), axis=-1)
+        more = jnp.sum((asked & again[None]).astype(jnp.int32), axis=-1)
+        fits = (jnp.max(counts) <= CAP) & (jnp.max(more) <= MORE)
+        ask_row, idx = lookup_plan(all_ids, tok_ids.reshape(-1), me, rows_dev)
+        args = (tok_ids, all_ids, again, ask_row, idx, grad_out, table_part) + weights
         return lax.cond(fits, functools.partial(run, True), functools.partial(run, False), *args)
 
     return jax.shard_map(device_step, mesh=mesh, in_specs=in_specs, out_specs=out_specs, check_vma=False)

time: 1770 us -> 1360 us (0.77)
  waiting for transfers between devices: 368 us -> 67.4 us
  Pallas kernels: 847 us -> 770 us
    reduce_scatter x5, waiting for transfers between devices: 364 us -> 0.03 us  [scatter(): return lax.psum_scatter(grad, AXIS, scatter_dimension=0, tiled=True)]
    all_gather x5, waiting for transfers between devices: 0.01 us -> 65.7 us  [whole(): return lax.all_gather(part, AXIS, axis=0, tiled=True)]
    pallas_call x1, Pallas kernels: 90.5 us -> 54.3 us  [build_table(): pl.pallas_call(table_kernel, grid_spec=pltpu.PrefetchScalarGridSpec(num_s...]
    pallas_call x1, Pallas kernels: 188 us -> 155 us  [lookup_exchange(): pl.pallas_call(lookup_kernel, out_shape=[jax.ShapeDtypeStruct(hot_rows.sh...]
    pallas_call x4, Pallas kernels: 164 us -> 138 us  [attention(): pl.pallas_call(attn_kernel, grid=(n_seq, n_heads), in_specs=[*third, tile...]
    dot_general x8 -> x5, matrix products: 128 us -> 110 us  [dot_nt(): lax.dot_general(a, b, (((1,), (1,)), ((), ())), preferred_element_type=jn...]
    cond x73 -> x75, local copies, waits for them, and re-layouts: 36.4 us -> 34.3 us
  transfers between devices with their start and end apart: 11 -> 11, of which waited for: 5 -> 1; matrix products, arithmetic and copies ran while one was open for 19% -> 32% of each run, Pallas kernels for 20% -> 57%
where the time goes in v3:
time: 1360 us; the launch traced here: 1350 us
  Pallas kernels  770 us (57%)
  matrix products  310 us (23%)
  local copies, waits for them, and re-layouts  82.7 us (6%)
  other arithmetic  77.5 us (6%)
  waiting for transfers between devices  67.4 us (5%)
  between operations  17.3 us (1%)
  blocking collectives  13.9 us (1%)
    pallas_call x1, Pallas kernels, grad_exchange(): pl.pallas_call(reduce_kernel, out_shape=[jax.ShapeDtypeStruct((HOT, width...  351 us
    pallas_call x1, Pallas kernels, lookup_exchange(): pl.pallas_call(lookup_kernel, out_shape=[jax.ShapeDtypeStruct(hot_rows.sh...  155 us
    pallas_call x4, Pallas kernels, attention(): pl.pallas_call(attn_kernel, grid=(n_seq, n_heads), in_specs=[*third, tile...  138 us
    dot_general x5, matrix products, dot_nt(): lax.dot_general(a, b, (((1,), (1,)), ((), ())), preferred_element_type=jn...  110 us
    dot_general x5, matrix products, dot_nn(): lax.dot_general(a, b, (((1,), (0,)), ((), ())), preferred_element_type=jn...  102 us
    dot_general x4, matrix products, block_fwd_bwd(): grad_w = lax.dot_general(hidden, d_lin, tn, preferred_element_type=f32)  76.2 us
    all_gather x5, waiting for transfers between devices, whole(): return lax.all_gather(part, AXIS, axis=0, tiled=True)  65.7 us
    pallas_call x1, Pallas kernels, build_table(): pl.pallas_call(table_kernel, grid_spec=pltpu.PrefetchScalarGridSpec(num_s...  54.3 us
  transfers between devices with their start and end apart: 11, of which 1 were waited for; matrix products, arithmetic and copies ran while one was open for 32% of the time, Pallas kernels for 57%

profile of v3, /device:TPU:0, one launch (start us, length us, event | category | flops | bytes accessed | tf_op | source)
XLA Modules:
  0.0 1348.3 jit_solution(12700073271364058770)
XLA Ops:
  8.8 13.9 %all-gather.1 = s32[8,1,2048]{2,1,0:T(1,128)S(1)} all-gather(s32[1,1,2048]{2,1,0:T(1,128)S(1)} %reshape.324), channel_id=1, replica_groups=mesh['fsdp'=8] {'fsdp'}, dimensions={0}, use_global_device_ids=true | all-gather | bytes 73728 | tf_op jit(solution)/shard_map/all_gather | solution.py:810
  25.0 7.7 sort.91
  32.9 8.3 sort.93
  41.9 2.3 reduce-window.6
  47.5 1293.0 %conditional.1 = (bf16[2,1024,2048]{2,1,0:T(8,128)(2,1)}, bf16[18992,2048]{1,0:T(8,128)(2,1)}, f32[256]{0:T(256)}, f32[256,2048]{1,0:T(8,128)}, f32[256]{0:T(256...) conditional(s32[]{:T(128)} %convert_element_type.88, ...), branch_computations={%region_10.26_spmd, %region_26.47_spmd} | conditional | flops 257974468608 | bytes 2525248768 | solution.py:820
  56.4 1.7 fusion.77
  60.6 28.1 %gather_fusion.1 = bf16[1408,2048]{1,0:T(8,128)(2,1)} fusion(bf16[18992,2048]{1,0:T(8,128)(2,1)} %get-tuple-element.87, s32[2048]{0:T(1024)S(1)} %pad_clamp_fusion), kind=kCustom, calls=%fused_computation.1 | custom fusion | bytes 11539968 | tf_op jit(solution)/shard_map/cond/branch_1_fun/jit(_take)/gather | solution.py:654
  88.7 7.3 copy.53
  96.0 8.0 slice_bitcast_fusion
  104.0 8.5 copy.54
  113.1 155.3 %lookup_exchange.1 = (bf16[4096,16,128]{2,1,0:T(8,128)(2,1)}, bf16[8,176,16,128]{3,2,1,0:T(8,128)(2,1)}, bf16[8,16,256]{2,1,0:T(8,128)(2,1)}) custom-call(bf16[8,176,16,128]{3,2,1,0:T(8,128)(2,1)} %bitcast.186, bf16[4096,16,128]{2,1,0:T(8,128)(2,1)} %bitcast.177, bf16[16,256]{1,0:T(8,128)(2,1)} %fusion.26.vec_ref), custom_call_target="tpu_custom_call", output_to_operand_aliasing={{0}: (1, {})} | custom-call | tf_op jit(solution)/shard_map/cond/branch_1_fun/lookup_exchange/pallas_call | solution.py:280
  276.1 2.0 fusion.12
  282.0 20.0 %pick_rows.1 = (bf16[2048,2048]{1,0:T(8,128)(2,1)}, bf16[2048,2048]{1,0:T(8,128)(2,1)}, f32[2048,1]{1,0:T(8,128)}) custom-call(s32[2048]{0:T(1024)} %compare_select_fusion.idx_ref, bf16[4096,16,128]{2,1,0:T(8,128)(2,1)} %get-tuple-element.93.hot_ref, bf16[1408,16,128]{2,1,0:T(8,128)(2,1)} %bitcast.189, f32[1,2048]{1,0:T(1,128)} %bitcast.204), custom_call_target="tpu_custom_call" | custom-call | tf_op jit(solution)/shard_map/cond/branch_1_fun/pick_rows/pallas_call | solution.py:332
  302.0 19.2 %fusion.95.q_ref.k_ref.v_ref = f32[2048,1536]{1,0:T(8,128)} fusion(bf16[2048,2048]{1,0:T(8,128)(2,1)} %get-tuple-element.117, bf16[2048,1536]{1,0:T(8,128)(2,1)} %all-gather.26.cloned.1.call-done), kind=kOutput, calls=%fused_computation.224 | convolution fusion | flops 12884901888 | bytes 27262976 | tf_op jit(solution)/shard_map/cond/branch_1_fun/dot_general | solution.py:30
  321.3 65.6 %all-gather.28.cloned.1.call-done = bf16[2048,2048]{1,0:T(8,128)(2,1)} async-done(((bf16[256,2048]{1,0:T(8,128)(2,1)}), bf16[2048,2048]{1,0:T(8,128)(2,1)}) %all-gather.28.cloned.1.call-update) | async-done | bytes 8388624 | tf_op jit(solution)/shard_map/cond/branch_1_fun/all_gather | solution.py:770
  386.9 23.6 %convert_bitcast_fusion.do_ref = bf16[2048,2048]{1,0:T(8,128)(2,1)} fusion(bf16[2048,2048]{1,0:T(8,128)(2,1)} %all-gather.28.cloned.1.call-done, bf16[2048,2048]{1,0:T(8,128)(2,1)} %bitcast.182), kind=kOutput, calls=%fused_computation.17 | convolution fusion | flops 17184063488 | bytes 25165824 | tf_op jit(solution)/shard_map/cond/branch_1_fun/dot_general | solution.py:34
  410.5 34.5 %attn_fwd_bwd.12 = (bf16[2048,512]{1,0:T(8,128)(2,1)}, bf16[2048,1536]{1,0:T(8,128)(2,1)}, f32[2,8,1536]{2,1,0:T(8,128)}) custom-call(f32[2048,1536]{1,0:T(8,128)} %fusion.95.q_ref.k_ref.v_ref, f32[2048,1536]{1,0:T(8,128)} %fusion.95.q_ref.k_ref.v_ref, f32[2048,1536]{1,0:T(8,128)} %fusion.95.q_ref.k_ref.v_ref, ...), custom_call_target="tpu_custom_call" | custom-call | flops 12884901888 | bytes 23068672 | tf_op jit(solution)/shard_map/cond/branch_1_fun/attn_fwd_bwd/pallas_call | solution.py:120
  445.0 19.2 %fusion.96 = f32[2048,1536]{1,0:T(8,128)} fusion(bf16[2048,2048]{1,0:T(8,128)(2,1)} %get-tuple-element.117, bf16[2048,1536]{1,0:T(8,128)(2,1)} %get-tuple-element.108), kind=kOutput, calls=%fused_computation.225 | convolution fusion | flops 12884901888 | bytes 27262976 | tf_op jit(solution)/shard_map/cond/branch_1_fun/dot_general | solution.py:156
  464.9 19.2 %fusion.97.q_ref.k_ref.v_ref = f32[2048,1536]{1,0:T(8,128)} fusion(bf16[2048,2048]{1,0:T(8,128)(2,1)} %get-tuple-element.117, bf16[2048,1536]{1,0:T(8,128)(2,1)} %all-gather.30.cloned.1.call-done), kind=kOutput, calls=%fused_computation.226 | convolution fusion | flops 12884901888 | bytes 27262976 | tf_op jit(solution)/shard_map/cond/branch_1_fun/dot_general | solution.py:30
  484.1 34.4 %attn_fwd_bwd.13 = (bf16[2048,512]{1,0:T(8,128)(2,1)}, bf16[2048,1536]{1,0:T(8,128)(2,1)}, f32[2,8,1536]{2,1,0:T(8,128)}) custom-call(f32[2048,1536]{1,0:T(8,128)} %fusion.97.q_ref.k_ref.v_ref, f32[2048,1536]{1,0:T(8,128)} %fusion.97.q_ref.k_ref.v_ref, f32[2048,1536]{1,0:T(8,128)} %fusion.97.q_ref.k_ref.v_ref, ...), custom_call_target="tpu_custom_call" | custom-call | flops 12884901888 | bytes 23068672 | tf_op jit(solution)/shard_map/cond/branch_1_fun/attn_fwd_bwd/pallas_call | solution.py:120
  518.4 19.0 %fusion.98 = f32[2048,1536]{1,0:T(8,128)} fusion(bf16[2048,2048]{1,0:T(8,128)(2,1)} %get-tuple-element.117, bf16[2048,1536]{1,0:T(8,128)(2,1)} %get-tuple-element.112), kind=kOutput, calls=%fused_computation.227 | convolution fusion | flops 12884901888 | bytes 27262976 | tf_op jit(solution)/shard_map/cond/branch_1_fun/dot_general | solution.py:156
  538.8 19.4 %fusion.99.q_ref.k_ref.v_ref = f32[2048,1536]{1,0:T(8,128)} fusion(bf16[2048,2048]{1,0:T(8,128)(2,1)} %get-tuple-element.117, bf16[2048,1536]{1,0:T(8,128)(2,1)} %all-gather.32.cloned.1.call-done), kind=kOutput, calls=%fused_computation.228 | convolution fusion | flops 12884901888 | bytes 27262976 | tf_op jit(solution)/shard_map/cond/branch_1_fun/dot_general | solution.py:30
  558.2 34.3 %attn_fwd_bwd.14 = (bf16[2048,512]{1,0:T(8,128)(2,1)}, bf16[2048,1536]{1,0:T(8,128)(2,1)}, f32[2,8,1536]{2,1,0:T(8,128)}) custom-call(f32[2048,1536]{1,0:T(8,128)} %fusion.99.q_ref.k_ref.v_ref, f32[2048,1536]{1,0:T(8,128)} %fusion.99.q_ref.k_ref.v_ref, f32[2048,1536]{1,0:T(8,128)} %fusion.99.q_ref.k_ref.v_ref, ...), custom_call_target="tpu_custom_call" | custom-call | flops 12884901888 | bytes 23068672 | tf_op jit(solution)/shard_map/cond/branch_1_fun/attn_fwd_bwd/pallas_call | solution.py:120
  592.5 19.0 %fusion.100 = f32[2048,1536]{1,0:T(8,128)} fusion(bf16[2048,2048]{1,0:T(8,128)(2,1)} %get-tuple-element.117, bf16[2048,1536]{1,0:T(8,128)(2,1)} %get-tuple-element.116), kind=kOutput, calls=%fused_computation.229 | convolution fusion | flops 12884901888 | bytes 27262976 | tf_op jit(solution)/shard_map/cond/branch_1_fun/dot_general | solution.py:156
  612.8 19.6 %fusion.101.q_ref.k_ref.v_ref = f32[2048,1536]{1,0:T(8,128)} fusion(bf16[2048,2048]{1,0:T(8,128)(2,1)} %get-tuple-element.117, bf16[2048,1536]{1,0:T(8,128)(2,1)} %all-gather.34.cloned.1.call-done), kind=kOutput, calls=%fused_computation.230 | convolution fusion | flops 12884901888 | bytes 27262976 | tf_op jit(solution)/shard_map/cond/branch_1_fun/dot_general | solution.py:30
  632.4 34.4 %attn_fwd_bwd.15 = (bf16[2048,512]{1,0:T(8,128)(2,1)}, bf16[2048,1536]{1,0:T(8,128)(2,1)}, f32[2,8,1536]{2,1,0:T(8,128)}) custom-call(f32[2048,1536]{1,0:T(8,128)} %fusion.101.q_ref.k_ref.v_ref, f32[2048,1536]{1,0:T(8,128)} %fusion.101.q_ref.k_ref.v_ref, f32[2048,1536]{1,0:T(8,128)} %fusion.101.q_ref.k_ref.v_ref, ...), custom_call_target="tpu_custom_call" | custom-call | flops 12884901888 | bytes 23068672 | tf_op jit(solution)/shard_map/cond/branch_1_fun/attn_fwd_bwd/pallas_call | solution.py:120
  666.8 19.0 %fusion.105 = f32[2048,1536]{1,0:T(8,128)} fusion(bf16[2048,2048]{1,0:T(8,128)(2,1)} %get-tuple-element.117, bf16[2048,1536]{1,0:T(8,128)(2,1)} %get-tuple-element.125), kind=kOutput, calls=%fused_computation.234 | convolution fusion | flops 12884901888 | bytes 27262976 | tf_op jit(solution)/shard_map/cond/branch_1_fun/dot_general | solution.py:156
  688.0 2.2 constant_dynamic-update-slice_fusion.2
  691.0 3.6 copy-done.15
  694.5 21.1 %fusion.106 = f32[2048,2048]{1,0:T(8,128)} fusion(bf16[2048,2048]{1,0:T(8,128)(2,1)S(1)} %constant_dynamic-update-slice_fusion, bf16[2048,2048]{1,0:T(8,128)(2,1)S(1)} %bitcast.185), kind=kOutput, calls=%fused_computation.235 | convolution fusion | flops 17179869184 | bytes 33554432 | tf_op jit(solution)/shard_map/cond/branch_1_fun/dot_general | solution.py:163
  715.7 19.6 %fusion.102 = f32[2048,2048]{1,0:T(8,128)} fusion(bf16[2048,1536]{1,0:T(8,128)(2,1)} %get-tuple-element.108, bf16[2048,1536]{1,0:T(8,128)(2,1)} %all-gather.26.cloned.1.call-done), kind=kOutput, calls=%fused_computation.231 | convolution fusion | flops 12884901888 | bytes 29360128 | tf_op jit(solution)/shard_map/cond/branch_1_fun/dot_general | solution.py:34
  735.4 17.8 %fusion.103 = f32[2048,2048]{1,0:T(8,128)} fusion(bf16[2048,1536]{1,0:T(8,128)(2,1)} %get-tuple-element.112, bf16[2048,1536]{1,0:T(8,128)(2,1)S(1)} %bitcast.246), kind=kOutput, calls=%fused_computation.232 | convolution fusion | flops 12884901888 | bytes 29360128 | tf_op jit(solution)/shard_map/cond/branch_1_fun/dot_general | solution.py:34
  753.3 16.4 %fusion.104 = f32[2048,2048]{1,0:T(8,128)} fusion(bf16[2048,1536]{1,0:T(8,128)(2,1)S(1)} %bitcast.254, bf16[2048,1536]{1,0:T(8,128)(2,1)S(1)} %bitcast.248), kind=kOutput, calls=%fused_computation.233 | convolution fusion | flops 12884901888 | bytes 29360128 | tf_op jit(solution)/shard_map/cond/branch_1_fun/dot_general | solution.py:34
  769.6 32.7 %fusion.8 = (f32[2048]{0:T(1024)S(1)}, f32[2048]{0:T(1024)S(1)}, f32[2048,2048]{1,0:T(8,128)}) fusion(bf16[2048,2048]{1,0:T(8,128)(2,1)} %get-tuple-element.96, f32[2048]{0:T(1024)S(1)} %reduce.9, f32[2048]{0:T(1024)S(1)} %bitcast.205, bf16[2048,1536]{1,0:T(8,128)(2,1)} %get-tuple-element.125, bf16[2048,1536]{1,0:T(8,128)(2,1)} %all-gather.34.cloned.1.call-done, ...), kind=kOutput, calls=%fused_computation.13 | convolution fusion | flops 12926840832 | bytes 88113152 | tf_op jit(solution)/shard_map/cond/branch_1_fun/dot_general | solution.py:34
  802.4 17.2 %fusion.7.mine_ref.rows_ref = f32[2048,2048]{1,0:T(8,128)} fusion(bf16[2048,2048]{1,0:T(8,128)(2,1)} %get-tuple-element.96, f32[2048,2048]{1,0:T(8,128)} %get-tuple-element.324, f32[2048]{0:T(1024)S(1)} %broadcast_multiply_fusion, f32[2048]{0:T(1024)S(1)} %bitcast.206, f32[2048]{0:T(1024)S(1)} %reduce.9, bf16[2,1024,2048]{2,1,0:T(8,128)(2,1)} %get-tuple-element.106), kind=kLoop, calls=%fused_computation.12 | loop fusion | flops 33554432 | bytes 50356224 | tf_op jit(solution)/shard_map/cond/branch_1_fun/add | solution.py:170
  820.7 5.8 sort.64
  831.6 5.0 sort.61
  841.9 17.6 %take_rows.1 = (bf16[1408,2048]{1,0:T(8,128)(2,1)}, f32[192,2048]{1,0:T(8,128)}) custom-call(s32[1408]{0:T(1024)} %reshape.279.idx_ref, s32[192]{0:T(256)} %reshape.280.idx2_ref, f32[2048,2048]{1,0:T(8,128)} %fusion.7.mine_ref.rows_ref), custom_call_target="tpu_custom_call" | custom-call | tf_op jit(solution)/shard_map/cond/branch_1_fun/take_rows/pallas_call | solution.py:371
  859.5 24.8 %fusion.9 = bf16[2048,2048]{1,0:T(8,128)(2,1)} fusion(bf16[2048,2048]{1,0:T(8,128)(2,1)} %get-tuple-element.96, bf16[2048,2048]{1,0:T(8,128)(2,1)} %copy-done.15, bf16[2048,2048]{1,0:T(8,128)(2,1)} %all-gather.28.cloned.1.call-done), kind=kOutput, calls=%fused_computation.14 | convolution fusion | flops 17192452096 | bytes 33554432 | tf_op jit(solution)/shard_map/cond/branch_1_fun/dot_general | solution.py:30
  884.3 34.5 %hot_seg_sum.1.part_ref = f32[2048,2048]{1,0:T(8,128)} custom-call(s32[4096]{0:T(1024)} %copy-done.25, s32[17]{0:T(128)} %convert_reduce_fusion.off_ref, f32[2048,2048]{1,0:T(8,128)} %fusion.7.mine_ref.rows_ref, f32[2048,2048]{1,0:T(8,128)} %collective-permute-done.mate_ref), custom_call_target="tpu_custom_call" | custom-call | tf_op jit(solution)/shard_map/cond/branch_1_fun/hot_seg_sum/pallas_call | solution.py:420
  918.8 351.1 %grad_exchange.1 = (f32[4096,2048]{1,0:T(8,128)}, bf16[8,176,2048]{2,1,0:T(8,128)(2,1)}, f32[8,24,2048]{2,1,0:T(8,128)}, f32[8,8,256]{2,1,0:T(8,128)}) custom-call(f32[2048,2048]{1,0:T(8,128)} %hot_seg_sum.1.part_ref, bf16[8,176,2048]{2,1,0:T(8,128)(2,1)} %bitcast.190, f32[8,24,2048]{2,1,0:T(8,128)} %bitcast.194, f32[8,8,256]{2,1,0:T(8,128)} %pad.13.vec_ref), custom_call_target="tpu_custom_call" | custom-call | tf_op jit(solution)/shard_map/cond/branch_1_fun/grad_exchange/pallas_call | solution.py:557
  1270.8 54.3 %build_table.1 = bf16[18992,2048]{1,0:T(8,128)(2,1)} custom-call(s32[1600]{0:T(1024)} %copy-done.27, s32[39]{0:T(128)} %convert_reduce_fusion.1.off_ref, s32[1]{0:T(128)} %bitcast.43.n_hot_ref, bf16[1408,2048]{1,0:T(8,128)(2,1)} %bitcast.188, f32[192,2048]{1,0:T(8,128)} %bitcast.193, f32[4096,2048]{1,0:T(8,128)} %get-tuple-element.134.hot_ref), custom_call_target="tpu_custom_call" | custom-call | tf_op jit(solution)/shard_map/cond/branch_1_fun/build_table/pallas_call | solution.py:614
  1325.7 1.5 fusion.73
  1327.2 2.3 fusion.74
  1329.5 2.4 fusion.75
  1333.4 2.7 pad_maximum_fusion.2
  1336.2 2.5 pad_maximum_fusion.1
  1338.7 1.5 pad_maximum_fusion
  (221 shorter events, 42.1 us)
Async XLA Ops:
  8.0 39.5 %sort.106.cloned.1.call-start = ((), (), s32[]{:S(2)}) async-start(), calls=%async_computation.39 | async-start | bytes 196640 | tf_op jit(solution)/shard_map/sort | solution.py:664
  55.0 218.8 %copy-start.10 = (s32[8,2048]{1,0:T(8,128)}, s32[8,2048]{1,0:T(8,128)S(1)}, u32[]{:S(2)}) copy-start(s32[8,2048]{1,0:T(8,128)S(1)} %get-tuple-element.120) | copy-start | bytes 196612 | tf_op jit(solution)/shard_map/cond
  55.0 4.8 copy-start.37
  55.0 4.9 copy-start.39
  55.0 4.9 copy-start.41
  55.1 4.9 copy-start.43
  55.1 4.9 copy-start.19
  55.1 246.9 %all-gather.26.cloned.1.call-start = ((), (), s32[]{:S(2)}) async-start(), calls=%async_computation.25 | async-start | bytes 7077888 | tf_op jit(solution)/shard_map/cond/branch_1_fun/all_gather | solution.py:770
  59.0 327.9 %all-gather.28.cloned.1.call-start = ((), (), s32[]{:S(2)}) async-start(), calls=%async_computation.26 | async-start | bytes 9437184 | tf_op jit(solution)/shard_map/cond/branch_1_fun/all_gather | solution.py:770
  113.1 160.0 %copy-start.17 = (pred[8,2048]{1,0:T(8,128)(4,1)S(1)}, pred[8,2048]{1,0:T(8,128)(4,1)}, u32[]{:S(2)}) copy-start(pred[8,2048]{1,0:T(8,128)(4,1)} %get-tuple-element.121) | copy-start | bytes 49156 | tf_op jit(solution)/shard_map/cond
  268.4 9.7 copy-start.26
  268.4 12.9 copy-start.13
  271.2 193.6 %all-gather.30.cloned.1.call-start = ((), (), s32[]{:S(2)}) async-start(), calls=%async_computation.27 | async-start | bytes 7077888 | tf_op jit(solution)/shard_map/cond/branch_1_fun/all_gather | solution.py:770
  271.8 267.0 %all-gather.32.cloned.1.call-start = ((), (), s32[]{:S(2)}) async-start(), calls=%async_computation.28 | async-start | bytes 7077888 | tf_op jit(solution)/shard_map/cond/branch_1_fun/all_gather | solution.py:770
  272.4 340.4 %all-gather.34.cloned.1.call-start = ((), (), s32[]{:S(2)}) async-start(), calls=%async_computation.29 | async-start | bytes 7077888 | tf_op jit(solution)/shard_map/cond/branch_1_fun/all_gather | solution.py:770
  273.0 554.3 %sort.98.cloned.1.call-start = ((), (), s32[]{:S(2)}) async-start(), calls=%async_computation.35 | async-start | bytes 196640 | tf_op jit(solution)/shard_map/cond/branch_1_fun/sort | solution.py:664
  273.7 554.3 %sort.100.cloned.1.call-start = ((), (), s32[]{:S(2)}) async-start(), calls=%async_computation.36 | async-start | bytes 196640 | tf_op jit(solution)/shard_map/cond/branch_1_fun/sort | solution.py:664
  274.5 554.4 %sort.104.cloned.1.call-start = ((), (), s32[]{:S(2)}) async-start(), calls=%async_computation.38 | async-start | bytes 196640 | tf_op jit(solution)/shard_map/cond/branch_1_fun/sort | solution.py:664
  275.3 554.9 %sort.102.cloned.1.call-start = ((), (), s32[]{:S(2)}) async-start(), calls=%async_computation.37 | async-start | bytes 196640 | tf_op jit(solution)/shard_map/cond/branch_1_fun/sort | solution.py:664
  276.0 1049.7 %reduce-scatter.27.cloned.1.call-start = ((), (), s32[]{:S(2)}) async-start(), calls=%async_computation.30 | async-start | bytes 14155776 | tf_op jit(solution)/shard_map/cond/branch_1_fun/reduce_scatter | solution.py:773
  464.2 863.0 %reduce-scatter.29.cloned.1.call-start = ((), (), s32[]{:S(2)}) async-start(), calls=%async_computation.31 | async-start | bytes 14155776 | tf_op jit(solution)/shard_map/cond/branch_1_fun/reduce_scatter | solution.py:773
  537.5 0.7 copy-start.33
  537.5 0.7 copy-start.34
  537.5 0.7 copy-start.35
  537.5 792.0 %reduce-scatter.31.cloned.1.call-start = ((), (), s32[]{:S(2)}) async-start(), calls=%async_computation.32 | async-start | bytes 14155776 | tf_op jit(solution)/shard_map/cond/branch_1_fun/reduce_scatter | solution.py:773
  611.5 0.7 copy-start.30
  611.5 0.7 copy-start.31
  611.5 0.7 copy-start.32
  611.5 720.5 %reduce-scatter.33.cloned.1.call-start = ((), (), s32[]{:S(2)}) async-start(), calls=%async_computation.33 | async-start | bytes 14155776 | tf_op jit(solution)/shard_map/cond/branch_1_fun/reduce_scatter | solution.py:773
  685.8 1.2 copy-start.11
  685.8 1.9 copy-start.6
  685.8 654.4 %reduce-scatter.35.cloned.1.call-start = ((), (), s32[]{:S(2)}) async-start(), calls=%async_computation.34 | async-start | bytes 18874368 | tf_op jit(solution)/shard_map/cond/branch_1_fun/reduce_scatter | solution.py:773
  687.4 2.9 copy-start.7
  687.4 3.2 copy-start.8
  687.7 6.8 slice-start.2
  690.3 4.3 slice-start.3
  691.0 3.6 copy-start.15
  715.7 19.7 %slice-start.4 = ((s8[6291456]{0:T(1024)(128)(4,1)}), s8[2097152]{0:T(1024)(128)(4,1)S(1)}, s32[]{:S(2)}) async-start(s8[6291456]{0:T(1024)(128)(4,1)} %bitcast.245), calls=%async_computation.49 | async-start | bytes 4194304 | tf_op jit(solution)/shard_map/cond
  715.7 19.7 %slice-start.5 = ((s8[6291456]{0:T(1024)(128)(4,1)}), s8[4194304]{0:T(1024)(128)(4,1)S(1)}, s32[]{:S(2)}) async-start(s8[6291456]{0:T(1024)(128)(4,1)} %bitcast.245), calls=%async_computation.50 | async-start | bytes 8388608 | tf_op jit(solution)/shard_map/cond
  715.7 37.5 %slice-start.6 = ((s8[6291456]{0:T(1024)(128)(4,1)}), s8[4194304]{0:T(1024)(128)(4,1)S(1)}, s32[]{:S(2)}) async-start(s8[6291456]{0:T(1024)(128)(4,1)} %bitcast.247), calls=%async_computation.51 | async-start | bytes 8388608 | tf_op jit(solution)/shard_map/cond
  715.7 37.5 %slice-start.10 = ((s8[6291456]{0:T(1024)(128)(4,1)}), s8[4194304]{0:T(1024)(128)(4,1)S(1)}, s32[]{:S(2)}) async-start(s8[6291456]{0:T(1024)(128)(4,1)} %bitcast.253), calls=%async_computation.55 | async-start | bytes 8388608 | tf_op jit(solution)/shard_map/cond
  735.4 17.8 %slice-start.7 = ((s8[6291456]{0:T(1024)(128)(4,1)}), s8[2097152]{0:T(1024)(128)(4,1)S(1)}, s32[]{:S(2)}) async-start(s8[6291456]{0:T(1024)(128)(4,1)} %bitcast.247), calls=%async_computation.52 | async-start | bytes 4194304 | tf_op jit(solution)/shard_map/cond
  735.4 17.8 %slice-start.11 = ((s8[6291456]{0:T(1024)(128)(4,1)}), s8[2097152]{0:T(1024)(128)(4,1)S(1)}, s32[]{:S(2)}) async-start(s8[6291456]{0:T(1024)(128)(4,1)} %bitcast.253), calls=%async_computation.56 | async-start | bytes 4194304 | tf_op jit(solution)/shard_map/cond
  753.2 16.4 %copy-start.24 = (f32[1,8,256]{2,0,1:T(1,128)S(1)}, f32[1,8,256]{2,0,1:T(1,128)}, u32[]{:S(2)}) copy-start(f32[1,8,256]{2,0,1:T(1,128)} %slice.340) | copy-start | bytes 24580 | tf_op jit(solution)/shard_map/cond
  802.4 18.3 %copy-start.28 = (s32[1,8,2,128]{3,1,2,0:T(8,128)S(1)}, s32[1,8,2,128]{3,1,2,0:T(8,128)}, u32[]{:S(2)}) copy-start(s32[1,8,2,128]{3,1,2,0:T(8,128)} %copy.68) | copy-start | bytes 24580 | tf_op jit(solution)/shard_map/cond
  819.6 64.7 %collective-permute-start = (f32[2048,2048]{1,0:T(8,128)}, f32[2048,2048]{1,0:T(8,128)}, u32[]{:S(2)}, u32[]{:S(2)}) collective-permute-start(f32[2048,2048]{1,0:T(8,128)} %fusion.7.mine_ref.rows_ref), channel_id=1, source_target_pairs={{0,1},{1,0},{2,3},{3,2},{4,5},{5,4},{6,7},{7,6}} | collective-permute-start | bytes 50331656 | tf_op jit(solution)/shard_map/cond/branch_1_fun/ppermute | solution.py:716
  826.5 33.0 %copy-start.25 = (s32[4096]{0:T(1024)}, s32[4096]{0:T(1024)S(1)}, u32[]{:S(2)}) copy-start(s32[4096]{0:T(1024)S(1)} %get-tuple-element.123.key_ref) | copy-start | bytes 49156 | tf_op jit(solution)/shard_map/cond
  836.6 22.8 %copy-start.27 = (s32[1600]{0:T(1024)}, s32[1600]{0:T(1024)S(1)}, u32[]{:S(2)}) copy-start(s32[1600]{0:T(1024)S(1)} %get-tuple-element.122.key_ref) | copy-start | bytes 19204 | tf_op jit(solution)/shard_map/cond
  (2 other events, 1.2 us)
Sparse Core Ops, SparseCore 0:
  23.5 7.5 sort.116.cloned.1.call-done
  59.1 39.5 all-gather.25
  271.3 115.5 all-gather.27
  389.1 39.5 all-gather.29
  430.9 39.5 all-gather.31
  472.8 39.5 all-gather.33
  515.8 82.4 reduce-scatter.26
  601.7 82.4 reduce-scatter.28
  687.7 82.4 reduce-scatter.30
  773.5 82.5 reduce-scatter.32
  860.2 147.7 reduce-scatter.34
  (1 shorter events, 0.0 us)
Sparse Core Ops, SparseCore 1:
  275.9 7.5 sort.108.cloned.1.call-done
  286.0 7.5 sort.110.cloned.1.call-done
  296.1 7.5 sort.114.cloned.1.call-done
  306.4 7.5 sort.112.cloned.1.call-done
  (4 shorter events, 0.0 us)

commit v4 on v3

--- a/solution.py
+++ b/solution.py
@@ -179,6 +179,7 @@
 
 
 LOOK_CHUNK = 64
+LOOK_LAG = 4
 LOOK_N = HOT // 2 // LOOK_CHUNK
 
 
@@ -229,7 +230,7 @@
 
     def stage(step, carry):
         for part in range(2):
-            k = step - place[part]
+            k = step - LOOK_LAG * place[part]
             live = (k >= 0) & (k < LOOK_N)
 
             @pl.when(live & (me != 0))
@@ -252,7 +253,7 @@
     for step in range(1, N_DEV):
         vec_copy(step).start()
     pl.when(me != 0)(start_cold)
-    lax.fori_loop(0, LOOK_N + 3, stage, 0)
+    lax.fori_loop(0, LOOK_N + 3 * LOOK_LAG, stage, 0)
     pl.when(me == 0)(start_cold)
 
     def drain(k, carry):
@@ -661,18 +662,24 @@
 
 
 def first_of(mask, values, count):
-    return lax.sort(jnp.where(mask, values, BIG), dimension=1)[:, :count]
+    return lax.sort(jnp.where(mask, values, BIG), dimension=1, is_stable=False)[:, :count]
+
+
+def sort_rows(keys):
+    keys = jnp.pad(keys, (0, max(0, 2048 - keys.shape[0])), constant_values=BIG)
+    fill = jnp.full((7,) + keys.shape, BIG, jnp.int32)
+    return lax.sort(jnp.concatenate([keys[None], fill]), dimension=1, is_stable=False)[0]
 
 
 def repeats(all_ids):
     flat = all_ids.reshape(-1).astype(jnp.uint32)
     pos = jnp.arange(flat.shape[0], dtype=jnp.uint32)
-    ordered = lax.sort(flat * jnp.uint32(16384) + pos)
+    ordered = lax.sort(flat * jnp.uint32(16384) + pos, is_stable=False)
     ident = ordered // jnp.uint32(16384)
     same = ident[1:] == ident[:-1]
     no = jnp.zeros((1,), jnp.bool_)
     again = jnp.concatenate([no, same]) | jnp.concatenate([same, no])
-    again = lax.sort((ordered % jnp.uint32(16384)) * jnp.uint32(2) + again.astype(jnp.uint32)) % jnp.uint32(2)
+    again = lax.sort((ordered % jnp.uint32(16384)) * jnp.uint32(2) + again.astype(jnp.uint32), is_stable=False) % jnp.uint32(2)
     return (again == 1).reshape(all_ids.shape)
 
 
@@ -696,12 +703,18 @@
         where = jnp.bitwise_and(lax.shift_right_logical(packed, 1), 32767)
         return jnp.where((packed != BIG) & (jnp.bitwise_and(packed, 1) == wanted), where * 2048 + slot, BIG).reshape(-1)
 
-    owner_keys = lax.sort(jnp.concatenate([owner_key(row, slots, 0), owner_key(more_row, more_slots, 1)]))
+    owner_keys = sort_rows(jnp.concatenate([owner_key(row, slots, 0), owner_key(more_row, more_slots, 1)]))
+    mate_ids = lax.dynamic_index_in_dim(all_ids, jnp.bitwise_xor(me, 1), 0, keepdims=False)
+    pair_ids = jnp.concatenate([own_ids, mate_ids])
+    base = (me % 2) * (HOT // 2)
+    inside = (pair_ids >= base) & (pair_ids < base + HOT // 2)
+    hot_keys = jnp.where(inside, (pair_ids - base) * 4096 + jnp.arange(2 * tokens, dtype=jnp.int32), BIG)
+    hot_keys = sort_rows(hot_keys)
 
     def clean(tok):
         return jnp.where(tok == BIG, 0, tok).reshape(-1)
 
-    return clean(slot_tok), clean(more_tok), owner_keys
+    return clean(slot_tok), clean(more_tok), owner_keys, hot_keys
 
 
 def block_offsets(keys, n_blocks, block, shift):
@@ -709,17 +722,11 @@
     return jnp.sum(keys[None, :] < edges[:, None], axis=1).astype(jnp.int32)
 
 
-def fast_table_grad(rows_dev, all_ids, own_ids, d_x, vecs, slot_tok, more_tok, owner_keys):
+def fast_table_grad(rows_dev, d_x, vecs, slot_tok, more_tok, owner_keys, keys):
     tokens, width = d_x.shape
     me = lax.axis_index(AXIS)
     mate_of = [(i, i ^ 1) for i in range(N_DEV)]
     dx_mate = lax.ppermute(d_x, AXIS, mate_of)
-    mate_ids = lax.dynamic_index_in_dim(all_ids, jnp.bitwise_xor(me, 1), 0, keepdims=False)
-    pair_ids = jnp.concatenate([own_ids, mate_ids])
-    base = (me % 2) * (HOT // 2)
-    inside = (pair_ids >= base) & (pair_ids < base + HOT // 2)
-    keys = jnp.where(inside, (pair_ids - base) * 4096 + jnp.arange(2 * tokens, dtype=jnp.int32), BIG)
-    keys = lax.sort(keys)
     part = seg_sum(keys, block_offsets(keys, HOT // 2 // ROW_BLOCK, ROW_BLOCK, 12), d_x, dx_mate, HOT // 2)
     cold, more = take2d(slot_tok, more_tok, d_x, N_DEV)
     cold = cold.reshape(N_DEV, CAP, width)
@@ -798,9 +805,8 @@
         grad_bias = grad_bias.reshape(GROUPS, 3, group)
         vecs = jnp.stack([grad_gain] + [grad_bias[:, j].reshape(-1) for j in range(3)])
         vecs = jnp.pad(vecs.reshape(4, N_DEV, part_w).transpose(1, 0, 2), ((0, 0), (0, 4), (0, 0)))
-        rest = (all_ids, own_ids, d_x, vecs)
         if fast:
-            grad_part, vec_sum = fast_table_grad(rows_dev, *rest, *grad_plan(*plan_ids, me, rows_dev))
+            grad_part, vec_sum = fast_table_grad(rows_dev, d_x, vecs, *grad_plan(*plan_ids, me, rows_dev))
         else:
             grad_part, vec_sum = slow_table_grad(rows_dev, all_ids, d_x, vecs)
         return (block_out.reshape(grad_out.shape), grad_part, vec_sum[0], gq, vec_sum[1], gk, vec_sum[2], gv, vec_sum[3], grad_wo)

time: 1360 us -> 1360 us (level)
  local copies, waits for them, and re-layouts: 82.7 us -> 99.5 us
  waiting for transfers between devices: 67.4 us -> 51.1 us
  other arithmetic: 77.5 us -> 63.3 us
    all_gather x5, waiting for transfers between devices: 65.7 us -> 48.6 us  [whole(): return lax.all_gather(part, AXIS, axis=0, tiled=True)]
    cond x75 -> x69, local copies, waits for them, and re-layouts: 34.3 us -> 47.2 us
  transfers between devices with their start and end apart: 11 -> 11, of which waited for: 1 -> 2; matrix products, arithmetic and copies ran while one was open for 32% -> 27% of each run, Pallas kernels for 57% -> 46%
where the time goes in v4:
time: 1360 us; the launch traced here: 1350 us
  Pallas kernels  781 us (57%)
  matrix products  310 us (23%)
  local copies, waits for them, and re-layouts  99.5 us (7%)
  other arithmetic  63.3 us (5%)
  waiting for transfers between devices  51.1 us (4%)
  between operations  17.5 us (1%)
  blocking collectives  13.9 us (1%)
    pallas_call x1, Pallas kernels, grad_exchange(): pl.pallas_call(reduce_kernel, out_shape=[jax.ShapeDtypeStruct((HOT, width...  362 us
    pallas_call x1, Pallas kernels, lookup_exchange(): pl.pallas_call(lookup_kernel, out_shape=[jax.ShapeDtypeStruct(hot_rows.sh...  155 us
    pallas_call x4, Pallas kernels, attention(): pl.pallas_call(attn_kernel, grid=(n_seq, n_heads), in_specs=[*third, tile...  138 us
    dot_general x5, matrix products, dot_nt(): lax.dot_general(a, b, (((1,), (1,)), ((), ())), preferred_element_type=jn...  110 us
    dot_general x5, matrix products, dot_nn(): lax.dot_general(a, b, (((1,), (0,)), ((), ())), preferred_element_type=jn...  102 us
    dot_general x4, matrix products, block_fwd_bwd(): grad_w = lax.dot_general(hidden, d_lin, tn, preferred_element_type=f32)  76.4 us
    pallas_call x1, Pallas kernels, build_table(): pl.pallas_call(table_kernel, grid_spec=pltpu.PrefetchScalarGridSpec(num_s...  54.4 us
    all_gather x5, waiting for transfers between devices, whole(): return lax.all_gather(part, AXIS, axis=0, tiled=True)  48.6 us
  transfers between devices with their start and end apart: 11, of which 2 were waited for; matrix products, arithmetic and copies ran while one was open for 27% of the time, Pallas kernels for 46%

profile of v4, /device:TPU:0, one launch (start us, length us, event | category | flops | bytes accessed | tf_op | source)
XLA Modules:
  0.0 1345.6 jit_solution(2919995668288993040)
XLA Ops:
  8.8 13.9 %all-gather.1 = s32[8,1,2048]{2,1,0:T(1,128)S(1)} all-gather(s32[1,1,2048]{2,1,0:T(1,128)S(1)} %reshape.413), channel_id=1, replica_groups=mesh['fsdp'=8] {'fsdp'}, dimensions={0}, use_global_device_ids=true | all-gather | bytes 73728 | tf_op jit(solution)/shard_map/all_gather | solution.py:816
  25.0 6.3 sort.65
  31.5 6.3 sort.67
  38.4 2.3 reduce-window.6
  44.1 1293.5 %conditional.1 = (bf16[2,1024,2048]{2,1,0:T(8,128)(2,1)}, bf16[18992,2048]{1,0:T(8,128)(2,1)}, f32[256]{0:T(256)}, f32[256,2048]{1,0:T(8,128)}, f32[256]{0:T(256...) conditional(s32[]{:T(128)} %convert_element_type.88, ...), branch_computations={%region_10.26_spmd, %region_26.47_spmd} | conditional | flops 257974468608 | bytes 2525248768 | solution.py:826
  57.5 14.2 %slice_bitcast_fusion = bf16[512,8,16,128]{3,1,2,0:T(8,128)(2,1)} fusion(bf16[18992,2048]{1,0:T(8,128)(2,1)} %get-tuple-element.83), kind=kLoop, calls=%fused_computation.16 | loop fusion | bytes 33554432 | tf_op jit(solution)/shard_map/cond
  71.6 28.6 %gather_fusion.1 = bf16[1408,2048]{1,0:T(8,128)(2,1)} fusion(bf16[18992,2048]{1,0:T(8,128)(2,1)} %get-tuple-element.83, s32[2048]{0:T(1024)S(1)} %pad_clamp_fusion), kind=kCustom, calls=%fused_computation.1 | custom fusion | bytes 11539968 | tf_op jit(solution)/shard_map/cond/branch_1_fun/jit(_take)/gather | solution.py:655
  100.2 7.3 copy.53
  107.5 15.2 %copy.54 = bf16[512,8,16,128]{3,2,1,0:T(8,128)(2,1)} copy(bf16[512,8,16,128]{3,1,2,0:T(8,128)(2,1)} %slice_bitcast_fusion) | data formatting | bytes 33554432 | tf_op jit(solution)/shard_map/cond
  126.3 155.3 %lookup_exchange.1 = (bf16[4096,16,128]{2,1,0:T(8,128)(2,1)}, bf16[8,176,16,128]{3,2,1,0:T(8,128)(2,1)}, bf16[8,16,256]{2,1,0:T(8,128)(2,1)}) custom-call(bf16[8,176,16,128]{3,2,1,0:T(8,128)(2,1)} %bitcast.189, bf16[4096,16,128]{2,1,0:T(8,128)(2,1)} %bitcast.180, bf16[16,256]{1,0:T(8,128)(2,1)} %fusion.26.vec_ref), custom_call_target="tpu_custom_call", output_to_operand_aliasing={{0}: (1, {})} | custom-call | tf_op jit(solution)/shard_map/cond/branch_1_fun/lookup_exchange/pallas_call | solution.py:281
  289.1 2.0 fusion.12
  292.9 1.3 pad_maximum_fusion.7
  294.9 19.6 %pick_rows.1 = (bf16[2048,2048]{1,0:T(8,128)(2,1)}, bf16[2048,2048]{1,0:T(8,128)(2,1)}, f32[2048,1]{1,0:T(8,128)}) custom-call(s32[2048]{0:T(1024)} %compare_select_fusion.idx_ref, bf16[4096,16,128]{2,1,0:T(8,128)(2,1)} %get-tuple-element.89.hot_ref, bf16[1408,16,128]{2,1,0:T(8,128)(2,1)} %bitcast.192, f32[1,2048]{1,0:T(1,128)} %bitcast.209), custom_call_target="tpu_custom_call" | custom-call | tf_op jit(solution)/shard_map/cond/branch_1_fun/pick_rows/pallas_call | solution.py:333
  317.0 17.8 %all-gather.26.cloned.1.call-done = bf16[2048,1536]{1,0:T(8,128)(2,1)} async-done(((bf16[256,1536]{1,0:T(8,128)(2,1)}), bf16[2048,1536]{1,0:T(8,128)(2,1)}) %all-gather.26.cloned.1.call-update) | async-done | bytes 6291472 | tf_op jit(solution)/shard_map/cond/branch_1_fun/all_gather | solution.py:777
  334.8 19.2 %fusion.95.q_ref.k_ref.v_ref = f32[2048,1536]{1,0:T(8,128)} fusion(bf16[2048,2048]{1,0:T(8,128)(2,1)} %get-tuple-element.113, bf16[2048,1536]{1,0:T(8,128)(2,1)} %all-gather.26.cloned.1.call-done), kind=kOutput, calls=%fused_computation.224 | convolution fusion | flops 12884901888 | bytes 27262976 | tf_op jit(solution)/shard_map/cond/branch_1_fun/dot_general | solution.py:30
  354.0 30.8 %all-gather.28.cloned.1.call-done = bf16[2048,2048]{1,0:T(8,128)(2,1)} async-done(((bf16[256,2048]{1,0:T(8,128)(2,1)}), bf16[2048,2048]{1,0:T(8,128)(2,1)}) %all-gather.28.cloned.1.call-update) | async-done | bytes 8388624 | tf_op jit(solution)/shard_map/cond/branch_1_fun/all_gather | solution.py:777
  384.8 23.6 %convert_bitcast_fusion.do_ref = bf16[2048,2048]{1,0:T(8,128)(2,1)} fusion(bf16[2048,2048]{1,0:T(8,128)(2,1)} %all-gather.28.cloned.1.call-done, bf16[2048,2048]{1,0:T(8,128)(2,1)} %bitcast.185), kind=kOutput, calls=%fused_computation.17 | convolution fusion | flops 17184063488 | bytes 25165824 | tf_op jit(solution)/shard_map/cond/branch_1_fun/dot_general | solution.py:34
  408.4 34.5 %attn_fwd_bwd.12 = (bf16[2048,512]{1,0:T(8,128)(2,1)}, bf16[2048,1536]{1,0:T(8,128)(2,1)}, f32[2,8,1536]{2,1,0:T(8,128)}) custom-call(f32[2048,1536]{1,0:T(8,128)} %fusion.95.q_ref.k_ref.v_ref, f32[2048,1536]{1,0:T(8,128)} %fusion.95.q_ref.k_ref.v_ref, f32[2048,1536]{1,0:T(8,128)} %fusion.95.q_ref.k_ref.v_ref, ...), custom_call_target="tpu_custom_call" | custom-call | flops 12884901888 | bytes 23068672 | tf_op jit(solution)/shard_map/cond/branch_1_fun/attn_fwd_bwd/pallas_call | solution.py:120
  442.8 19.3 %fusion.96 = f32[2048,1536]{1,0:T(8,128)} fusion(bf16[2048,2048]{1,0:T(8,128)(2,1)} %get-tuple-element.113, bf16[2048,1536]{1,0:T(8,128)(2,1)} %get-tuple-element.104), kind=kOutput, calls=%fused_computation.225 | convolution fusion | flops 12884901888 | bytes 27262976 | tf_op jit(solution)/shard_map/cond/branch_1_fun/dot_general | solution.py:156
  462.9 19.2 %fusion.97.q_ref.k_ref.v_ref = f32[2048,1536]{1,0:T(8,128)} fusion(bf16[2048,2048]{1,0:T(8,128)(2,1)} %get-tuple-element.113, bf16[2048,1536]{1,0:T(8,128)(2,1)} %all-gather.30.cloned.1.call-done), kind=kOutput, calls=%fused_computation.226 | convolution fusion | flops 12884901888 | bytes 27262976 | tf_op jit(solution)/shard_map/cond/branch_1_fun/dot_general | solution.py:30
  482.1 34.3 %attn_fwd_bwd.13 = (bf16[2048,512]{1,0:T(8,128)(2,1)}, bf16[2048,1536]{1,0:T(8,128)(2,1)}, f32[2,8,1536]{2,1,0:T(8,128)}) custom-call(f32[2048,1536]{1,0:T(8,128)} %fusion.97.q_ref.k_ref.v_ref, f32[2048,1536]{1,0:T(8,128)} %fusion.97.q_ref.k_ref.v_ref, f32[2048,1536]{1,0:T(8,128)} %fusion.97.q_ref.k_ref.v_ref, ...), custom_call_target="tpu_custom_call" | custom-call | flops 12884901888 | bytes 23068672 | tf_op jit(solution)/shard_map/cond/branch_1_fun/attn_fwd_bwd/pallas_call | solution.py:120
  516.4 19.0 %fusion.98 = f32[2048,1536]{1,0:T(8,128)} fusion(bf16[2048,2048]{1,0:T(8,128)(2,1)} %get-tuple-element.113, bf16[2048,1536]{1,0:T(8,128)(2,1)} %get-tuple-element.108), kind=kOutput, calls=%fused_computation.227 | convolution fusion | flops 12884901888 | bytes 27262976 | tf_op jit(solution)/shard_map/cond/branch_1_fun/dot_general | solution.py:156
  536.7 19.6 %fusion.99.q_ref.k_ref.v_ref = f32[2048,1536]{1,0:T(8,128)} fusion(bf16[2048,2048]{1,0:T(8,128)(2,1)} %get-tuple-element.113, bf16[2048,1536]{1,0:T(8,128)(2,1)} %all-gather.32.cloned.1.call-done), kind=kOutput, calls=%fused_computation.228 | convolution fusion | flops 12884901888 | bytes 27262976 | tf_op jit(solution)/shard_map/cond/branch_1_fun/dot_general | solution.py:30
  556.4 34.3 %attn_fwd_bwd.14 = (bf16[2048,512]{1,0:T(8,128)(2,1)}, bf16[2048,1536]{1,0:T(8,128)(2,1)}, f32[2,8,1536]{2,1,0:T(8,128)}) custom-call(f32[2048,1536]{1,0:T(8,128)} %fusion.99.q_ref.k_ref.v_ref, f32[2048,1536]{1,0:T(8,128)} %fusion.99.q_ref.k_ref.v_ref, f32[2048,1536]{1,0:T(8,128)} %fusion.99.q_ref.k_ref.v_ref, ...), custom_call_target="tpu_custom_call" | custom-call | flops 12884901888 | bytes 23068672 | tf_op jit(solution)/shard_map/cond/branch_1_fun/attn_fwd_bwd/pallas_call | solution.py:120
  590.7 19.0 %fusion.100 = f32[2048,1536]{1,0:T(8,128)} fusion(bf16[2048,2048]{1,0:T(8,128)(2,1)} %get-tuple-element.113, bf16[2048,1536]{1,0:T(8,128)(2,1)} %get-tuple-element.112), kind=kOutput, calls=%fused_computation.229 | convolution fusion | flops 12884901888 | bytes 27262976 | tf_op jit(solution)/shard_map/cond/branch_1_fun/dot_general | solution.py:156
  611.0 19.4 %fusion.101.q_ref.k_ref.v_ref = f32[2048,1536]{1,0:T(8,128)} fusion(bf16[2048,2048]{1,0:T(8,128)(2,1)} %get-tuple-element.113, bf16[2048,1536]{1,0:T(8,128)(2,1)} %all-gather.34.cloned.1.call-done), kind=kOutput, calls=%fused_computation.230 | convolution fusion | flops 12884901888 | bytes 27262976 | tf_op jit(solution)/shard_map/cond/branch_1_fun/dot_general | solution.py:30
  630.4 34.4 %attn_fwd_bwd.15 = (bf16[2048,512]{1,0:T(8,128)(2,1)}, bf16[2048,1536]{1,0:T(8,128)(2,1)}, f32[2,8,1536]{2,1,0:T(8,128)}) custom-call(f32[2048,1536]{1,0:T(8,128)} %fusion.101.q_ref.k_ref.v_ref, f32[2048,1536]{1,0:T(8,128)} %fusion.101.q_ref.k_ref.v_ref, f32[2048,1536]{1,0:T(8,128)} %fusion.101.q_ref.k_ref.v_ref, ...), custom_call_target="tpu_custom_call" | custom-call | flops 12884901888 | bytes 23068672 | tf_op jit(solution)/shard_map/cond/branch_1_fun/attn_fwd_bwd/pallas_call | solution.py:120
  664.8 19.0 %fusion.105 = f32[2048,1536]{1,0:T(8,128)} fusion(bf16[2048,2048]{1,0:T(8,128)(2,1)} %get-tuple-element.113, bf16[2048,1536]{1,0:T(8,128)(2,1)} %get-tuple-element.120), kind=kOutput, calls=%fused_computation.234 | convolution fusion | flops 12884901888 | bytes 27262976 | tf_op jit(solution)/shard_map/cond/branch_1_fun/dot_general | solution.py:156
  686.0 2.2 constant_dynamic-update-slice_fusion.2
  689.0 3.6 copy-done.16
  692.5 21.2 %fusion.106 = f32[2048,2048]{1,0:T(8,128)} fusion(bf16[2048,2048]{1,0:T(8,128)(2,1)S(1)} %constant_dynamic-update-slice_fusion, bf16[2048,2048]{1,0:T(8,128)(2,1)S(1)} %bitcast.188), kind=kOutput, calls=%fused_computation.235 | convolution fusion | flops 17179869184 | bytes 33554432 | tf_op jit(solution)/shard_map/cond/branch_1_fun/dot_general | solution.py:163
  713.8 19.6 %fusion.102 = f32[2048,2048]{1,0:T(8,128)} fusion(bf16[2048,1536]{1,0:T(8,128)(2,1)} %get-tuple-element.104, bf16[2048,1536]{1,0:T(8,128)(2,1)} %all-gather.26.cloned.1.call-done), kind=kOutput, calls=%fused_computation.231 | convolution fusion | flops 12884901888 | bytes 29360128 | tf_op jit(solution)/shard_map/cond/branch_1_fun/dot_general | solution.py:34
  733.5 17.8 %fusion.103 = f32[2048,2048]{1,0:T(8,128)} fusion(bf16[2048,1536]{1,0:T(8,128)(2,1)} %get-tuple-element.108, bf16[2048,1536]{1,0:T(8,128)(2,1)S(1)} %bitcast.253), kind=kOutput, calls=%fused_computation.232 | convolution fusion | flops 12884901888 | bytes 29360128 | tf_op jit(solution)/shard_map/cond/branch_1_fun/dot_general | solution.py:34
  751.4 16.4 %fusion.104 = f32[2048,2048]{1,0:T(8,128)} fusion(bf16[2048,1536]{1,0:T(8,128)(2,1)S(1)} %bitcast.261, bf16[2048,1536]{1,0:T(8,128)(2,1)S(1)} %bitcast.255), kind=kOutput, calls=%fused_computation.233 | convolution fusion | flops 12884901888 | bytes 29360128 | tf_op jit(solution)/shard_map/cond/branch_1_fun/dot_general | solution.py:34
  767.8 32.7 %fusion.8 = (f32[2048]{0:T(1024)S(1)}, f32[2048]{0:T(1024)S(1)}, f32[2048,2048]{1,0:T(8,128)}) fusion(bf16[2048,2048]{1,0:T(8,128)(2,1)} %get-tuple-element.92, f32[2048]{0:T(1024)S(1)} %reduce.9, f32[2048]{0:T(1024)S(1)} %bitcast.210, bf16[2048,1536]{1,0:T(8,128)(2,1)} %get-tuple-element.120, bf16[2048,1536]{1,0:T(8,128)(2,1)} %all-gather.34.cloned.1.call-done, ...), kind=kOutput, calls=%fused_computation.13 | convolution fusion | flops 12926840832 | bytes 88113152 | tf_op jit(solution)/shard_map/cond/branch_1_fun/dot_general | solution.py:34
  800.5 17.2 %fusion.7.mine_ref.rows_ref = f32[2048,2048]{1,0:T(8,128)} fusion(bf16[2048,2048]{1,0:T(8,128)(2,1)} %get-tuple-element.92, f32[2048,2048]{1,0:T(8,128)} %get-tuple-element.315, f32[2048]{0:T(1024)S(1)} %broadcast_multiply_fusion, f32[2048]{0:T(1024)S(1)} %bitcast.211, f32[2048]{0:T(1024)S(1)} %reduce.9, bf16[2,1024,2048]{2,1,0:T(8,128)(2,1)} %get-tuple-element.102), kind=kLoop, calls=%fused_computation.12 | loop fusion | flops 33554432 | bytes 50356224 | tf_op jit(solution)/shard_map/cond/branch_1_fun/add | solution.py:170
  828.5 17.6 %take_rows.1 = (bf16[1408,2048]{1,0:T(8,128)(2,1)}, f32[192,2048]{1,0:T(8,128)}) custom-call(s32[1408]{0:T(1024)} %reshape.368.idx_ref, s32[192]{0:T(256)} %reshape.369.idx2_ref, f32[2048,2048]{1,0:T(8,128)} %fusion.7.mine_ref.rows_ref), custom_call_target="tpu_custom_call" | custom-call | tf_op jit(solution)/shard_map/cond/branch_1_fun/take_rows/pallas_call | solution.py:372
  846.1 24.6 %fusion.9 = bf16[2048,2048]{1,0:T(8,128)(2,1)} fusion(bf16[2048,2048]{1,0:T(8,128)(2,1)} %get-tuple-element.92, bf16[2048,2048]{1,0:T(8,128)(2,1)} %copy-done.16, bf16[2048,2048]{1,0:T(8,128)(2,1)} %all-gather.28.cloned.1.call-done), kind=kOutput, calls=%fused_computation.14 | convolution fusion | flops 17192452096 | bytes 33554432 | tf_op jit(solution)/shard_map/cond/branch_1_fun/dot_general | solution.py:30
  870.7 34.4 %hot_seg_sum.1.part_ref = f32[2048,2048]{1,0:T(8,128)} custom-call(s32[4096]{0:T(1024)} %bitcast.205, s32[17]{0:T(128)} %convert_reduce_fusion.off_ref, f32[2048,2048]{1,0:T(8,128)} %fusion.7.mine_ref.rows_ref, f32[2048,2048]{1,0:T(8,128)} %collective-permute-done.mate_ref), custom_call_target="tpu_custom_call" | custom-call | tf_op jit(solution)/shard_map/cond/branch_1_fun/hot_seg_sum/pallas_call | solution.py:421
  905.1 361.9 %grad_exchange.1 = (f32[4096,2048]{1,0:T(8,128)}, bf16[8,176,2048]{2,1,0:T(8,128)(2,1)}, f32[8,24,2048]{2,1,0:T(8,128)}, f32[8,8,256]{2,1,0:T(8,128)}) custom-call(f32[2048,2048]{1,0:T(8,128)} %hot_seg_sum.1.part_ref, bf16[8,176,2048]{2,1,0:T(8,128)(2,1)} %bitcast.193, f32[8,24,2048]{2,1,0:T(8,128)} %bitcast.197, f32[8,8,256]{2,1,0:T(8,128)} %pad.19.vec_ref), custom_call_target="tpu_custom_call" | custom-call | tf_op jit(solution)/shard_map/cond/branch_1_fun/grad_exchange/pallas_call | solution.py:558
  1267.8 54.4 %build_table.1 = bf16[18992,2048]{1,0:T(8,128)(2,1)} custom-call(s32[2048]{0:T(1024)} %bitcast.213, s32[39]{0:T(128)} %convert_reduce_fusion.1.off_ref, s32[1]{0:T(128)} %bitcast.45.n_hot_ref, bf16[1408,2048]{1,0:T(8,128)(2,1)} %bitcast.191, f32[192,2048]{1,0:T(8,128)} %bitcast.196, f32[4096,2048]{1,0:T(8,128)} %get-tuple-element.129.hot_ref), custom_call_target="tpu_custom_call" | custom-call | tf_op jit(solution)/shard_map/cond/branch_1_fun/build_table/pallas_call | solution.py:615
  1322.8 1.5 fusion.73
  1324.3 2.3 fusion.74
  1326.6 2.4 fusion.75
  1329.0 1.5 fusion.76
  1330.5 2.7 pad_maximum_fusion.2
  1333.2 2.5 pad_maximum_fusion.1
  1335.8 1.5 pad_maximum_fusion
  (218 shorter events, 45.4 us)
Async XLA Ops:
  8.0 36.1 %sort.84.cloned.1.call-start = ((), (), s32[]{:S(2)}) async-start(), calls=%async_computation.41 | async-start | bytes 196640 | tf_op jit(solution)/shard_map/sort | solution.py:665
  37.8 0.6 copy-start.17
  40.7 0.6 copy-start.13
  52.0 262.6 %sort.72.cloned.1.call-start = ((), (), s32[]{:S(2)}) async-start(), calls=%async_computation.35 | async-start | bytes 196640 | tf_op jit(solution)/shard_map/cond/branch_1_fun/sort | solution.py:665
  107.5 15.2 %copy-start.2 = (bf16[256,2048]{1,0:T(8,128)(2,1)S(1)}, bf16[256,2048]{1,0:T(8,128)(2,1)}, u32[]{:S(2)}) copy-start(bf16[256,2048]{1,0:T(8,128)(2,1)} %get-tuple-element.94) | copy-start | bytes 3145732 | tf_op jit(solution)/shard_map/cond
  107.5 15.2 %copy-start.4 = (bf16[256,2048]{1,0:T(8,128)(2,1)S(1)}, bf16[256,2048]{1,0:T(8,128)(2,1)}, u32[]{:S(2)}) copy-start(bf16[256,2048]{1,0:T(8,128)(2,1)} %get-tuple-element.95) | copy-start | bytes 3145732 | tf_op jit(solution)/shard_map/cond
  126.3 155.4 %copy-start.18 = (pred[8,2048]{1,0:T(8,128)(4,1)S(1)}, pred[8,2048]{1,0:T(8,128)(4,1)}, u32[]{:S(2)}) copy-start(pred[8,2048]{1,0:T(8,128)(4,1)} %get-tuple-element.117) | copy-start | bytes 49156 | tf_op jit(solution)/shard_map/cond
  281.6 9.4 copy-start.28
  281.6 12.6 copy-start.14
  281.6 12.7 copy-start.20
  282.4 32.9 %sort.74.cloned.1.call-start = ((), (), s32[]{:S(2)}) async-start(), calls=%async_computation.36 | async-start | bytes 196640 | tf_op jit(solution)/shard_map/cond/branch_1_fun/sort | solution.py:665
  283.1 51.7 %all-gather.26.cloned.1.call-start = ((), (), s32[]{:S(2)}) async-start(), calls=%async_computation.25 | async-start | bytes 7077888 | tf_op jit(solution)/shard_map/cond/branch_1_fun/all_gather | solution.py:777
  284.1 100.7 %all-gather.28.cloned.1.call-start = ((), (), s32[]{:S(2)}) async-start(), calls=%async_computation.26 | async-start | bytes 9437184 | tf_op jit(solution)/shard_map/cond/branch_1_fun/all_gather | solution.py:777
  284.7 178.1 %all-gather.30.cloned.1.call-start = ((), (), s32[]{:S(2)}) async-start(), calls=%async_computation.27 | async-start | bytes 7077888 | tf_op jit(solution)/shard_map/cond/branch_1_fun/all_gather | solution.py:777
  285.3 251.4 %all-gather.32.cloned.1.call-start = ((), (), s32[]{:S(2)}) async-start(), calls=%async_computation.28 | async-start | bytes 7077888 | tf_op jit(solution)/shard_map/cond/branch_1_fun/all_gather | solution.py:777
  286.0 324.9 %all-gather.34.cloned.1.call-start = ((), (), s32[]{:S(2)}) async-start(), calls=%async_computation.29 | async-start | bytes 7077888 | tf_op jit(solution)/shard_map/cond/branch_1_fun/all_gather | solution.py:777
  286.8 531.2 %sort.82.cloned.1.call-start = ((), (), s32[]{:S(2)}) async-start(), calls=%async_computation.40 | async-start | bytes 196640 | tf_op jit(solution)/shard_map/cond/branch_1_fun/sort | solution.py:665
  287.6 531.7 %sort.80.cloned.1.call-start = ((), (), s32[]{:S(2)}) async-start(), calls=%async_computation.39 | async-start | bytes 196640 | tf_op jit(solution)/shard_map/cond/branch_1_fun/sort | solution.py:665
  288.2 532.5 %sort.78.cloned.1.call-start = ((), (), s32[]{:S(2)}) async-start(), calls=%async_computation.38 | async-start | bytes 393248 | tf_op jit(solution)/shard_map/cond/branch_1_fun/sort | solution.py:671
  289.0 532.6 %sort.76.cloned.1.call-start = ((), (), s32[]{:S(2)}) async-start(), calls=%async_computation.37 | async-start | bytes 196640 | tf_op jit(solution)/shard_map/cond/branch_1_fun/sort | solution.py:671
  316.8 1006.0 %reduce-scatter.27.cloned.1.call-start = ((), (), s32[]{:S(2)}) async-start(), calls=%async_computation.30 | async-start | bytes 14155776 | tf_op jit(solution)/shard_map/cond/branch_1_fun/reduce_scatter | solution.py:780
  462.2 862.1 %reduce-scatter.29.cloned.1.call-start = ((), (), s32[]{:S(2)}) async-start(), calls=%async_computation.31 | async-start | bytes 14155776 | tf_op jit(solution)/shard_map/cond/branch_1_fun/reduce_scatter | solution.py:780
  535.4 0.7 copy-start.33
  535.5 0.7 copy-start.34
  535.5 0.7 copy-start.35
  535.5 791.1 %reduce-scatter.31.cloned.1.call-start = ((), (), s32[]{:S(2)}) async-start(), calls=%async_computation.32 | async-start | bytes 14155776 | tf_op jit(solution)/shard_map/cond/branch_1_fun/reduce_scatter | solution.py:780
  609.7 0.7 copy-start.30
  609.7 0.7 copy-start.31
  609.7 0.7 copy-start.32
  609.7 719.3 %reduce-scatter.33.cloned.1.call-start = ((), (), s32[]{:S(2)}) async-start(), calls=%async_computation.33 | async-start | bytes 14155776 | tf_op jit(solution)/shard_map/cond/branch_1_fun/reduce_scatter | solution.py:780
  683.8 1.2 copy-start.12
  683.8 1.9 copy-start.8
  683.8 653.5 %reduce-scatter.35.cloned.1.call-start = ((), (), s32[]{:S(2)}) async-start(), calls=%async_computation.34 | async-start | bytes 18874368 | tf_op jit(solution)/shard_map/cond/branch_1_fun/reduce_scatter | solution.py:780
  685.4 2.9 copy-start.9
  685.4 3.2 copy-start.10
  685.7 6.8 slice-start.2
  688.3 4.3 slice-start.3
  689.0 3.6 copy-start.16
  713.8 19.7 %slice-start.4 = ((s8[6291456]{0:T(1024)(128)(4,1)}), s8[2097152]{0:T(1024)(128)(4,1)S(1)}, s32[]{:S(2)}) async-start(s8[6291456]{0:T(1024)(128)(4,1)} %bitcast.252), calls=%async_computation.53 | async-start | bytes 4194304 | tf_op jit(solution)/shard_map/cond
  713.8 19.7 %slice-start.5 = ((s8[6291456]{0:T(1024)(128)(4,1)}), s8[4194304]{0:T(1024)(128)(4,1)S(1)}, s32[]{:S(2)}) async-start(s8[6291456]{0:T(1024)(128)(4,1)} %bitcast.252), calls=%async_computation.54 | async-start | bytes 8388608 | tf_op jit(solution)/shard_map/cond
  713.8 37.5 %slice-start.6 = ((s8[6291456]{0:T(1024)(128)(4,1)}), s8[4194304]{0:T(1024)(128)(4,1)S(1)}, s32[]{:S(2)}) async-start(s8[6291456]{0:T(1024)(128)(4,1)} %bitcast.254), calls=%async_computation.55 | async-start | bytes 8388608 | tf_op jit(solution)/shard_map/cond
  713.8 37.5 %slice-start.10 = ((s8[6291456]{0:T(1024)(128)(4,1)}), s8[4194304]{0:T(1024)(128)(4,1)S(1)}, s32[]{:S(2)}) async-start(s8[6291456]{0:T(1024)(128)(4,1)} %bitcast.260), calls=%async_computation.59 | async-start | bytes 8388608 | tf_op jit(solution)/shard_map/cond
  733.5 17.8 %slice-start.7 = ((s8[6291456]{0:T(1024)(128)(4,1)}), s8[2097152]{0:T(1024)(128)(4,1)S(1)}, s32[]{:S(2)}) async-start(s8[6291456]{0:T(1024)(128)(4,1)} %bitcast.254), calls=%async_computation.56 | async-start | bytes 4194304 | tf_op jit(solution)/shard_map/cond
  733.5 17.8 %slice-start.11 = ((s8[6291456]{0:T(1024)(128)(4,1)}), s8[2097152]{0:T(1024)(128)(4,1)S(1)}, s32[]{:S(2)}) async-start(s8[6291456]{0:T(1024)(128)(4,1)} %bitcast.260), calls=%async_computation.60 | async-start | bytes 4194304 | tf_op jit(solution)/shard_map/cond
  751.4 16.4 %copy-start.26 = (f32[1,8,256]{2,0,1:T(1,128)S(1)}, f32[1,8,256]{2,0,1:T(1,128)}, u32[]{:S(2)}) copy-start(f32[1,8,256]{2,0,1:T(1,128)} %slice.346) | copy-start | bytes 24580 | tf_op jit(solution)/shard_map/cond
  817.7 53.0 %collective-permute-start = (f32[2048,2048]{1,0:T(8,128)}, f32[2048,2048]{1,0:T(8,128)}, u32[]{:S(2)}, u32[]{:S(2)}) collective-permute-start(f32[2048,2048]{1,0:T(8,128)} %fusion.7.mine_ref.rows_ref), channel_id=1, source_target_pairs={{0,1},{1,0},{2,3},{3,2},{4,5},{5,4},{6,7},{7,6}} | collective-permute-start | bytes 50331656 | tf_op jit(solution)/shard_map/cond/branch_1_fun/ppermute | solution.py:729
  821.6 24.5 %copy-start.21 = (s32[1,4096]{1,0:T(1,128)}, s32[1,4096]{1,0:T(1,128)S(1)}, u32[]{:S(2)}) copy-start(s32[1,4096]{1,0:T(1,128)S(1)} %slice.362) | copy-start | bytes 49156 | tf_op jit(solution)/shard_map/cond
  822.5 23.6 %copy-start.27 = (s32[1,2048]{1,0:T(1,128)}, s32[1,2048]{1,0:T(1,128)S(1)}, u32[]{:S(2)}) copy-start(s32[1,2048]{1,0:T(1,128)S(1)} %slice.361) | copy-start | bytes 24580 | tf_op jit(solution)/shard_map/cond
Sparse Core Ops, SparseCore 0:
  23.5 7.5 sort.98.cloned.1.call-done
  282.5 7.5 sort.86.cloned.1.call-done
  292.8 7.5 sort.88.cloned.1.call-done
  303.0 7.5 sort.96.cloned.1.call-done
  313.2 7.5 sort.94.cloned.1.call-done
  323.3 12.5 sort.92.cloned.1.call-done
  338.5 7.5 sort.90.cloned.1.call-done
  (7 shorter events, 0.1 us)
Sparse Core Ops, SparseCore 1:
  286.0 48.7 all-gather.25
  336.5 48.3 all-gather.27
  387.1 39.5 all-gather.29
  429.0 39.5 all-gather.31
  470.9 39.5 all-gather.33
  513.9 82.3 reduce-scatter.26
  599.6 82.3 reduce-scatter.28
  685.2 82.3 reduce-scatter.30
  770.9 82.3 reduce-scatter.32
  857.4 155.9 reduce-scatter.34
